TPU v7x, 8 devices: a whole 2x2x1 slice. The times are simulated.
8 devices in a mesh: data: 2 (over z, y), stage: 4 (over x, core).
Axes of the slice: x: 2, y: 2, z: 1, core: 2. Of those that a mesh axis runs over, the one named last changes fastest.
Arguments:
- w_in: float32 [4, 512, 2048], P('stage')
- w_out: float32 [4, 2048, 512], P('stage')
- mom_in: float32 [4, 512, 2048], P('stage')
- mom_out: float32 [4, 2048, 512], P('stage')
- var_in: float32 [4, 512, 2048], P('stage')
- var_out: float32 [4, 2048, 512], P('stage')
- acc_in: float32 [2, 4, 512, 2048], P('data', 'stage')
- acc_out: float32 [2, 4, 2048, 512], P('data', 'stage')
- stage_acts: bfloat16 [4, 4096, 512], P('stage', 'data')
- d_out: bfloat16 [4096, 512], P('data')
- next_x: bfloat16 [16, 4096, 512], P(None, 'data')
- learn_rate: float32 [1], replicated
- max_norm: float32 [1], replicated
Outputs:
- output 1: float32 [4, 512, 2048], P('stage')
- output 2: float32 [4, 2048, 512], P('stage')
- output 3: float32 [4, 512, 2048], P('stage')
- output 4: float32 [4, 2048, 512], P('stage')
- output 5: float32 [4, 512, 2048], P('stage')
- output 6: float32 [4, 2048, 512], P('stage')
- output 7: bfloat16 [16, 4096, 512], P(None, 'data')
All inputs are finite; a program needn't handle non-finite values.
Results may differ from a plain program's by a relative error of at most 0.0070407.
Values are sent between devices in bfloat16 or wider.
A program may use at most 1 GiB of HBM per device.

v0:
```python
import jax
import jax.numpy as jnp
from jax import lax
from jax.sharding import PartitionSpec as P

BETA_ONE = 0.9
BETA_TWO = 0.95
ADAM_EPS = 1e-8
WEIGHT_DECAY = 0.1
STEP_COUNT = 10
NORM_EPS = 1e-6
TRANS_DIMS = (((1,), (1,)), ((), ()))
FIRST_DIMS = (((0,), (0,)), ((), ()))


def gelu_tanh(gelu_in):
    return jax.nn.gelu(gelu_in, approximate=True)


def block_forward(row_block, w_first, w_second):
    hidden = jnp.dot(row_block, w_first, preferred_element_type=jnp.float32)
    act_h = gelu_tanh(hidden).astype(jnp.bfloat16)
    branch = jnp.dot(act_h, w_second, preferred_element_type=jnp.float32)
    return (row_block.astype(jnp.float32) + branch).astype(jnp.bfloat16)


def adamw_update(param_old, moment, second, grad_val, clip_coef, lr_value):
    scaled = clip_coef * grad_val
    mom_new = BETA_ONE * moment + (1.0 - BETA_ONE) * scaled
    sec_new = BETA_TWO * second + (1.0 - BETA_TWO) * scaled * scaled
    mom_hat = mom_new / (1.0 - BETA_ONE ** STEP_COUNT)
    sec_hat = sec_new / (1.0 - BETA_TWO ** STEP_COUNT)
    param_new = param_old - lr_value * (mom_hat / (jnp.sqrt(sec_hat) + ADAM_EPS) + WEIGHT_DECAY * param_old)
    return param_new, mom_new, sec_new


def solution(mesh):
    n_stage = mesh.shape['stage']
    n_rep = mesh.shape['data']
    last_stage = n_stage - 1
    back_perm = [(src, src - 1) for src in range(1, n_stage)]
    fwd_perm = [(src, src + 1) for src in range(last_stage)]
    w_spec = P('stage', None, None)
    acc_spec = P('data', 'stage', None, None)
    row_spec = P(None, 'data', None)

    def stage_program(w_in, w_out, mom_in, mom_out, var_in, var_out, acc_in, acc_out, stage_acts, d_out, next_x, learn_rate, max_norm):
        stage_idx = lax.axis_index('stage')
        w_first = w_in[0].astype(jnp.bfloat16)
        w_second = w_out[0].astype(jnp.bfloat16)
        stage_in = stage_acts[0]
        pre_act = jnp.dot(stage_in, w_first, preferred_element_type=jnp.float32)
        act_h, gelu_vjp = jax.vjp(gelu_tanh, pre_act)
        act_h = act_h.astype(jnp.bfloat16)

        def run_active(operands):
            grad_val = operands[0]
            d_hid = lax.dot_general(grad_val, w_second, TRANS_DIMS, preferred_element_type=jnp.float32)
            d_pre = gelu_vjp(d_hid)[0].astype(jnp.bfloat16)
            d_in = grad_val.astype(jnp.float32) + lax.dot_general(d_pre, w_first, TRANS_DIMS, preferred_element_type=jnp.float32)
            return d_in.astype(jnp.bfloat16), grad_val, d_pre

        def back_step(step_idx, loop_carry):
            return lax.cond(stage_idx == last_stage - step_idx, run_active, lambda operands: operands, loop_carry)

        def back_body(step_idx, loop_carry):
            sent_buf, grad_keep, pre_keep = back_step(step_idx, loop_carry)
            return lax.ppermute(sent_buf, 'stage', back_perm), grad_keep, pre_keep

        init_carry = (d_out, jnp.zeros_like(d_out), jnp.zeros((stage_in.shape[0], w_first.shape[1]), jnp.bfloat16))
        back_carry = lax.fori_loop(0, last_stage, back_body, init_carry)
        _, grad_keep, pre_keep = back_step(last_stage, back_carry)
        dw_first = lax.dot_general(stage_in, pre_keep, FIRST_DIMS, preferred_element_type=jnp.float32)
        dw_second = lax.dot_general(act_h, grad_keep, FIRST_DIMS, preferred_element_type=jnp.float32)
        grad_first = lax.psum(acc_in[0, 0] + dw_first, 'data') / n_rep
        grad_second = lax.psum(acc_out[0, 0] + dw_second, 'data') / n_rep
        part_sq = jnp.sum(grad_first * grad_first) + jnp.sum(grad_second * grad_second)
        total_norm = jnp.sqrt(lax.psum(part_sq, 'stage'))
        clip_coef = jnp.minimum(1.0, max_norm[0] / (total_norm + NORM_EPS))
        new_first, mom_first, sec_first = adamw_update(w_in[0], mom_in[0], var_in[0], grad_first, clip_coef, learn_rate[0])
        new_second, mom_second, sec_second = adamw_update(w_out[0], mom_out[0], var_out[0], grad_second, clip_coef, learn_rate[0])
        fw_first = new_first.astype(jnp.bfloat16)
        fw_second = new_second.astype(jnp.bfloat16)
        n_micro = next_x.shape[0]

        def fwd_step(tick_idx, recv_buf, out_buf):
            micro_idx = tick_idx - stage_idx
            is_valid = (micro_idx >= 0) & (micro_idx < n_micro)
            safe_idx = jnp.clip(micro_idx, 0, n_micro - 1)
            first_in = lax.dynamic_index_in_dim(next_x, safe_idx, 0, keepdims=False)
            row_block = jnp.where(stage_idx == 0, first_in, recv_buf)
            result = lax.cond(is_valid, lambda rows_in: block_forward(rows_in, fw_first, fw_second), lambda rows_in: rows_in, row_block)
            old_slice = lax.dynamic_index_in_dim(out_buf, safe_idx, 0, keepdims=False)
            new_slice = jnp.where(is_valid & (stage_idx == last_stage), result, old_slice)
            return result, lax.dynamic_update_index_in_dim(out_buf, new_slice, safe_idx, 0)

        def fwd_body(tick_idx, loop_carry):
            result, out_buf = fwd_step(tick_idx, loop_carry[0], loop_carry[1])
            return lax.ppermute(result, 'stage', fwd_perm), out_buf

        n_ticks = n_stage + n_micro - 1
        fwd_carry = lax.fori_loop(0, n_ticks - 1, fwd_body, (jnp.zeros_like(next_x[0]), jnp.zeros_like(next_x)))
        _, out_buf = fwd_step(n_ticks - 1, fwd_carry[0], fwd_carry[1])
        next_y = lax.psum(jnp.where(stage_idx == last_stage, out_buf, jnp.zeros_like(out_buf)), 'stage')
        return (new_first[None], new_second[None], mom_first[None], mom_second[None], sec_first[None], sec_second[None], next_y)

    return jax.shard_map(stage_program, mesh=mesh, in_specs=(w_spec, w_spec, w_spec, w_spec, w_spec, w_spec, acc_spec, acc_spec, P('stage', 'data', None), P('data', None), row_spec, P(None), P(None)), out_specs=(w_spec, w_spec, w_spec, w_spec, w_spec, w_spec, row_spec), check_vma=False)
```

profile of v0, /device:TPU:7, one launch (start us, length us, event | category | flops | bytes accessed | tf_op | source)
XLA Modules:
  0.0 1894.4 jit_solution(10673800149322571244)
XLA Ops:
  15.8 26.1 %multiply_multiply_fusion.2 = (f32[2048,2048]{1,0:T(8,128)}, f32[2048,2048]{1,0:T(8,128)}, f32[2048,2048]{1,0:T(8,128)}, f32[2048,2048]{1,0:T(8,128)}) fusion(f32[1,512,2048]{2,1,0:T(8,128)} %param.25, bf16[1,2048,512]{2,1,0:T(8,128)(2,1)S(1)} %copy-done), kind=kOutput, calls=%fused_computation.40 | convolution fusion | flops 4337958912 | bytes 73400320 | tf_op jit(solution)/shard_map/dot_general | solution.py:52
  59.2 121.3 %while.33 = (s32[]{:T(128)}, bf16[2048,512]{1,0:T(8,128)(2,1)}, bf16[2048,512]{1,0:T(8,128)(2,1)}, bf16[2048,2048]{1,0:T(8,128)(2,1)}, s32[]{:T(128)}, /*index=5...) while((s32[]{:T(128)}, bf16[2048,512]{1,0:T(8,128)(2,1)}, ...), condition=%wide.region_3.0_spmd, body=%wide.region_0.0_spmd.sunk | while | flops 8635023360 | bytes 115343680 | solution.py:71
  59.2 40.9 %conditional.8 = (bf16[2048,512]{1,0:T(8,128)(2,1)}, bf16[2048,512]{1,0:T(8,128)(2,1)}, bf16[2048,2048]{1,0:T(8,128)(2,1)}) conditional(s32[]{:T(128)} %convert_element_type.112, (bf16[2048,512]{1,0:T(8,128)(2,1)}, bf16[2048,512]{1,0:T(8,128)(2,1)}, bf16[2048,2048]{1,0:T(8,128)(2,1)}) %tuple.108, (bf16[2048,512]{1,0:T(8,128)(2,1)}, ...), branch_computations={%region_1.0_spmd, %region_2.0_spmd} | conditional | flops 8635023360 | bytes 106954800 | solution.py:64
  59.2 28.2 %add_convert_fusion = bf16[2048,2048]{1,0:T(8,128)(2,1)} fusion(f32[2048,2048]{1,0:T(8,128)} %get-tuple-element.390, f32[2048,2048]{1,0:T(8,128)} %get-tuple-element.389, f32[2048,2048]{1,0:T(8,128)} %get-tuple-element.388, f32[2048,2048]{1,0:T(8,128)} %get-tuple-element.387, bf16[2048,512]{1,0:T(8,128)(2,1)} %get-tuple-element.666, ...), kind=kOutput, calls=%fused_computation | convolution fusion | flops 4336910336 | bytes 79691776 | tf_op jit(solution)/shard_map/while/body/eval_jaxpr/cond/branch_1_fun/dot_general | solution.py:58
  108.1 41.4 %collective-permute-start = (bf16[2048,512]{1,0:T(8,128)(2,1)}, bf16[2048,512]{1,0:T(8,128)(2,1)}, u32[]{:S(2)}, u32[]{:S(2)}) collective-permute-start(bf16[2048,512]{1,0:T(8,128)(2,1)} %get-tuple-element.650), channel_id=1, source_target_pairs={{1,0},{2,1},{3,2},{5,4},{6,5},{7,6}} | collective-permute-start | bytes 6291464 | tf_op jit(solution)/shard_map/while/body/eval_jaxpr/ppermute | solution.py:68
  155.0 23.0 %collective-permute-start = (bf16[2048,512]{1,0:T(8,128)(2,1)}, bf16[2048,512]{1,0:T(8,128)(2,1)}, u32[]{:S(2)}, u32[]{:S(2)}) collective-permute-start(bf16[2048,512]{1,0:T(8,128)(2,1)} %get-tuple-element.650), channel_id=1, source_target_pairs={{1,0},{2,1},{3,2},{5,4},{6,5},{7,6}} | collective-permute-start | bytes 6291464 | tf_op jit(solution)/shard_map/while/body/eval_jaxpr/ppermute | solution.py:68
  216.6 249.4 %all-reduce.6.cloned.1.call-done = (f32[512,2048]{0,1:T(8,128)}, f32[2048,512]{1,0:T(8,128)}) async-done(((f32[512,2048]{0,1:T(8,128)}, f32[2048,512]{1,0:T(8,128)}), (f32[512,2048]{0,1:T(8,128)}, f32[2048,512]{1,0:T(8,128)})) %all-reduce.6.cloned.1.call-update) | async-done | bytes 8388624 | tf_op jit(solution)/shard_map/psum | solution.py:75
  518.6 748.0 %while.34 = (s32[]{:T(128)}, bf16[2048,512]{1,0:T(8,128)(2,1)}, bf16[16,2048,512]{2,1,0:T(8,128)(2,1)}, s32[]{:T(128)}, pred[]{:T(512)}, /*index=5*/bf16[16,2048...) while((s32[]{:T(128)}, bf16[2048,512]{1,0:T(8,128)(2,1)}, ...), condition=%wide.region_14.15_spmd, body=%wide.region_11.14_spmd.sunk | while | flops 8632926208 | bytes 37749012 | solution.py:102
  534.7 22.4 %collective-permute-done.1 = bf16[2048,512]{1,0:T(8,128)(2,1)} collective-permute-done((bf16[2048,512]{1,0:T(8,128)(2,1)S(1)}, bf16[2048,512]{1,0:T(8,128)(2,1)}, u32[]{:S(2)}, u32[]{:S(2)}) %collective-permute-start.1) | collective-permute-done | bytes 2097184 | tf_op jit(solution)/shard_map/while/body/eval_jaxpr/ppermute | solution.py:99
  564.5 47.6 %collective-permute-done.1 = bf16[2048,512]{1,0:T(8,128)(2,1)} collective-permute-done((bf16[2048,512]{1,0:T(8,128)(2,1)S(1)}, bf16[2048,512]{1,0:T(8,128)(2,1)}, u32[]{:S(2)}, u32[]{:S(2)}) %collective-permute-start.1) | collective-permute-done | bytes 2097184 | tf_op jit(solution)/shard_map/while/body/eval_jaxpr/ppermute | solution.py:99
  633.4 22.4 %collective-permute-done.1 = bf16[2048,512]{1,0:T(8,128)(2,1)} collective-permute-done((bf16[2048,512]{1,0:T(8,128)(2,1)S(1)}, bf16[2048,512]{1,0:T(8,128)(2,1)}, u32[]{:S(2)}, u32[]{:S(2)}) %collective-permute-start.1) | collective-permute-done | bytes 2097184 | tf_op jit(solution)/shard_map/while/body/eval_jaxpr/ppermute | solution.py:99
  677.0 22.4 %collective-permute-done.1 = bf16[2048,512]{1,0:T(8,128)(2,1)} collective-permute-done((bf16[2048,512]{1,0:T(8,128)(2,1)S(1)}, bf16[2048,512]{1,0:T(8,128)(2,1)}, u32[]{:S(2)}, u32[]{:S(2)}) %collective-permute-start.1) | collective-permute-done | bytes 2097184 | tf_op jit(solution)/shard_map/while/body/eval_jaxpr/ppermute | solution.py:99
  720.6 22.4 %collective-permute-done.1 = bf16[2048,512]{1,0:T(8,128)(2,1)} collective-permute-done((bf16[2048,512]{1,0:T(8,128)(2,1)S(1)}, bf16[2048,512]{1,0:T(8,128)(2,1)}, u32[]{:S(2)}, u32[]{:S(2)}) %collective-permute-start.1) | collective-permute-done | bytes 2097184 | tf_op jit(solution)/shard_map/while/body/eval_jaxpr/ppermute | solution.py:99
  764.3 22.4 %collective-permute-done.1 = bf16[2048,512]{1,0:T(8,128)(2,1)} collective-permute-done((bf16[2048,512]{1,0:T(8,128)(2,1)S(1)}, bf16[2048,512]{1,0:T(8,128)(2,1)}, u32[]{:S(2)}, u32[]{:S(2)}) %collective-permute-start.1) | collective-permute-done | bytes 2097184 | tf_op jit(solution)/shard_map/while/body/eval_jaxpr/ppermute | solution.py:99
  807.9 22.4 %collective-permute-done.1 = bf16[2048,512]{1,0:T(8,128)(2,1)} collective-permute-done((bf16[2048,512]{1,0:T(8,128)(2,1)S(1)}, bf16[2048,512]{1,0:T(8,128)(2,1)}, u32[]{:S(2)}, u32[]{:S(2)}) %collective-permute-start.1) | collective-permute-done | bytes 2097184 | tf_op jit(solution)/shard_map/while/body/eval_jaxpr/ppermute | solution.py:99
  851.5 22.4 %collective-permute-done.1 = bf16[2048,512]{1,0:T(8,128)(2,1)} collective-permute-done((bf16[2048,512]{1,0:T(8,128)(2,1)S(1)}, bf16[2048,512]{1,0:T(8,128)(2,1)}, u32[]{:S(2)}, u32[]{:S(2)}) %collective-permute-start.1) | collective-permute-done | bytes 2097184 | tf_op jit(solution)/shard_map/while/body/eval_jaxpr/ppermute | solution.py:99
  895.1 22.4 %collective-permute-done.1 = bf16[2048,512]{1,0:T(8,128)(2,1)} collective-permute-done((bf16[2048,512]{1,0:T(8,128)(2,1)S(1)}, bf16[2048,512]{1,0:T(8,128)(2,1)}, u32[]{:S(2)}, u32[]{:S(2)}) %collective-permute-start.1) | collective-permute-done | bytes 2097184 | tf_op jit(solution)/shard_map/while/body/eval_jaxpr/ppermute | solution.py:99
  938.8 22.4 %collective-permute-done.1 = bf16[2048,512]{1,0:T(8,128)(2,1)} collective-permute-done((bf16[2048,512]{1,0:T(8,128)(2,1)S(1)}, bf16[2048,512]{1,0:T(8,128)(2,1)}, u32[]{:S(2)}, u32[]{:S(2)}) %collective-permute-start.1) | collective-permute-done | bytes 2097184 | tf_op jit(solution)/shard_map/while/body/eval_jaxpr/ppermute | solution.py:99
  982.4 22.4 %collective-permute-done.1 = bf16[2048,512]{1,0:T(8,128)(2,1)} collective-permute-done((bf16[2048,512]{1,0:T(8,128)(2,1)S(1)}, bf16[2048,512]{1,0:T(8,128)(2,1)}, u32[]{:S(2)}, u32[]{:S(2)}) %collective-permute-start.1) | collective-permute-done | bytes 2097184 | tf_op jit(solution)/shard_map/while/body/eval_jaxpr/ppermute | solution.py:99
  1026.0 22.4 %collective-permute-done.1 = bf16[2048,512]{1,0:T(8,128)(2,1)} collective-permute-done((bf16[2048,512]{1,0:T(8,128)(2,1)S(1)}, bf16[2048,512]{1,0:T(8,128)(2,1)}, u32[]{:S(2)}, u32[]{:S(2)}) %collective-permute-start.1) | collective-permute-done | bytes 2097184 | tf_op jit(solution)/shard_map/while/body/eval_jaxpr/ppermute | solution.py:99
  1156.9 22.4 %collective-permute-done.1 = bf16[2048,512]{1,0:T(8,128)(2,1)} collective-permute-done((bf16[2048,512]{1,0:T(8,128)(2,1)S(1)}, bf16[2048,512]{1,0:T(8,128)(2,1)}, u32[]{:S(2)}, u32[]{:S(2)}) %collective-permute-start.1) | collective-permute-done | bytes 2097184 | tf_op jit(solution)/shard_map/while/body/eval_jaxpr/ppermute | solution.py:99
  1289.3 22.9 %broadcast_select_fusion = bf16[16,2048,512]{2,1,0:T(8,128)(2,1)} fusion(bf16[16,2048,512]{2,1,0:T(8,128)(2,1)} %bitcast_dynamic-update-slice_fusion.1, pred[]{:T(512)} %eq.30), kind=kLoop, calls=%fused_computation.39 | loop fusion | flops 16777216 | bytes 67108864 | tf_op jit(solution)/shard_map/jit(_where)/select_n | solution.py:104
  1328.2 536.0 %all-reduce.4.cloned.1.call-done = bf16[16,2048,512]{2,1,0:T(8,128)(2,1)} async-done(((bf16[16,2048,512]{2,1,0:T(8,128)(2,1)}), bf16[16,2048,512]{2,1,0:T(8,128)(2,1)}) %all-reduce.4.cloned.1.call-update) | async-done | bytes 33554448 | tf_op jit(solution)/shard_map/psum | solution.py:104
  1864.3 22.9 %copy.79 = bf16[16,2048,512]{2,1,0:T(8,128)(2,1)} copy(bf16[16,2048,512]{2,1,0:T(8,128)(2,1)} %all-reduce.4.cloned.1.call-done) | data formatting | bytes 67108864
  (183 shorter events, 837.0 us)
Async XLA Ops:
  7.2 458.8 %all-reduce.6.cloned.1.call-start = ((), (), s32[]{:S(2)}) async-start(), calls=%async_computation.1 | async-start | bytes 16777216 | tf_op jit(solution)/shard_map/psum | solution.py:75
  59.2 28.3 %copy-start.6 = (bf16[512,2048]{1,0:T(8,128)(2,1)S(1)}, bf16[512,2048]{1,0:T(8,128)(2,1)}, u32[]{:S(2)}) copy-start(bf16[512,2048]{1,0:T(8,128)(2,1)} %get-tuple-element.391) | copy-start | bytes 6291460 | tf_op jit(solution)/shard_map/while/body/eval_jaxpr/cond
  100.0 5.1 collective-permute-start
  108.1 43.8 %collective-permute-start = (bf16[2048,512]{1,0:T(8,128)(2,1)}, bf16[2048,512]{1,0:T(8,128)(2,1)}, u32[]{:S(2)}, u32[]{:S(2)}) collective-permute-start(bf16[2048,512]{1,0:T(8,128)(2,1)} %get-tuple-element.650), channel_id=1, source_target_pairs={{1,0},{2,1},{3,2},{5,4},{6,5},{7,6}} | collective-permute-start | bytes 6291464 | tf_op jit(solution)/shard_map/while/body/eval_jaxpr/ppermute | solution.py:68
  155.0 25.4 %collective-permute-start = (bf16[2048,512]{1,0:T(8,128)(2,1)}, bf16[2048,512]{1,0:T(8,128)(2,1)}, u32[]{:S(2)}, u32[]{:S(2)}) collective-permute-start(bf16[2048,512]{1,0:T(8,128)(2,1)} %get-tuple-element.650), channel_id=1, source_target_pairs={{1,0},{2,1},{3,2},{5,4},{6,5},{7,6}} | collective-permute-start | bytes 6291464 | tf_op jit(solution)/shard_map/while/body/eval_jaxpr/ppermute | solution.py:68
  204.5 1659.7 %all-reduce.4.cloned.1.call-start = ((), (), s32[]{:S(2)}) async-start(), calls=%async_computation | async-start | bytes 67108864 | tf_op jit(solution)/shard_map/psum | solution.py:104
  521.1 6.2 collective-permute-start.1
  529.8 27.4 %collective-permute-start.1 = (bf16[2048,512]{1,0:T(8,128)(2,1)S(1)}, bf16[2048,512]{1,0:T(8,128)(2,1)}, u32[]{:S(2)}, u32[]{:S(2)}) collective-permute-start(bf16[2048,512]{1,0:T(8,128)(2,1)S(1)} %get-tuple-element.761), channel_id=1, source_target_pairs={{0,1},{1,2},{2,3},{4,5},{5,6},{6,7}} | collective-permute-start | bytes 6291464 | tf_op jit(solution)/shard_map/while/body/eval_jaxpr/ppermute | solution.py:99
  559.6 52.5 %collective-permute-start.1 = (bf16[2048,512]{1,0:T(8,128)(2,1)S(1)}, bf16[2048,512]{1,0:T(8,128)(2,1)}, u32[]{:S(2)}, u32[]{:S(2)}) collective-permute-start(bf16[2048,512]{1,0:T(8,128)(2,1)S(1)} %get-tuple-element.761), channel_id=1, source_target_pairs={{0,1},{1,2},{2,3},{4,5},{5,6},{6,7}} | collective-permute-start | bytes 6291464 | tf_op jit(solution)/shard_map/while/body/eval_jaxpr/ppermute | solution.py:99
  628.4 27.3 %collective-permute-start.1 = (bf16[2048,512]{1,0:T(8,128)(2,1)S(1)}, bf16[2048,512]{1,0:T(8,128)(2,1)}, u32[]{:S(2)}, u32[]{:S(2)}) collective-permute-start(bf16[2048,512]{1,0:T(8,128)(2,1)S(1)} %get-tuple-element.761), channel_id=1, source_target_pairs={{0,1},{1,2},{2,3},{4,5},{5,6},{6,7}} | collective-permute-start | bytes 6291464 | tf_op jit(solution)/shard_map/while/body/eval_jaxpr/ppermute | solution.py:99
  672.0 27.3 %collective-permute-start.1 = (bf16[2048,512]{1,0:T(8,128)(2,1)S(1)}, bf16[2048,512]{1,0:T(8,128)(2,1)}, u32[]{:S(2)}, u32[]{:S(2)}) collective-permute-start(bf16[2048,512]{1,0:T(8,128)(2,1)S(1)} %get-tuple-element.761), channel_id=1, source_target_pairs={{0,1},{1,2},{2,3},{4,5},{5,6},{6,7}} | collective-permute-start | bytes 6291464 | tf_op jit(solution)/shard_map/while/body/eval_jaxpr/ppermute | solution.py:99
  715.7 27.3 %collective-permute-start.1 = (bf16[2048,512]{1,0:T(8,128)(2,1)S(1)}, bf16[2048,512]{1,0:T(8,128)(2,1)}, u32[]{:S(2)}, u32[]{:S(2)}) collective-permute-start(bf16[2048,512]{1,0:T(8,128)(2,1)S(1)} %get-tuple-element.761), channel_id=1, source_target_pairs={{0,1},{1,2},{2,3},{4,5},{5,6},{6,7}} | collective-permute-start | bytes 6291464 | tf_op jit(solution)/shard_map/while/body/eval_jaxpr/ppermute | solution.py:99
  759.3 27.3 %collective-permute-start.1 = (bf16[2048,512]{1,0:T(8,128)(2,1)S(1)}, bf16[2048,512]{1,0:T(8,128)(2,1)}, u32[]{:S(2)}, u32[]{:S(2)}) collective-permute-start(bf16[2048,512]{1,0:T(8,128)(2,1)S(1)} %get-tuple-element.761), channel_id=1, source_target_pairs={{0,1},{1,2},{2,3},{4,5},{5,6},{6,7}} | collective-permute-start | bytes 6291464 | tf_op jit(solution)/shard_map/while/body/eval_jaxpr/ppermute | solution.py:99
  802.9 27.3 %collective-permute-start.1 = (bf16[2048,512]{1,0:T(8,128)(2,1)S(1)}, bf16[2048,512]{1,0:T(8,128)(2,1)}, u32[]{:S(2)}, u32[]{:S(2)}) collective-permute-start(bf16[2048,512]{1,0:T(8,128)(2,1)S(1)} %get-tuple-element.761), channel_id=1, source_target_pairs={{0,1},{1,2},{2,3},{4,5},{5,6},{6,7}} | collective-permute-start | bytes 6291464 | tf_op jit(solution)/shard_map/while/body/eval_jaxpr/ppermute | solution.py:99
  846.6 27.3 %collective-permute-start.1 = (bf16[2048,512]{1,0:T(8,128)(2,1)S(1)}, bf16[2048,512]{1,0:T(8,128)(2,1)}, u32[]{:S(2)}, u32[]{:S(2)}) collective-permute-start(bf16[2048,512]{1,0:T(8,128)(2,1)S(1)} %get-tuple-element.761), channel_id=1, source_target_pairs={{0,1},{1,2},{2,3},{4,5},{5,6},{6,7}} | collective-permute-start | bytes 6291464 | tf_op jit(solution)/shard_map/while/body/eval_jaxpr/ppermute | solution.py:99
  890.2 27.3 %collective-permute-start.1 = (bf16[2048,512]{1,0:T(8,128)(2,1)S(1)}, bf16[2048,512]{1,0:T(8,128)(2,1)}, u32[]{:S(2)}, u32[]{:S(2)}) collective-permute-start(bf16[2048,512]{1,0:T(8,128)(2,1)S(1)} %get-tuple-element.761), channel_id=1, source_target_pairs={{0,1},{1,2},{2,3},{4,5},{5,6},{6,7}} | collective-permute-start | bytes 6291464 | tf_op jit(solution)/shard_map/while/body/eval_jaxpr/ppermute | solution.py:99
  933.8 27.3 %collective-permute-start.1 = (bf16[2048,512]{1,0:T(8,128)(2,1)S(1)}, bf16[2048,512]{1,0:T(8,128)(2,1)}, u32[]{:S(2)}, u32[]{:S(2)}) collective-permute-start(bf16[2048,512]{1,0:T(8,128)(2,1)S(1)} %get-tuple-element.761), channel_id=1, source_target_pairs={{0,1},{1,2},{2,3},{4,5},{5,6},{6,7}} | collective-permute-start | bytes 6291464 | tf_op jit(solution)/shard_map/while/body/eval_jaxpr/ppermute | solution.py:99
  977.4 27.3 %collective-permute-start.1 = (bf16[2048,512]{1,0:T(8,128)(2,1)S(1)}, bf16[2048,512]{1,0:T(8,128)(2,1)}, u32[]{:S(2)}, u32[]{:S(2)}) collective-permute-start(bf16[2048,512]{1,0:T(8,128)(2,1)S(1)} %get-tuple-element.761), channel_id=1, source_target_pairs={{0,1},{1,2},{2,3},{4,5},{5,6},{6,7}} | collective-permute-start | bytes 6291464 | tf_op jit(solution)/shard_map/while/body/eval_jaxpr/ppermute | solution.py:99
  1021.1 27.3 %collective-permute-start.1 = (bf16[2048,512]{1,0:T(8,128)(2,1)S(1)}, bf16[2048,512]{1,0:T(8,128)(2,1)}, u32[]{:S(2)}, u32[]{:S(2)}) collective-permute-start(bf16[2048,512]{1,0:T(8,128)(2,1)S(1)} %get-tuple-element.761), channel_id=1, source_target_pairs={{0,1},{1,2},{2,3},{4,5},{5,6},{6,7}} | collective-permute-start | bytes 6291464 | tf_op jit(solution)/shard_map/while/body/eval_jaxpr/ppermute | solution.py:99
  1064.7 27.3 %collective-permute-start.1 = (bf16[2048,512]{1,0:T(8,128)(2,1)S(1)}, bf16[2048,512]{1,0:T(8,128)(2,1)}, u32[]{:S(2)}, u32[]{:S(2)}) collective-permute-start(bf16[2048,512]{1,0:T(8,128)(2,1)S(1)} %get-tuple-element.761), channel_id=1, source_target_pairs={{0,1},{1,2},{2,3},{4,5},{5,6},{6,7}} | collective-permute-start | bytes 6291464 | tf_op jit(solution)/shard_map/while/body/eval_jaxpr/ppermute | solution.py:99
  1108.3 27.3 %collective-permute-start.1 = (bf16[2048,512]{1,0:T(8,128)(2,1)S(1)}, bf16[2048,512]{1,0:T(8,128)(2,1)}, u32[]{:S(2)}, u32[]{:S(2)}) collective-permute-start(bf16[2048,512]{1,0:T(8,128)(2,1)S(1)} %get-tuple-element.761), channel_id=1, source_target_pairs={{0,1},{1,2},{2,3},{4,5},{5,6},{6,7}} | collective-permute-start | bytes 6291464 | tf_op jit(solution)/shard_map/while/body/eval_jaxpr/ppermute | solution.py:99
  1152.0 27.3 %collective-permute-start.1 = (bf16[2048,512]{1,0:T(8,128)(2,1)S(1)}, bf16[2048,512]{1,0:T(8,128)(2,1)}, u32[]{:S(2)}, u32[]{:S(2)}) collective-permute-start(bf16[2048,512]{1,0:T(8,128)(2,1)S(1)} %get-tuple-element.761), channel_id=1, source_target_pairs={{0,1},{1,2},{2,3},{4,5},{5,6},{6,7}} | collective-permute-start | bytes 6291464 | tf_op jit(solution)/shard_map/while/body/eval_jaxpr/ppermute | solution.py:99
  1195.6 27.3 %collective-permute-start.1 = (bf16[2048,512]{1,0:T(8,128)(2,1)S(1)}, bf16[2048,512]{1,0:T(8,128)(2,1)}, u32[]{:S(2)}, u32[]{:S(2)}) collective-permute-start(bf16[2048,512]{1,0:T(8,128)(2,1)S(1)} %get-tuple-element.761), channel_id=1, source_target_pairs={{0,1},{1,2},{2,3},{4,5},{5,6},{6,7}} | collective-permute-start | bytes 6291464 | tf_op jit(solution)/shard_map/while/body/eval_jaxpr/ppermute | solution.py:99
  1239.2 27.3 %collective-permute-start.1 = (bf16[2048,512]{1,0:T(8,128)(2,1)S(1)}, bf16[2048,512]{1,0:T(8,128)(2,1)}, u32[]{:S(2)}, u32[]{:S(2)}) collective-permute-start(bf16[2048,512]{1,0:T(8,128)(2,1)S(1)} %get-tuple-element.761), channel_id=1, source_target_pairs={{0,1},{1,2},{2,3},{4,5},{5,6},{6,7}} | collective-permute-start | bytes 6291464 | tf_op jit(solution)/shard_map/while/body/eval_jaxpr/ppermute | solution.py:99
  (6 other events, 75.1 us)
Sparse Core Ops, SparseCore 0:
  204.7 261.2 all-reduce.5
  1312.3 551.8 all-reduce.3
where the time goes:
time: 1910 us; the launch traced here: 1890 us
  waiting for transfers between devices  1200 us (63%)
  matrix products  282 us (15%)
  local copies, waits for them, and re-layouts  153 us (8%)
  other arithmetic  143 us (7%)
  starting transfers between devices  90.5 us (5%)
    psum x1, waiting for transfers between devices, stage_program(): lax.psum(jnp.where(stage_idx == last_stage, out_buf, jnp.zeros_like(out_b...  536 us
    ppermute x18, waiting for transfers between devices, fwd_body(): return (lax.ppermute(result, 'stage', fwd_perm), out_buf)  407 us
    psum x1, waiting for transfers between devices, stage_program(): grad_first = lax.psum(acc_in[0, 0] + dw_first, 'data') / n_rep  249 us
    dot_general x16, matrix products, block_forward(): branch = jnp.dot(act_h, w_second, preferred_element_type=jnp.float32)  200 us
    ppermute x3, starting transfers between devices, back_body(): return (lax.ppermute(sent_buf, 'stage', back_perm), grad_keep, pre_keep)  67.1 us
    unnamed x21, local copies, waits for them, and re-layouts  63.5 us
    select_n x19, other arithmetic, fwd_step(): row_block = jnp.where(stage_idx == 0, first_in, recv_buf)  46.4 us
  transfers between devices with their start and end apart: 23, of which 23 were waited for; matrix products, arithmetic and copies ran while one was open for 5% of the time, Pallas kernels for 0%

commit v1 on v0

v1 whole, which is shorter than its diff:
```python
import functools

import jax
import jax.numpy as jnp
from jax import lax
from jax.experimental import pallas as pl
from jax.experimental.pallas import tpu as pltpu
from jax.sharding import PartitionSpec as P

BETA_ONE = 0.9
BETA_TWO = 0.95
ADAM_EPS = 1e-8
WEIGHT_DECAY = 0.1
STEP_COUNT = 10
NORM_EPS = 1e-6
TRANS_DIMS = (((1,), (1,)), ((), ()))
FIRST_DIMS = (((0,), (0,)), ((), ()))
TILE = 512
CHUNK = 512
SLOTS = 8
LAG = 6


def gelu_tanh(gelu_in):
    return jax.nn.gelu(gelu_in, approximate=True)


def fast_gelu(z):
    inner = z * (0.7978845608028654 + 0.035677408136300125 * (z * z))
    half = 0.5 * z
    return half + half * jnp.tanh(inner)


def adamw_update(param_old, moment, second, grad_val, clip_coef, lr_value):
    scaled = clip_coef * grad_val
    mom_new = BETA_ONE * moment + (1.0 - BETA_ONE) * scaled
    sec_new = BETA_TWO * second + (1.0 - BETA_TWO) * scaled * scaled
    mom_hat = mom_new / (1.0 - BETA_ONE ** STEP_COUNT)
    sec_hat = sec_new / (1.0 - BETA_TWO ** STEP_COUNT)
    param_new = param_old - lr_value * (mom_hat / (jnp.sqrt(sec_hat) + ADAM_EPS) + WEIGHT_DECAY * param_old)
    return param_new, mom_new, sec_new


def forward_kernel(n_tiles, x_ref, w1_ref, w2_ref, y_ref, xv, yv, w1v, w2v, xsem, wsem, osem, psend, nsend, fsend, precv, nrecv, frecv):
    stage = lax.axis_index('stage')
    partner = stage + 1 - 2 * (stage % 2)
    across = (stage + 2) % 4
    n_blocks = w1v.shape[0]
    width = w1v.shape[2]

    def rows(owner, tile):
        return pl.ds(pl.multiple_of((owner * n_tiles + tile) * TILE, TILE), TILE)

    def load_x(tile):
        return pltpu.make_async_copy(x_ref.at[rows(stage, tile)], xv.at[tile % 2], xsem.at[tile % 2])

    def load_w(block):
        return (pltpu.make_async_copy(w1_ref.at[block], w1v.at[block], wsem.at[block, 0]),
                pltpu.make_async_copy(w2_ref.at[block], w2v.at[block], wsem.at[block, 1]))

    def store_own(tile):
        return pltpu.make_async_copy(yv.at[tile % SLOTS], y_ref.at[rows(stage, tile)], osem.at[tile % SLOTS])

    def remote(src, owner, tile, send, recv, target):
        return pltpu.make_async_remote_copy(src_ref=src, dst_ref=y_ref.at[rows(owner, tile)], send_sem=send, recv_sem=recv,
                                            device_id={'stage': target}, device_id_type=pl.DeviceIdType.MESH)

    def to_partner(tile):
        return remote(yv.at[tile % SLOTS], stage, tile, psend.at[tile % SLOTS], precv.at[tile], partner)

    def to_across(tile):
        return remote(yv.at[tile % SLOTS], stage, tile, nsend.at[tile % SLOTS], nrecv.at[tile], across)

    def pass_on(tile):
        return remote(y_ref.at[rows(across, tile)], across, tile, fsend.at[tile], frecv.at[tile], partner)

    load_x(0).start()
    for block in range(n_blocks):
        for copy in load_w(block):
            copy.start()
    barrier = pltpu.get_barrier_semaphore()
    for peer in (partner, across):
        pl.semaphore_signal(barrier, inc=1, device_id={'stage': peer}, device_id_type=pl.DeviceIdType.MESH)
    pl.semaphore_wait(barrier, 2)

    def relay(tile):
        remote(y_ref.at[rows(across, tile)], across, tile, nsend.at[0], nrecv.at[tile], across).wait_recv()
        pass_on(tile).start()

    def free_slot(tile):
        store_own(tile).wait()
        to_partner(tile).wait_send()
        to_across(tile).wait_send()

    @pl.loop(0, n_tiles)
    def _(tile):
        load_x(tile).wait()

        @pl.when(tile + 1 < n_tiles)
        def _():
            load_x(tile + 1).start()

        @pl.when(tile >= SLOTS)
        def _():
            free_slot(tile - SLOTS)

        @pl.loop(0, n_blocks)
        def _(block):
            @pl.when(tile == 0)
            def _():
                for copy in load_w(block):
                    copy.wait()

            x_rows = xv[tile % 2]
            total = x_rows.astype(jnp.float32)
            for first in range(0, width, CHUNK):
                hidden = jnp.dot(x_rows, w1v[block, :, first:first + CHUNK], preferred_element_type=jnp.float32)
                act_h = fast_gelu(hidden).astype(jnp.bfloat16)
                part = jnp.dot(act_h, w2v[block, first:first + CHUNK, :], preferred_element_type=jnp.float32)
                total = part if first == 0 else total + part
            total = x_rows.astype(jnp.float32) + total
            xv[tile % 2] = total.astype(jnp.bfloat16)

            @pl.when(block == n_blocks - 1)
            def _():
                yv[tile % SLOTS] = total.astype(jnp.bfloat16)

        store_own(tile).start()
        to_across(tile).start()
        to_partner(tile).start()

        @pl.when(tile >= LAG)
        def _():
            relay(tile - LAG)

    for tile in range(n_tiles - LAG, n_tiles):
        relay(tile)
    for tile in range(n_tiles - SLOTS, n_tiles):
        free_slot(tile)

    @pl.loop(0, n_tiles)
    def _(tile):
        remote(y_ref.at[rows(partner, tile)], partner, tile, psend.at[0], precv.at[tile], partner).wait_recv()
        other = (partner + 2) % 4
        remote(y_ref.at[rows(other, tile)], other, tile, fsend.at[0], frecv.at[tile], partner).wait_recv()
        pass_on(tile).wait_send()


def forward_all(x_rows, w_first, w_second, n_stage):
    n_rows, dim = x_rows.shape
    n_blocks, _, width = w_first.shape
    n_tiles = n_rows // (n_stage * TILE)
    dma = pltpu.SemaphoreType.DMA
    flops = 4 * n_tiles * TILE * dim * width * n_blocks
    return pl.pallas_call(
        functools.partial(forward_kernel, n_tiles),
        out_shape=jax.ShapeDtypeStruct((n_rows, dim), jnp.bfloat16),
        in_specs=[pl.BlockSpec(memory_space=pl.ANY)] * 3,
        out_specs=pl.BlockSpec(memory_space=pl.ANY),
        scratch_shapes=[
            pltpu.VMEM((2, TILE, dim), jnp.bfloat16),
            pltpu.VMEM((SLOTS, TILE, dim), jnp.bfloat16),
            pltpu.VMEM((n_blocks, dim, width), jnp.bfloat16),
            pltpu.VMEM((n_blocks, width, dim), jnp.bfloat16),
            dma((2,)), dma((n_blocks, 2)), dma((SLOTS,)), dma((SLOTS,)), dma((SLOTS,)),
            dma((n_tiles,)), dma((n_tiles,)), dma((n_tiles,)), dma((n_tiles,)),
        ],
        compiler_params=pltpu.CompilerParams(collective_id=0, has_side_effects=True, vmem_limit_bytes=48 * 2 ** 20),
        cost_estimate=pl.CostEstimate(flops=flops, bytes_accessed=2 * n_rows * dim * 2, transcendentals=0),
        name='forward_all',
    )(x_rows, w_first, w_second)


def solution(mesh):
    n_stage = mesh.shape['stage']
    n_rep = mesh.shape['data']
    last_stage = n_stage - 1
    back_perm = [(src, src - 1) for src in range(1, n_stage)]
    swap = [(0, 1), (1, 0)]
    w_spec = P('stage', None, None)
    acc_spec = P('data', 'stage', None, None)
    row_spec = P(None, 'data', None)

    def stage_program(w_in, w_out, mom_in, mom_out, var_in, var_out, acc_in, acc_out, stage_acts, d_out, next_x, learn_rate, max_norm):
        stage_idx = lax.axis_index('stage')
        rep_idx = lax.axis_index('data')
        w_first = w_in[0].astype(jnp.bfloat16)
        w_second = w_out[0].astype(jnp.bfloat16)
        stage_in = stage_acts[0]
        pre_act = jnp.dot(stage_in, w_first, preferred_element_type=jnp.float32)
        act_h, gelu_vjp = jax.vjp(gelu_tanh, pre_act)
        act_h = act_h.astype(jnp.bfloat16)

        def run_active(operands):
            grad_val = operands[0]
            d_hid = lax.dot_general(grad_val, w_second, TRANS_DIMS, preferred_element_type=jnp.float32)
            d_pre = gelu_vjp(d_hid)[0].astype(jnp.bfloat16)
            d_in = grad_val.astype(jnp.float32) + lax.dot_general(d_pre, w_first, TRANS_DIMS, preferred_element_type=jnp.float32)
            return d_in.astype(jnp.bfloat16), grad_val, d_pre

        def back_step(step_idx, loop_carry):
            return lax.cond(stage_idx == last_stage - step_idx, run_active, lambda operands: operands, loop_carry)

        def back_body(step_idx, loop_carry):
            sent_buf, grad_keep, pre_keep = back_step(step_idx, loop_carry)
            return lax.ppermute(sent_buf, 'stage', back_perm), grad_keep, pre_keep

        init_carry = (d_out, jnp.zeros_like(d_out), jnp.zeros((stage_in.shape[0], w_first.shape[1]), jnp.bfloat16))
        back_carry = lax.fori_loop(0, last_stage, back_body, init_carry)
        _, grad_keep, pre_keep = back_step(last_stage, back_carry)
        dw_first = lax.dot_general(stage_in, pre_keep, FIRST_DIMS, preferred_element_type=jnp.float32)
        dw_second = lax.dot_general(act_h, grad_keep, FIRST_DIMS, preferred_element_type=jnp.float32)
        loc_first = acc_in[0, 0] + dw_first
        loc_second = acc_out[0, 0] + dw_second

        def half_of(arr, idx):
            size = arr.shape[0] // n_rep
            return lax.dynamic_slice_in_dim(arr, idx * size, size, 0)

        other_idx = 1 - rep_idx
        half_first = (half_of(loc_first, rep_idx) + lax.ppermute(half_of(loc_first, other_idx), 'data', swap)) / n_rep
        half_second = (half_of(loc_second, rep_idx) + lax.ppermute(half_of(loc_second, other_idx), 'data', swap)) / n_rep
        far_first = lax.ppermute(half_first, 'data', swap)
        far_second = lax.ppermute(half_second, 'data', swap)
        part_sq = jnp.sum(half_first * half_first) + jnp.sum(half_second * half_second)
        total_norm = jnp.sqrt(lax.psum(part_sq, ('data', 'stage')))
        clip_coef = jnp.minimum(1.0, max_norm[0] / (total_norm + NORM_EPS))

        def early(param, moment, second, grad_val):
            new_w, _, _ = adamw_update(half_of(param, rep_idx), half_of(moment, rep_idx), half_of(second, rep_idx), grad_val, clip_coef, learn_rate[0])
            gathered = lax.all_gather(new_w.astype(jnp.bfloat16), ('stage', 'data'), axis=0, tiled=True)
            return gathered.reshape((n_stage,) + param.shape)

        fw_first = early(w_in[0], mom_in[0], var_in[0], half_first)
        fw_second = early(w_out[0], mom_out[0], var_out[0], half_second)
        n_micro, n_rows, dim = next_x.shape
        next_y = forward_all(next_x.reshape(n_micro * n_rows, dim), fw_first, fw_second, n_stage).reshape(next_x.shape)

        def whole(near, far):
            is_low = rep_idx == 0
            return jnp.concatenate([jnp.where(is_low, near, far), jnp.where(is_low, far, near)], axis=0)

        new_first, mom_first, sec_first = adamw_update(w_in[0], mom_in[0], var_in[0], whole(half_first, far_first), clip_coef, learn_rate[0])
        new_second, mom_second, sec_second = adamw_update(w_out[0], mom_out[0], var_out[0], whole(half_second, far_second), clip_coef, learn_rate[0])
        return (new_first[None], new_second[None], mom_first[None], mom_second[None], sec_first[None], sec_second[None], next_y)

    return jax.shard_map(stage_program, mesh=mesh, in_specs=(w_spec, w_spec, w_spec, w_spec, w_spec, w_spec, acc_spec, acc_spec, P('stage', 'data', None), P('data', None), row_spec, P(None), P(None)), out_specs=(w_spec, w_spec, w_spec, w_spec, w_spec, w_spec, row_spec), check_vma=False)
```

time: 1910 us -> 792 us (0.41)
  waiting for transfers between devices: 1200 us -> 186 us
  Pallas kernels: 0 us -> 203 us
  matrix products: 282 us -> 85.2 us
  blocking collectives: 6.67 us -> 127 us
  local copies, waits for them, and re-layouts: 153 us -> 47.5 us
  other arithmetic: 143 us -> 52 us
  starting transfers between devices: 90.5 us -> 70.3 us
    psum x2 -> x0, waiting for transfers between devices: 785 us -> none  [the longest x1 536 us: stage_program(): lax.psum(jnp.where(stage_idx == last_stage, out_buf, jnp.zeros_like(out_b...]
    ppermute x18 -> x4, waiting for transfers between devices: 407 us -> 179 us  [the longest x1 78.7 us: stage_program(): far_second = lax.ppermute(half_second, 'data', swap)]
    pallas_call x0 -> x1, Pallas kernels: none -> 203 us  [forward_all(): pl.pallas_call(functools.partial(forward_kernel, n_tiles), out_shape=jax....]
    dot_general x16 -> x0, matrix products: 200 us -> none  [block_forward(): branch = jnp.dot(act_h, w_second, preferred_element_type=jnp.float32)]
    psum x1, blocking collectives: 6.67 us -> 127 us  [stage_program(): total_norm = jnp.sqrt(lax.psum(part_sq, ('data', 'stage')))]
    select_n x20 -> x0, other arithmetic: 69.2 us -> none  [the longest x19 46.4 us: fwd_step(): row_block = jnp.where(stage_idx == 0, first_in, recv_buf)]
    dynamic_update_slice x19 -> x0, other arithmetic: 37.9 us -> none  [fwd_step(): lax.dynamic_update_index_in_dim(out_buf, new_slice, safe_idx, 0)]
    unnamed x21 -> x22, local copies, waits for them, and re-layouts: 63.5 us -> 26.2 us
  transfers between devices with their start and end apart: 23 -> 9, of which waited for: 23 -> 7; matrix products, arithmetic and copies ran while one was open for 5% -> 6% of each run, Pallas kernels for 0% -> 0%
where the time goes in v1:
time: 792 us; the launch traced here: 789 us
  Pallas kernels  203 us (26%)
  waiting for transfers between devices  186 us (23%)
  blocking collectives  127 us (16%)
  matrix products  85.2 us (11%)
  starting transfers between devices  70.3 us (9%)
  other arithmetic  52 us (7%)
  local copies, waits for them, and re-layouts  47.5 us (6%)
  between operations  17.4 us (2%)
    pallas_call x1, Pallas kernels, forward_all(): pl.pallas_call(functools.partial(forward_kernel, n_tiles), out_shape=jax....  203 us
    psum x1, blocking collectives, stage_program(): total_norm = jnp.sqrt(lax.psum(part_sq, ('data', 'stage')))  127 us
    ppermute x1, waiting for transfers between devices, stage_program(): far_second = lax.ppermute(half_second, 'data', swap)  78.7 us
    ppermute x1, waiting for transfers between devices, stage_program(): far_first = lax.ppermute(half_first, 'data', swap)  72.4 us
    ppermute x3, starting transfers between devices, back_body(): return (lax.ppermute(sent_buf, 'stage', back_perm), grad_keep, pre_keep)  67.1 us
    dot_general x1, matrix products, run_active(): lax.dot_general(grad_val, w_second, TRANS_DIMS, preferred_element_type=jn...  28.3 us
    unnamed x22, local copies, waits for them, and re-layouts  26.2 us
    dot_general x1, matrix products, stage_program(): pre_act = jnp.dot(stage_in, w_first, preferred_element_type=jnp.float32)  25.5 us
  transfers between devices with their start and end apart: 9, of which 7 were waited for; matrix products, arithmetic and copies ran while one was open for 6% of the time, Pallas kernels for 0%

profile of v1, /device:TPU:7, one launch (start us, length us, event | category | flops | bytes accessed | tf_op | source)
XLA Modules:
  0.0 788.8 jit_solution(12773964059348590103)
XLA Ops:
  15.9 25.5 %multiply_multiply_fusion = (f32[2048,2048]{1,0:T(8,128)}, f32[2048,2048]{1,0:T(8,128)}, f32[2048,2048]{1,0:T(8,128)}, f32[2048,2048]{1,0:T(8,128)}) fusion(bf16[512,2048]{1,0:T(8,128)(2,1)} %convert_bitcast_fusion, bf16[1,2048,512]{2,1,0:T(8,128)(2,1)S(1)} %copy-done), kind=kOutput, calls=%fused_computation.3 | convolution fusion | flops 4336910336 | bytes 71303168 | tf_op jit(solution)/shard_map/dot_general | solution.py:190
  41.4 4.3 broadcast_in_dim.5
  47.2 121.3 %while.17 = (s32[]{:T(128)}, bf16[2048,512]{1,0:T(8,128)(2,1)}, bf16[2048,512]{1,0:T(8,128)(2,1)}, bf16[2048,2048]{1,0:T(8,128)(2,1)}, s32[]{:T(128)}, /*index=5...) while((s32[]{:T(128)}, bf16[2048,512]{1,0:T(8,128)(2,1)}, ...), condition=%wide.region_3.0_spmd, body=%wide.region_0.0_spmd.sunk | while | flops 8635023360 | bytes 115343680 | solution.py:209
  47.2 40.9 %conditional.4 = (bf16[2048,512]{1,0:T(8,128)(2,1)}, bf16[2048,512]{1,0:T(8,128)(2,1)}, bf16[2048,2048]{1,0:T(8,128)(2,1)}) conditional(s32[]{:T(128)} %convert_element_type.65, (bf16[2048,512]{1,0:T(8,128)(2,1)}, bf16[2048,512]{1,0:T(8,128)(2,1)}, bf16[2048,2048]{1,0:T(8,128)(2,1)}) %tuple.61, (bf16[2048,512]{1,0:T(8,128)(2,1)}, ...), branch_computations={%region_1.0_spmd, %region_2.0_spmd} | conditional | flops 8635023360 | bytes 106954800 | solution.py:202
  47.2 28.3 %add_convert_fusion = bf16[2048,2048]{1,0:T(8,128)(2,1)} fusion(f32[2048,2048]{1,0:T(8,128)} %get-tuple-element.216, f32[2048,2048]{1,0:T(8,128)} %get-tuple-element.215, f32[2048,2048]{1,0:T(8,128)} %get-tuple-element.214, f32[2048,2048]{1,0:T(8,128)} %get-tuple-element.213, bf16[2048,512]{1,0:T(8,128)(2,1)} %get-tuple-element.373, ...), kind=kOutput, calls=%fused_computation | convolution fusion | flops 4336910336 | bytes 79691776 | tf_op jit(solution)/shard_map/while/body/eval_jaxpr/cond/branch_1_fun/dot_general | solution.py:196
  75.5 9.6 %add_convert_fusion.1 = bf16[2048,512]{1,0:T(8,128)(2,1)} fusion(bf16[2048,512]{1,0:T(8,128)(2,1)} %get-tuple-element.373, bf16[2048,2048]{1,0:T(8,128)(2,1)} %add_convert_fusion, bf16[512,2048]{1,0:T(8,128)(2,1)S(1)} %copy-done.8), kind=kOutput, calls=%fused_computation.1 | convolution fusion | flops 4298113024 | bytes 14680064 | tf_op jit(solution)/shard_map/while/body/eval_jaxpr/cond/branch_1_fun/dot_general | solution.py:198
  96.2 41.4 %collective-permute-start = (bf16[2048,512]{1,0:T(8,128)(2,1)}, bf16[2048,512]{1,0:T(8,128)(2,1)}, u32[]{:S(2)}, u32[]{:S(2)}) collective-permute-start(bf16[2048,512]{1,0:T(8,128)(2,1)} %get-tuple-element.366), channel_id=1, source_target_pairs={{1,0},{2,1},{3,2},{5,4},{6,5},{7,6}} | collective-permute-start | bytes 6291464 | tf_op jit(solution)/shard_map/while/body/eval_jaxpr/ppermute | solution.py:206
  143.0 23.0 %collective-permute-start = (bf16[2048,512]{1,0:T(8,128)(2,1)}, bf16[2048,512]{1,0:T(8,128)(2,1)}, u32[]{:S(2)}, u32[]{:S(2)}) collective-permute-start(bf16[2048,512]{1,0:T(8,128)(2,1)} %get-tuple-element.366), channel_id=1, source_target_pairs={{1,0},{2,1},{3,2},{5,4},{6,5},{7,6}} | collective-permute-start | bytes 6291464 | tf_op jit(solution)/shard_map/while/body/eval_jaxpr/ppermute | solution.py:206
  168.5 12.3 %bitcast_add_fusion = f32[2048,512]{1,0:T(8,128)} fusion(f32[1,1,2048,512]{3,2,1,0:T(8,128)} %param.26, bf16[2048,512]{1,0:T(8,128)(2,1)} %get-tuple-element.255, f32[2048,2048]{1,0:T(8,128)} %get-tuple-element.435), kind=kOutput, calls=%fused_computation.19 | convolution fusion | flops 4333764608 | bytes 27262976 | tf_op jit(solution)/shard_map/dot_general | solution.py:212
  184.2 9.5 %bitcast_add_fusion.1 = f32[512,2048]{1,0:T(8,128)} fusion(f32[1,1,512,2048]{3,2,1,0:T(8,128)S(1)} %copy-done.10, bf16[2048,2048]{1,0:T(8,128)(2,1)} %get-tuple-element.254, bf16[1,2048,512]{2,1,0:T(8,128)(2,1)S(1)} %copy-done), kind=kOutput, calls=%fused_computation.20 | convolution fusion | flops 4296015872 | bytes 18874368 | tf_op jit(solution)/shard_map/dot_general | solution.py:211
  198.8 10.1 %collective-permute-done.2 = f32[1024,512]{1,0:T(8,128)} collective-permute-done((f32[1024,512]{1,0:T(8,128)}, f32[1024,512]{1,0:T(8,128)}, u32[]{:S(2)}, u32[]{:S(2)}) %collective-permute-start.2) | collective-permute-done | bytes 2097184 | tf_op jit(solution)/shard_map/ppermute | solution.py:222
  208.9 4.7 multiply_reduce_fusion
  213.6 17.8 %collective-permute-done.1 = f32[256,2048]{1,0:T(8,128)} collective-permute-done((f32[256,2048]{1,0:T(8,128)}, f32[256,2048]{1,0:T(8,128)}, u32[]{:S(2)}, u32[]{:S(2)}) %collective-permute-start.1) | collective-permute-done | bytes 2097184 | tf_op jit(solution)/shard_map/ppermute | solution.py:221
  231.4 4.0 multiply_reduce_fusion.1
  237.3 127.2 %psum.7 = f32[]{:T(128)} all-reduce(f32[]{:T(128)S(6)} %add.146), channel_id=1, replica_groups=mesh['data'=2,'stage'=4] {'data','stage'}, use_global_device_ids=true, to_apply=%region_8.0 | all-reduce | flops 1 | bytes 8 | tf_op jit(solution)/shard_map/psum | solution.py:226
  365.3 7.0 fusion.20
  372.5 6.9 fusion.22
  380.9 78.7 %collective-permute-done.4 = f32[1024,512]{1,0:T(8,128)} collective-permute-done((f32[1024,512]{1,0:T(8,128)}, f32[1024,512]{1,0:T(8,128)}, u32[]{:S(2)}, u32[]{:S(2)}) %collective-permute-start.4) | collective-permute-done | bytes 2097184 | tf_op jit(solution)/shard_map/ppermute | solution.py:224
  459.6 5.0 select_bitcast_fusion.1
  464.6 72.4 %collective-permute-done.3 = f32[256,2048]{1,0:T(8,128)} collective-permute-done((f32[256,2048]{1,0:T(8,128)}, f32[256,2048]{1,0:T(8,128)}, u32[]{:S(2)}, u32[]{:S(2)}) %collective-permute-start.3) | collective-permute-done | bytes 2097184 | tf_op jit(solution)/shard_map/ppermute | solution.py:223
  540.3 7.9 %multiply_subtract_fusion = (f32[1,2048,512]{2,1,0:T(8,128)}, f32[1,2048,512]{2,1,0:T(8,128)}, f32[1,2048,512]{2,1,0:T(8,128)}) fusion(f32[1,2048,512]{2,1,0:T(8,128)S(1)} %copy-done.1, f32[]{:T(128)} %bitcast.83, f32[1,1024,512]{2,1,0:T(8,128)} %get-tuple-element.292, f32[1,1024,512]{2,1,0:T(8,128)} %get-tuple-element.291, f32[]{:T(128)S(6)} %min.3, ...), kind=kLoop, calls=%fused_computation.21 | loop fusion | flops 17825792 | bytes 29360136 | tf_op jit(solution)/shard_map/sub | solution.py:40
  548.2 7.9 multiply_subtract_fusion.1
  556.1 203.0 %forward_all.1 = bf16[32768,512]{1,0:T(8,128)(2,1)} custom-call(bf16[32768,512]{1,0:T(8,128)(2,1)} %bitcast.88, bf16[4,512,2048]{2,1,0:T(8,128)(2,1)} %bitcast.90, bf16[4,2048,512]{2,1,0:T(8,128)(2,1)} %bitcast.89), custom_call_target="tpu_custom_call" | custom-call | flops 137438953472 | bytes 67108864 | tf_op jit(solution)/shard_map/forward_all/pallas_call | solution.py:155
  759.1 22.9 %copy.47 = bf16[16,2048,512]{2,1,0:T(8,128)(2,1)} copy(bf16[16,2048,512]{2,1,0:T(8,128)(2,1)} %bitcast.87) | data formatting | bytes 67108864
  (49 shorter events, 48.2 us)
Async XLA Ops:
  7.2 8.7 %copy-start = (bf16[1,2048,512]{2,1,0:T(8,128)(2,1)S(1)}, bf16[1,2048,512]{2,1,0:T(8,128)(2,1)}, u32[]{:S(2)}) copy-start(bf16[1,2048,512]{2,1,0:T(8,128)(2,1)} %param.27) | copy-start | bytes 6291460
  7.2 548.9 %all-gather.5.cloned.1.call-start = ((), (), s32[]{:S(2)}) async-start(), calls=%async_computation.1 | async-start | bytes 9437184 | tf_op jit(solution)/shard_map/all_gather | solution.py:231
  7.2 3.3 copy-start.2
  47.2 28.3 %copy-start.8 = (bf16[512,2048]{1,0:T(8,128)(2,1)S(1)}, bf16[512,2048]{1,0:T(8,128)(2,1)}, u32[]{:S(2)}) copy-start(bf16[512,2048]{1,0:T(8,128)(2,1)} %get-tuple-element.217) | copy-start | bytes 6291460 | tf_op jit(solution)/shard_map/while/body/eval_jaxpr/cond
  88.1 5.1 collective-permute-start
  96.2 43.8 %collective-permute-start = (bf16[2048,512]{1,0:T(8,128)(2,1)}, bf16[2048,512]{1,0:T(8,128)(2,1)}, u32[]{:S(2)}, u32[]{:S(2)}) collective-permute-start(bf16[2048,512]{1,0:T(8,128)(2,1)} %get-tuple-element.366), channel_id=1, source_target_pairs={{1,0},{2,1},{3,2},{5,4},{6,5},{7,6}} | collective-permute-start | bytes 6291464 | tf_op jit(solution)/shard_map/while/body/eval_jaxpr/ppermute | solution.py:206
  143.0 25.4 %collective-permute-start = (bf16[2048,512]{1,0:T(8,128)(2,1)}, bf16[2048,512]{1,0:T(8,128)(2,1)}, u32[]{:S(2)}, u32[]{:S(2)}) collective-permute-start(bf16[2048,512]{1,0:T(8,128)(2,1)} %get-tuple-element.366), channel_id=1, source_target_pairs={{1,0},{2,1},{3,2},{5,4},{6,5},{7,6}} | collective-permute-start | bytes 6291464 | tf_op jit(solution)/shard_map/while/body/eval_jaxpr/ppermute | solution.py:206
  180.8 3.5 copy-start.10
  184.0 24.9 %collective-permute-start.2 = (f32[1024,512]{1,0:T(8,128)}, f32[1024,512]{1,0:T(8,128)}, u32[]{:S(2)}, u32[]{:S(2)}) collective-permute-start(f32[1024,512]{1,0:T(8,128)} %constant_dynamic-slice_fusion), channel_id=1, source_target_pairs={{0,4},{4,0},{1,5},{5,1},{2,6},{6,2},{3,7},{7,3}} | collective-permute-start | bytes 6291464 | tf_op jit(solution)/shard_map/ppermute | solution.py:222
  196.9 34.5 %collective-permute-start.1 = (f32[256,2048]{1,0:T(8,128)}, f32[256,2048]{1,0:T(8,128)}, u32[]{:S(2)}, u32[]{:S(2)}) collective-permute-start(f32[256,2048]{1,0:T(8,128)} %constant_dynamic-slice_fusion.1), channel_id=1, source_target_pairs={{0,4},{4,0},{1,5},{5,1},{2,6},{6,2},{3,7},{7,3}} | collective-permute-start | bytes 6291464 | tf_op jit(solution)/shard_map/ppermute | solution.py:221
  198.8 32.6 %copy-start.4 = (f32[512,2048]{1,0:T(8,128)S(1)}, f32[512,2048]{1,0:T(8,128)}, u32[]{:S(2)}) copy-start(f32[512,2048]{1,0:T(8,128)} %bitcast_add_fusion.1) | copy-start | bytes 12582916
  372.2 183.8 %all-gather.3.cloned.1.call-start = ((), (), s32[]{:S(2)}) async-start(), calls=%async_computation | async-start | bytes 9437184 | tf_op jit(solution)/shard_map/all_gather | solution.py:231
  379.4 80.2 %collective-permute-start.4 = (f32[1024,512]{1,0:T(8,128)}, f32[1024,512]{1,0:T(8,128)}, u32[]{:S(2)}, u32[]{:S(2)}) collective-permute-start(f32[1024,512]{1,0:T(8,128)} %get-tuple-element.285), channel_id=1, source_target_pairs={{0,4},{4,0},{1,5},{5,1},{2,6},{6,2},{3,7},{7,3}} | collective-permute-start | bytes 6291464 | tf_op jit(solution)/shard_map/ppermute | solution.py:224
  380.7 156.3 %collective-permute-start.3 = (f32[256,2048]{1,0:T(8,128)}, f32[256,2048]{1,0:T(8,128)}, u32[]{:S(2)}, u32[]{:S(2)}) collective-permute-start(f32[256,2048]{1,0:T(8,128)} %get-tuple-element.287), channel_id=1, source_target_pairs={{0,4},{4,0},{1,5},{5,1},{2,6},{6,2},{3,7},{7,3}} | collective-permute-start | bytes 6291464 | tf_op jit(solution)/shard_map/ppermute | solution.py:223
  380.9 156.1 %copy-start.9 = (f32[256,2048]{1,0:T(8,128)S(1)}, f32[256,2048]{1,0:T(8,128)}, u32[]{:S(2)}) copy-start(f32[256,2048]{1,0:T(8,128)} %get-tuple-element.287) | copy-start | bytes 6291460
  459.6 80.6 %copy-start.6 = (f32[1,2048,512]{2,1,0:T(8,128)S(1)}, f32[1,2048,512]{2,1,0:T(8,128)}, u32[]{:S(2)}) copy-start(f32[1,2048,512]{2,1,0:T(8,128)} %param.24) | copy-start | bytes 12582916
  464.6 75.6 %copy-start.1 = (f32[1,2048,512]{2,1,0:T(8,128)S(1)}, f32[1,2048,512]{2,1,0:T(8,128)}, u32[]{:S(2)}) copy-start(f32[1,2048,512]{2,1,0:T(8,128)} %param.20) | copy-start | bytes 12582916
  464.6 75.6 %copy-start.5 = (f32[1,2048,512]{2,1,0:T(8,128)S(1)}, f32[1,2048,512]{2,1,0:T(8,128)}, u32[]{:S(2)}) copy-start(f32[1,2048,512]{2,1,0:T(8,128)} %param.22) | copy-start | bytes 12582916
  540.2 7.9 %copy-start.3 = (f32[1,512,2048]{2,1,0:T(8,128)S(1)}, f32[1,512,2048]{2,1,0:T(8,128)}, u32[]{:S(2)}) copy-start(f32[1,512,2048]{2,1,0:T(8,128)} %param.19) | copy-start | bytes 12582916
  540.2 8.0 %copy-start.7 = (f32[1,512,2048]{2,1,0:T(8,128)S(1)}, f32[1,512,2048]{2,1,0:T(8,128)}, u32[]{:S(2)}) copy-start(f32[1,512,2048]{2,1,0:T(8,128)} %param.21) | copy-start | bytes 12582916
Sparse Core Ops, SparseCore 0:
  372.4 84.5 all-gather.4
  458.8 82.0 all-gather.2

commit v2 on v1

--- a/solution.py
+++ b/solution.py
@@ -19,10 +19,8 @@
 CHUNK = 512
 SLOTS = 8
 LAG = 6
-
-
-def gelu_tanh(gelu_in):
-    return jax.nn.gelu(gelu_in, approximate=True)
+ROWS = 256
+PART = 512
 
 
 def fast_gelu(z):
@@ -171,59 +169,203 @@
     )(x_rows, w_first, w_second)
 
 
+def backward_kernel(act_ref, dout_ref, w1_ref, w2_ref, acc1_ref, acc2_ref, g1_ref, g2_ref, sq_ref,
+                    actv, grad, w1v, w2v, hid, slope, dpre, sent, accv, inbox,
+                    lsem, asem, csend, crecv, rsend, rrecv):
+    stage = lax.axis_index('stage')
+    rep = lax.axis_index('data')
+    far = 1 - rep
+    n_rows, dim = actv.shape
+    width = w1v.shape[1]
+    n_chunks = n_rows // ROWS
+    last = 3
+    half1 = dim // 2
+    half2 = width // 2
+    n_parts = inbox.shape[0]
+    n_cols = width // PART
+
+    def chunk(idx):
+        return pl.ds(pl.multiple_of(idx * ROWS, ROWS), ROWS)
+
+    def peer(**where):
+        return dict(device_id=where, device_id_type=pl.DeviceIdType.MESH)
+
+    loads = [pltpu.make_async_copy(act_ref, actv, lsem.at[0]), pltpu.make_async_copy(w1_ref, w1v, lsem.at[1]), pltpu.make_async_copy(w2_ref, w2v, lsem.at[2])]
+    for copy in loads:
+        copy.start()
+    top = pltpu.make_async_copy(dout_ref, grad, lsem.at[3])
+
+    @pl.when(stage == last)
+    def _():
+        top.start()
+
+    def load_acc(idx, side, step):
+        slot = step % accv.shape[0]
+        if idx < n_cols:
+            src = acc1_ref.at[pl.ds(pl.multiple_of(side * half1, half1), half1), pl.ds(idx * PART, PART)]
+        else:
+            src = acc2_ref.at[pl.ds(pl.multiple_of(side * half2 + (idx - n_cols) * half1, half1), half1), :]
+        return pltpu.make_async_copy(src, accv.at[slot], asem.at[slot])
+
+    steps = [(idx, far) for idx in range(n_parts)] + [(idx, rep) for idx in range(n_parts)]
+    ahead = accv.shape[0]
+    for step in range(ahead):
+        load_acc(*steps[step], step).start()
+
+    barrier = pltpu.get_barrier_semaphore()
+    pl.semaphore_signal(barrier, inc=1, **peer(stage=(stage + 1) % 4))
+    pl.semaphore_signal(barrier, inc=1, **peer(stage=(stage + 3) % 4))
+    pl.semaphore_signal(barrier, inc=1, **peer(data=far))
+    pl.semaphore_wait(barrier, 3)
+
+    def hop(idx):
+        return pltpu.make_async_remote_copy(src_ref=sent.at[chunk(idx)], dst_ref=grad.at[chunk(idx)], send_sem=csend.at[idx], recv_sem=crecv.at[idx],
+                                            **peer(stage=(stage + 3) % 4))
+
+    def prepare(idx):
+        act = actv[chunk(idx), :]
+        for first in range(0, width, CHUNK):
+            cols = slice(first, first + CHUNK)
+            z = jnp.dot(act, w1v[:, cols], preferred_element_type=jnp.float32)
+            sq = z * z
+            th = jnp.tanh(z * (0.7978845608028654 + 0.035677408136300125 * sq))
+            gate = 0.5 + 0.5 * th
+            hid[chunk(idx), cols] = (z * gate).astype(jnp.bfloat16)
+            slope[chunk(idx), cols] = gate + (0.5 * z) * (1.0 - th * th) * (0.7978845608028654 + 0.10703222440890037 * sq)
+
+    def descend(idx):
+        grad_rows = grad[chunk(idx), :]
+        total = None
+        for first in range(0, width, CHUNK):
+            cols = slice(first, first + CHUNK)
+            d_hid = lax.dot_general(grad_rows, w2v[cols, :], TRANS_DIMS, preferred_element_type=jnp.float32)
+            d_pre = (slope[chunk(idx), cols] * d_hid).astype(jnp.bfloat16)
+            dpre[chunk(idx), cols] = d_pre
+            part = lax.dot_general(d_pre, w1v[:, cols], TRANS_DIMS, preferred_element_type=jnp.float32)
+            total = part if first == 0 else total + part
+        sent[chunk(idx), :] = (grad_rows.astype(jnp.float32) + total).astype(jnp.bfloat16)
+
+    for copy in loads:
+        copy.wait()
+    prepare(0)
+
+    @pl.when(stage == last)
+    def _():
+        top.wait()
+
+    @pl.loop(0, n_chunks)
+    def _(idx):
+        @pl.when(stage < last)
+        def _():
+            hop(idx).wait_recv()
+
+        descend(idx)
+
+        @pl.when(stage > 0)
+        def _():
+            hop(idx).start()
+
+        @pl.when(idx + 1 < n_chunks)
+        def _():
+            prepare(idx + 1)
+
+    def weight_grad(idx, side):
+        if idx < n_cols:
+            left = actv[:, pl.ds(pl.multiple_of(side * half1, half1), half1)]
+            right = dpre[:, idx * PART:(idx + 1) * PART]
+        else:
+            left = hid[:, pl.ds(pl.multiple_of(side * half2 + (idx - n_cols) * half1, half1), half1)]
+            right = grad[...]
+        return lax.dot_general(left, right, FIRST_DIMS, preferred_element_type=jnp.float32)
+
+    def own_part(idx):
+        if idx < n_cols:
+            return g1_ref, (slice(None), slice(idx * PART, (idx + 1) * PART))
+        return g2_ref, (slice((idx - n_cols) * half1, (idx - n_cols + 1) * half1), slice(None))
+
+    def outbox(idx):
+        return slope.at[pl.ds((idx // n_cols) * half1, half1), pl.ds((idx % n_cols) * PART, PART)]
+
+    def post(idx):
+        return pltpu.make_async_remote_copy(src_ref=outbox(idx), dst_ref=inbox.at[idx], send_sem=rsend.at[idx], recv_sem=rrecv.at[idx], **peer(data=far))
+
+    for step, (idx, side) in enumerate(steps):
+        load_acc(idx, side, step).wait()
+        value = accv[step % ahead] + weight_grad(idx, side)
+        if step < n_parts:
+            outbox(idx)[...] = value
+            post(idx).start()
+        else:
+            ref, where = own_part(idx)
+            ref[where] = value
+        if step + ahead < len(steps):
+            load_acc(*steps[step + ahead], step + ahead).start()
+
+    squares = jnp.zeros(sq_ref.shape, jnp.float32)
+    for idx in range(n_parts):
+        post(idx).wait_recv()
+        ref, where = own_part(idx)
+        mean = 0.5 * (ref[where] + inbox[idx])
+        ref[where] = mean
+        squares = squares + jnp.sum((mean * mean).reshape(half1 // 8, 8, PART), axis=0)
+    sq_ref[...] = squares
+    for idx in range(n_parts):
+        post(idx).wait_send()
+
+    @pl.when(stage > 0)
+    def _():
+        @pl.loop(0, n_chunks)
+        def _(idx):
+            hop(idx).wait_send()
+
+
+def backward_all(act, d_out, w_first, w_second, acc_first, acc_second):
+    n_rows, dim = act.shape
+    width = w_first.shape[1]
+    half1 = dim // 2
+    n_chunks = n_rows // ROWS
+    n_parts = 2 * (width // PART)
+    dma = pltpu.SemaphoreType.DMA
+    bf16, f32 = jnp.bfloat16, jnp.float32
+    vmem = pl.BlockSpec(memory_space=pltpu.VMEM)
+    return pl.pallas_call(
+        backward_kernel,
+        out_shape=(jax.ShapeDtypeStruct((half1, width), f32), jax.ShapeDtypeStruct((width // 2, dim), f32), jax.ShapeDtypeStruct((8, PART), f32)),
+        in_specs=[pl.BlockSpec(memory_space=pl.ANY)] * 6,
+        out_specs=(vmem, vmem, vmem),
+        scratch_shapes=[
+            pltpu.VMEM((n_rows, dim), bf16), pltpu.VMEM((n_rows, dim), bf16),
+            pltpu.VMEM((dim, width), bf16), pltpu.VMEM((width, dim), bf16),
+            pltpu.VMEM((n_rows, width), bf16), pltpu.VMEM((n_rows, width), f32), pltpu.VMEM((n_rows, width), bf16),
+            pltpu.VMEM((n_rows, dim), bf16), pltpu.VMEM((4, half1, PART), f32), pltpu.VMEM((n_parts, half1, PART), f32),
+            dma((4,)), dma((4,)), dma((n_chunks,)), dma((n_chunks,)), dma((n_parts,)), dma((n_parts,)),
+        ],
+        compiler_params=pltpu.CompilerParams(collective_id=1, has_side_effects=True, vmem_limit_bytes=63 * 2 ** 20),
+        cost_estimate=pl.CostEstimate(flops=10 * n_rows * dim * width, bytes_accessed=40 * 2 ** 20, transcendentals=0),
+        name='backward_all',
+    )(act, d_out, w_first, w_second, acc_first, acc_second)
+
+
 def solution(mesh):
     n_stage = mesh.shape['stage']
     n_rep = mesh.shape['data']
-    last_stage = n_stage - 1
-    back_perm = [(src, src - 1) for src in range(1, n_stage)]
     swap = [(0, 1), (1, 0)]
     w_spec = P('stage', None, None)
     acc_spec = P('data', 'stage', None, None)
     row_spec = P(None, 'data', None)
 
     def stage_program(w_in, w_out, mom_in, mom_out, var_in, var_out, acc_in, acc_out, stage_acts, d_out, next_x, learn_rate, max_norm):
-        stage_idx = lax.axis_index('stage')
         rep_idx = lax.axis_index('data')
-        w_first = w_in[0].astype(jnp.bfloat16)
-        w_second = w_out[0].astype(jnp.bfloat16)
-        stage_in = stage_acts[0]
-        pre_act = jnp.dot(stage_in, w_first, preferred_element_type=jnp.float32)
-        act_h, gelu_vjp = jax.vjp(gelu_tanh, pre_act)
-        act_h = act_h.astype(jnp.bfloat16)
-
-        def run_active(operands):
-            grad_val = operands[0]
-            d_hid = lax.dot_general(grad_val, w_second, TRANS_DIMS, preferred_element_type=jnp.float32)
-            d_pre = gelu_vjp(d_hid)[0].astype(jnp.bfloat16)
-            d_in = grad_val.astype(jnp.float32) + lax.dot_general(d_pre, w_first, TRANS_DIMS, preferred_element_type=jnp.float32)
-            return d_in.astype(jnp.bfloat16), grad_val, d_pre
-
-        def back_step(step_idx, loop_carry):
-            return lax.cond(stage_idx == last_stage - step_idx, run_active, lambda operands: operands, loop_carry)
-
-        def back_body(step_idx, loop_carry):
-            sent_buf, grad_keep, pre_keep = back_step(step_idx, loop_carry)
-            return lax.ppermute(sent_buf, 'stage', back_perm), grad_keep, pre_keep
-
-        init_carry = (d_out, jnp.zeros_like(d_out), jnp.zeros((stage_in.shape[0], w_first.shape[1]), jnp.bfloat16))
-        back_carry = lax.fori_loop(0, last_stage, back_body, init_carry)
-        _, grad_keep, pre_keep = back_step(last_stage, back_carry)
-        dw_first = lax.dot_general(stage_in, pre_keep, FIRST_DIMS, preferred_element_type=jnp.float32)
-        dw_second = lax.dot_general(act_h, grad_keep, FIRST_DIMS, preferred_element_type=jnp.float32)
-        loc_first = acc_in[0, 0] + dw_first
-        loc_second = acc_out[0, 0] + dw_second
+        half_first, half_second, squares = backward_all(
+            stage_acts[0], d_out, w_in[0].astype(jnp.bfloat16), w_out[0].astype(jnp.bfloat16), acc_in[0, 0], acc_out[0, 0])
 
         def half_of(arr, idx):
             size = arr.shape[0] // n_rep
             return lax.dynamic_slice_in_dim(arr, idx * size, size, 0)
 
-        other_idx = 1 - rep_idx
-        half_first = (half_of(loc_first, rep_idx) + lax.ppermute(half_of(loc_first, other_idx), 'data', swap)) / n_rep
-        half_second = (half_of(loc_second, rep_idx) + lax.ppermute(half_of(loc_second, other_idx), 'data', swap)) / n_rep
         far_first = lax.ppermute(half_first, 'data', swap)
         far_second = lax.ppermute(half_second, 'data', swap)
-        part_sq = jnp.sum(half_first * half_first) + jnp.sum(half_second * half_second)
-        total_norm = jnp.sqrt(lax.psum(part_sq, ('data', 'stage')))
+        total_norm = jnp.sqrt(lax.psum(jnp.sum(squares), ('data', 'stage')))
         clip_coef = jnp.minimum(1.0, max_norm[0] / (total_norm + NORM_EPS))
 
         def early(param, moment, second, grad_val):

time: 792 us -> 589 us (0.74)
  Pallas kernels: 203 us -> 320 us
  matrix products: 85.2 us -> 0 us
  waiting for transfers between devices: 186 us -> 109 us
  starting transfers between devices: 70.3 us -> 2.68 us
  blocking collectives: 127 us -> 71.6 us
  local copies, waits for them, and re-layouts: 47.5 us -> 27.1 us
  other arithmetic: 52 us -> 39.9 us
    pallas_call x0 -> x1, Pallas kernels: none -> 119 us  [backward_all(): pl.pallas_call(backward_kernel, out_shape=(jax.ShapeDtypeStruct((half1, w...]
    dot_general x5 -> x0, matrix products: 85.2 us -> none  [the longest x1 28.3 us: run_active(): lax.dot_general(grad_val, w_second, TRANS_DIMS, preferred_element_type=jn...]
    ppermute x1, waiting for transfers between devices: 72.4 us -> 0.01 us  [stage_program(): far_first = lax.ppermute(half_first, 'data', swap)]
    ppermute x5 -> x0, starting transfers between devices: 68.5 us -> none  [the longest x3 67.1 us: back_body(): return (lax.ppermute(sent_buf, 'stage', back_perm), grad_keep, pre_keep)]
    psum x1, blocking collectives: 127 us -> 71.6 us  [stage_program(): total_norm = jnp.sqrt(lax.psum(jnp.sum(squares), ('data', 'stage')))]
    ppermute x5 -> x0, waiting for transfers between devices: 35.1 us -> none  [the longest x1 17.8 us: stage_program(): lax.ppermute(half_of(loc_first, other_idx), 'data', swap)]
    all_gather x2, waiting for transfers between devices: 0.01 us -> 33.9 us  [early(): lax.all_gather(new_w.astype(jnp.bfloat16), ('stage', 'data'), axis=0, til...]
    convert_element_type x4 -> x2, other arithmetic: 19.2 us -> 5.57 us  [the longest x1 3.98 us: stage_program(): w_in[0].astype(jnp.bfloat16)]
  transfers between devices with their start and end apart: 9 -> 4, of which waited for: 7 -> 2; matrix products, arithmetic and copies ran while one was open for 6% -> 5% of each run, Pallas kernels for 0% -> 0%
where the time goes in v2:
time: 589 us; the launch traced here: 586 us
  Pallas kernels  320 us (54%)
  waiting for transfers between devices  109 us (19%)
  blocking collectives  71.6 us (12%)
  other arithmetic  39.9 us (7%)
  local copies, waits for them, and re-layouts  27.1 us (5%)
  between operations  16.1 us (3%)
    pallas_call x1, Pallas kernels, forward_all(): pl.pallas_call(functools.partial(forward_kernel, n_tiles), out_shape=jax....  202 us
    pallas_call x1, Pallas kernels, backward_all(): pl.pallas_call(backward_kernel, out_shape=(jax.ShapeDtypeStruct((half1, w...  119 us
    ppermute x1, waiting for transfers between devices, stage_program(): far_second = lax.ppermute(half_second, 'data', swap)  74.6 us
    psum x1, blocking collectives, stage_program(): total_norm = jnp.sqrt(lax.psum(jnp.sum(squares), ('data', 'stage')))  71.6 us
    all_gather x2, waiting for transfers between devices, early(): lax.all_gather(new_w.astype(jnp.bfloat16), ('stage', 'data'), axis=0, til...  33.9 us
    unnamed x13, local copies, waits for them, and re-layouts  27.1 us
    sub x2, other arithmetic, adamw_update(): param_old - lr_value * (mom_hat / (jnp.sqrt(sec_hat) + ADAM_EPS) + WEIGHT...  17.4 us
    concatenate x2, other arithmetic, whole(): jnp.concatenate([jnp.where(is_low, near, far), jnp.where(is_low, far, nea...  15.6 us
  transfers between devices with their start and end apart: 4, of which 2 were waited for; matrix products, arithmetic and copies ran while one was open for 5% of the time, Pallas kernels for 0%

profile of v2, /device:TPU:7, one launch (start us, length us, event | category | flops | bytes accessed | tf_op | source)
XLA Modules:
  0.0 586.1 jit_solution(8732911824371477128)
XLA Ops:
  7.2 0.0 all-gather.3.cloned.1.call-start
  7.2 0.0 copy-start
  7.2 4.0 convert_bitcast_fusion.1.w1_ref
  11.2 1.6 convert_bitcast_fusion.w2_ref
  12.8 118.6 %backward_all.1 = (f32[256,2048]{1,0:T(8,128)}, f32[1024,512]{1,0:T(8,128)}, f32[8,512]{1,0:T(8,128)}) custom-call(bf16[2048,512]{1,0:T(8,128)(2,1)} %bitcast.74, bf16[2048,512]{1,0:T(8,128)(2,1)} %dout_ref.1, bf16[512,2048]{1,0:T(8,128)(2,1)} %convert_bitcast_fusion.1.w1_ref, bf16[2048,512]{1,0:T(8,128)(2,1)} %convert_bitcast_fusion.w2_ref, ...), custom_call_target="tpu_custom_call" | custom-call | flops 21474836480 | bytes 41943040 | tf_op jit(solution)/shard_map/backward_all/pallas_call | solution.py:331
  131.4 1.2 collective-permute-start
  132.6 1.3 reduce_sum.9
  134.0 71.6 %psum.7 = f32[]{:T(128)} all-reduce(f32[]{:T(128)} %reduce_sum.9), channel_id=1, replica_groups=mesh['data'=2,'stage'=4] {'data','stage'}, use_global_device_ids=true, to_apply=%region_1.0 | all-reduce | flops 1 | bytes 8 | tf_op jit(solution)/shard_map/psum | solution.py:368
  207.6 1.3 copy-done.5
  208.9 7.6 %select_bitcast_fusion.3 = (f32[1,256,2048]{2,1,0:T(8,128)S(1)}, f32[1,256,2048]{2,1,0:T(8,128)}, bf16[256,2048]{1,0:T(8,128)(2,1)}) fusion(f32[256,2048]{1,0:T(8,128)} %get-tuple-element.11, f32[256,2048]{1,0:T(8,128)} %copy-done.5, pred[]{:T(512)S(6)} %eq.4, f32[1,512,2048]{2,1,0:T(8,128)} %param.17, s32[]{:T(128)S(6)} %select_n.40, f32[]{:T(128)S(6)} %min_shard_map.3, ...), kind=kLoop, calls=%fused_computation.37 | loop fusion | flops 9961472 | bytes 15728653 | tf_op jit(solution)/shard_map/concatenate | solution.py:383
  216.5 0.0 all-gather.3.cloned.1.call-update
  216.5 0.0 all-gather.5.cloned.1.call-start
  216.6 1.4 collective-permute-start.1
  218.0 74.6 %collective-permute-done.1 = f32[1024,512]{1,0:T(8,128)} collective-permute-done((f32[1024,512]{1,0:T(8,128)}, f32[1024,512]{1,0:T(8,128)}, u32[]{:S(2)}, u32[]{:S(2)}) %collective-permute-start.1) | collective-permute-done | bytes 2097184 | tf_op jit(solution)/shard_map/ppermute | solution.py:367
  292.6 8.0 %select_bitcast_fusion.1 = (f32[1,1024,512]{2,1,0:T(8,128)}, f32[1,1024,512]{2,1,0:T(8,128)}, bf16[1024,512]{1,0:T(8,128)(2,1)}) fusion(f32[1024,512]{1,0:T(8,128)} %get-tuple-element.12, f32[1024,512]{1,0:T(8,128)} %collective-permute-done.1, pred[]{:T(512)S(6)} %eq.4, f32[1,2048,512]{2,1,0:T(8,128)} %param.18, s32[]{:T(128)S(6)} %select_n.41, ...), kind=kLoop, calls=%fused_computation.35 | loop fusion | flops 9961472 | bytes 15728653 | tf_op jit(solution)/shard_map/concatenate | solution.py:383
  300.6 0.0 all-gather.5.cloned.1.call-update
  300.7 11.6 %multiply_subtract_fusion = (f32[1,2048,512]{2,1,0:T(8,128)}, f32[1,2048,512]{2,1,0:T(8,128)}, f32[1,2048,512]{2,1,0:T(8,128)}) fusion(f32[1,2048,512]{2,1,0:T(8,128)} %param.14, f32[]{:T(128)} %bitcast.64, f32[1,1024,512]{2,1,0:T(8,128)} %get-tuple-element.20, f32[1,1024,512]{2,1,0:T(8,128)} %get-tuple-element.19, f32[]{:T(128)S(6)} %min_shard_map.3, ...), kind=kLoop, calls=%fused_computation.6 | loop fusion | flops 17825792 | bytes 29360136 | tf_op jit(solution)/shard_map/sub | solution.py:38
  312.3 1.1 copy-done.2
  313.4 1.2 copy-done.3
  314.6 0.6 copy-done.4
  315.2 5.8 multiply_subtract_fusion.1
  320.9 33.9 %all-gather.5.cloned.1.call-done = bf16[8192,512]{1,0:T(8,128)(2,1)} async-done(((bf16[1024,512]{1,0:T(8,128)(2,1)}), bf16[8192,512]{1,0:T(8,128)(2,1)}) %all-gather.5.cloned.1.call-update) | async-done | bytes 8388624 | tf_op jit(solution)/shard_map/all_gather | solution.py:373
  354.9 201.6 %forward_all.1 = bf16[32768,512]{1,0:T(8,128)(2,1)} custom-call(bf16[32768,512]{1,0:T(8,128)(2,1)} %bitcast.69, bf16[4,512,2048]{2,1,0:T(8,128)(2,1)} %bitcast.70, bf16[4,2048,512]{2,1,0:T(8,128)(2,1)} %bitcast.71), custom_call_target="tpu_custom_call" | custom-call | flops 137438953472 | bytes 67108864 | tf_op jit(solution)/shard_map/forward_all/pallas_call | solution.py:153
  556.4 22.9 %copy.23 = bf16[16,2048,512]{2,1,0:T(8,128)(2,1)} copy(bf16[16,2048,512]{2,1,0:T(8,128)(2,1)} %bitcast.68) | data formatting | bytes 67108864
  (9 shorter events, 0.0 us)
Async XLA Ops:
  7.2 313.8 %all-gather.3.cloned.1.call-start = ((), (), s32[]{:S(2)}) async-start(), calls=%async_computation | async-start | bytes 9437184 | tf_op jit(solution)/shard_map/all_gather | solution.py:373
  7.2 4.0 copy-start
  131.4 76.2 %collective-permute-start = (f32[256,2048]{1,0:T(8,128)}, f32[256,2048]{1,0:T(8,128)S(1)}, u32[]{:S(2)}, u32[]{:S(2)}) collective-permute-start(f32[256,2048]{1,0:T(8,128)} %get-tuple-element.11), channel_id=1, source_target_pairs={{0,4},{4,0},{1,5},{5,1},{2,6},{6,2},{3,7},{7,3}} | collective-permute-start | bytes 6291464 | tf_op jit(solution)/shard_map/ppermute | solution.py:366
  207.6 1.3 copy-start.5
  216.5 138.3 %all-gather.5.cloned.1.call-start = ((), (), s32[]{:S(2)}) async-start(), calls=%async_computation.1 | async-start | bytes 9437184 | tf_op jit(solution)/shard_map/all_gather | solution.py:373
  216.6 76.0 %collective-permute-start.1 = (f32[1024,512]{1,0:T(8,128)}, f32[1024,512]{1,0:T(8,128)}, u32[]{:S(2)}, u32[]{:S(2)}) collective-permute-start(f32[1024,512]{1,0:T(8,128)} %get-tuple-element.12), channel_id=1, source_target_pairs={{0,4},{4,0},{1,5},{5,1},{2,6},{6,2},{3,7},{7,3}} | collective-permute-start | bytes 6291464 | tf_op jit(solution)/shard_map/ppermute | solution.py:367
  300.6 11.7 %copy-start.1 = (f32[1,512,2048]{2,1,0:T(8,128)S(1)}, f32[1,512,2048]{2,1,0:T(8,128)}, u32[]{:S(2)}) copy-start(f32[1,512,2048]{2,1,0:T(8,128)} %param.13) | copy-start | bytes 12582916
  300.6 12.7 %copy-start.2 = (f32[1,512,2048]{2,1,0:T(8,128)S(1)}, f32[1,512,2048]{2,1,0:T(8,128)}, u32[]{:S(2)}) copy-start(f32[1,512,2048]{2,1,0:T(8,128)} %param.17) | copy-start | bytes 12582916
  300.7 13.9 %copy-start.3 = (f32[1,512,2048]{2,1,0:T(8,128)S(1)}, f32[1,512,2048]{2,1,0:T(8,128)}, u32[]{:S(2)}) copy-start(f32[1,512,2048]{2,1,0:T(8,128)} %param.15) | copy-start | bytes 12582916
  300.7 14.5 %copy-start.4 = (f32[1,256,2048]{2,1,0:T(8,128)S(1)}, f32[1,256,2048]{2,1,0:T(8,128)}, u32[]{:S(2)}) copy-start(f32[1,256,2048]{2,1,0:T(8,128)} %get-tuple-element.22) | copy-start | bytes 6291460
Sparse Core Ops, SparseCore 0:
  216.7 82.6 all-gather.2
  301.2 53.6 all-gather.4

commit v3 on v2

v3 whole, which is shorter than its diff:
```python
import functools

import jax
import jax.numpy as jnp
from jax import lax
from jax.experimental import pallas as pl
from jax.experimental.pallas import tpu as pltpu
from jax.sharding import PartitionSpec as P

BETA_ONE = 0.9
BETA_TWO = 0.95
ADAM_EPS = 1e-8
WEIGHT_DECAY = 0.1
STEP_COUNT = 10
NORM_EPS = 1e-6
TRANS_DIMS = (((1,), (1,)), ((), ()))
FIRST_DIMS = (((0,), (0,)), ((), ()))
TILE = 512
CHUNK = 512
SLOTS = 8
LAG = 4
PRE = 4
SHARED = 4
UPDATE_STEPS = 8
ROWS = 256
PART = 512


def fast_gelu(z):
    inner = z * (0.7978845608028654 + 0.035677408136300125 * (z * z))
    half = 0.5 * z
    return half + half * jnp.tanh(inner)


def forward_kernel(n_own, n_both, x_ref, w1_ref, w2_ref, g1_ref, g2_ref, y_ref, far1_ref, far2_ref,
                   xv, pv, yv, w1v, w2v, xsem, psem, lsem, osem, csend, asend, rsend, crecv, arecv, rrecv, wsend, wrecv, fsend, frecv):
    stage = lax.axis_index('stage')
    rep = lax.axis_index('data')
    far = 1 - rep
    core = stage % 2
    partner = stage + 1 - 2 * core
    across = (stage + 2) % 4
    corner = (partner + 2) % 4
    early = stage < 2
    n_tiles = n_own + n_both
    n_blocks, dim, width = w1v.shape
    half1, half2 = dim // 2, width // 2
    to_core, to_chip, to_rep = {'stage': partner}, {'stage': across}, {'data': far}

    def rows(owner, tile):
        place = jnp.where(tile < n_own, owner * n_own + tile, 4 * n_own + (owner % 2) * n_both + tile - n_own)
        return pl.ds(pl.multiple_of(place * TILE, TILE), TILE)

    def remote(src, dst, send, recv, target):
        return pltpu.make_async_remote_copy(src_ref=src, dst_ref=dst, send_sem=send, recv_sem=recv, device_id=target, device_id_type=pl.DeviceIdType.MESH)

    def load_x(tile):
        return pltpu.make_async_copy(x_ref.at[rows(stage, tile)], xv.at[tile % 2], xsem.at[tile % 2])

    def load_p(tile):
        return pltpu.make_async_copy(x_ref.at[rows(stage, tile)], pv.at[tile], psem.at[tile])

    def part(owner, block, kind):
        if kind == 0:
            return w1v.at[block, pl.ds(pl.multiple_of(owner * half1, half1), half1), :]
        return w2v.at[block, pl.ds(pl.multiple_of(owner * half2, half2), half2), :]

    def move(owner, block, kind, target, lane):
        ref = part(owner, block, kind)
        return remote(ref, ref, wsend.at[lane], wrecv.at[(owner * n_blocks + block) * 2 + kind], target)

    def arrive(owner, block, kind):
        move(owner, block, kind, to_core, 0).wait_recv()

    own = [pltpu.make_async_copy(ref, part(rep, stage, kind), lsem.at[kind]) for kind, ref in enumerate((w1_ref, w2_ref))]
    for copy in own:
        copy.start()

    @pl.when(early)
    def _():
        for tile in range(PRE):
            load_p(tile).start()

    @pl.when(stage >= 2)
    def _():
        load_x(0).start()

    barrier = pltpu.get_barrier_semaphore()
    for target in (to_core, to_chip, to_rep):
        pl.semaphore_signal(barrier, inc=1, device_id=target, device_id_type=pl.DeviceIdType.MESH)
    pl.semaphore_wait(barrier, 3)

    sends = []

    def send(owner, block, kind, target):
        copy = move(owner, block, kind, target, len(sends))
        sends.append(copy)
        copy.start()

    for kind in (0, 1):
        own[kind].wait()
        for target in (to_chip, to_rep, to_core):
            send(rep, stage, kind, target)
    arrive(far, stage, 0)
    send(far, stage, 0, to_core)
    arrive(rep, across, 0)
    send(rep, across, 0, to_rep)
    send(rep, across, 0, to_core)
    arrive(far, stage, 1)
    send(far, stage, 1, to_chip)
    send(far, stage, 1, to_core)
    arrive(rep, across, 1)
    send(rep, across, 1, to_core)
    for owner in (rep, far):
        for kind in (0, 1):
            arrive(owner, partner, kind)

    def block_step(x_rows, block):
        total = None
        for first in range(0, width, CHUNK):
            hidden = jnp.dot(x_rows, w1v[block, :, first:first + CHUNK], preferred_element_type=jnp.float32)
            act_h = fast_gelu(hidden).astype(jnp.bfloat16)
            piece = jnp.dot(act_h, w2v[block, first:first + CHUNK, :], preferred_element_type=jnp.float32)
            total = piece if first == 0 else total + piece
        return (x_rows.astype(jnp.float32) + total).astype(jnp.bfloat16)

    @pl.when(early)
    def _():
        @pl.loop(0, PRE)
        def _(tile):
            load_p(tile).wait()

            @pl.loop(0, 2)
            def _(block):
                pv[tile] = block_step(pv[tile], block)

    for kind in (0, 1):
        arrive(far, across, kind)
        send(far, across, kind, to_core)
    swaps = [remote(src, dst, fsend.at[idx], frecv.at[idx], to_rep) for idx, (src, dst) in enumerate(((g1_ref, far1_ref), (g2_ref, far2_ref)))]
    for copy in swaps:
        copy.start()
    for owner in (rep, far):
        for kind in (0, 1):
            arrive(owner, corner, kind)

    def store_own(tile):
        return pltpu.make_async_copy(yv.at[tile % SLOTS], y_ref.at[rows(stage, tile)], osem.at[tile % SLOTS])

    def give_core(tile):
        return remote(yv.at[tile % SLOTS], y_ref.at[rows(stage, tile)], csend.at[tile % SLOTS], crecv.at[tile], to_core)

    def give_chip(tile):
        return remote(yv.at[tile % SLOTS], y_ref.at[rows(stage, tile)], asend.at[tile % SLOTS], arecv.at[tile], to_chip)

    def pass_on(tile):
        ref = y_ref.at[rows(across, tile)]
        return remote(ref, ref, rsend.at[tile], rrecv.at[tile], to_core)

    def relay(tile):
        ref = y_ref.at[rows(across, tile)]
        remote(ref, ref, asend.at[0], arecv.at[tile], to_chip).wait_recv()
        pass_on(tile).start()

    def free_slot(tile):
        store_own(tile).wait()
        give_core(tile).wait_send()

        @pl.when(tile < n_own)
        def _():
            give_chip(tile).wait_send()

    @pl.loop(0, n_tiles)
    def _(tile):
        skip = jnp.where(early, PRE, 0)

        @pl.when(tile < skip)
        def _():
            xv[tile % 2] = pv[tile % PRE]

        @pl.when(tile >= skip)
        def _():
            load_x(tile).wait()

        @pl.when((tile + 1 >= skip) & (tile + 1 < n_tiles))
        def _():
            load_x(tile + 1).start()

        @pl.when(tile >= SLOTS)
        def _():
            free_slot(tile - SLOTS)

        @pl.loop(0, n_blocks)
        def _(block):
            @pl.when((block >= 2) | (tile >= skip))
            def _():
                result = block_step(xv[tile % 2], block)

                @pl.when(block < n_blocks - 1)
                def _():
                    xv[tile % 2] = result

                @pl.when(block == n_blocks - 1)
                def _():
                    yv[tile % SLOTS] = result

        store_own(tile).start()
        give_core(tile).start()

        @pl.when(tile < n_own)
        def _():
            give_chip(tile).start()

        @pl.when((tile >= LAG) & (tile < LAG + n_own))
        def _():
            relay(tile - LAG)

    for tile in range(max(n_tiles - LAG, 0), n_own):
        relay(tile)

    @pl.loop(n_tiles - SLOTS, n_tiles)
    def _(tile):
        free_slot(tile)

    @pl.loop(0, n_tiles)
    def _(tile):
        ref = y_ref.at[rows(partner, tile)]
        remote(ref, ref, csend.at[0], crecv.at[tile], to_core).wait_recv()

    @pl.loop(0, n_own)
    def _(tile):
        ref = y_ref.at[rows(corner, tile)]
        remote(ref, ref, rsend.at[0], rrecv.at[tile], to_core).wait_recv()
        pass_on(tile).wait_send()

    for copy in sends:
        copy.wait_send()
    for copy in swaps:
        copy.wait()


def forward_all(x_rows, w_first, w_second, near_first, near_second, n_stage, n_both):
    n_rows, dim = x_rows.shape
    width = w_first.shape[1]
    n_own = (n_rows // TILE - 2 * n_both) // 4
    n_tiles = n_own + n_both
    dma = pltpu.SemaphoreType.DMA
    flops = 4 * n_tiles * TILE * dim * width * n_stage
    return pl.pallas_call(
        functools.partial(forward_kernel, n_own, n_both),
        out_shape=(jax.ShapeDtypeStruct((n_rows, dim), jnp.bfloat16), jax.ShapeDtypeStruct(near_first.shape, jnp.float32), jax.ShapeDtypeStruct(near_second.shape, jnp.float32)),
        in_specs=[pl.BlockSpec(memory_space=pl.ANY)] * 5,
        out_specs=(pl.BlockSpec(memory_space=pl.ANY),) * 3,
        scratch_shapes=[
            pltpu.VMEM((2, TILE, dim), jnp.bfloat16),
            pltpu.VMEM((PRE, TILE, dim), jnp.bfloat16),
            pltpu.VMEM((SLOTS, TILE, dim), jnp.bfloat16),
            pltpu.VMEM((n_stage, dim, width), jnp.bfloat16),
            pltpu.VMEM((n_stage, width, dim), jnp.bfloat16),
            dma((2,)), dma((PRE,)), dma((2,)), dma((SLOTS,)), dma((SLOTS,)), dma((SLOTS,)), dma((n_own,)),
            dma((n_tiles,)), dma((n_own,)), dma((n_own,)), dma((14,)), dma((4 * n_stage,)), dma((2,)), dma((2,)),
        ],
        compiler_params=pltpu.CompilerParams(collective_id=0, has_side_effects=True, vmem_limit_bytes=56 * 2 ** 20),
        cost_estimate=pl.CostEstimate(flops=flops, bytes_accessed=2 * n_rows * dim * 2, transcendentals=0),
        name='forward_all',
    )(x_rows, w_first, w_second, near_first, near_second)


def adamw_rows(coef, rate, param, moment, second, grad_val):
    scaled = coef * grad_val
    mom_new = BETA_ONE * moment + (1.0 - BETA_ONE) * scaled
    sec_new = BETA_TWO * second + (1.0 - BETA_TWO) * scaled * scaled
    mom_hat = mom_new * (1.0 / (1.0 - BETA_ONE ** STEP_COUNT))
    sec_hat = sec_new * (1.0 / (1.0 - BETA_TWO ** STEP_COUNT))
    return param - rate * (mom_hat / (jnp.sqrt(sec_hat) + ADAM_EPS) + WEIGHT_DECAY * param), mom_new, sec_new


def near_kernel(half_ref, rate_ref, clip_ref, *refs):
    for side in (0, 1):
        param, moment, second, grad_val = (ref[...] for ref in refs[4 * side:4 * side + 4])
        outs = refs[8 + 4 * side:12 + 4 * side]
        news = adamw_rows(clip_ref[0:1, 0:1], rate_ref[0], param, moment, second, grad_val)
        for ref, new in zip(outs, news):
            ref[...] = new
        outs[3][...] = news[0].astype(jnp.bfloat16)


def far_kernel(half_ref, rate_ref, clip_ref, *refs):
    for side in (0, 1):
        param, moment, second, grad_val = (ref[...] for ref in refs[4 * side:4 * side + 4])
        news = adamw_rows(clip_ref[0:1, 0:1], rate_ref[0], param, moment, second, grad_val)
        for ref, new in zip(refs[14 + 3 * side:17 + 3 * side], news):
            ref[...] = new


def half_update(half_idx, rate, clip, first, second, grads, made):
    steps = UPDATE_STEPS
    f32, bf16 = jnp.float32, jnp.bfloat16
    full, grad_specs, out_specs, out_shape = [], [], [], []
    for arr, grad in zip((first[0], second[0]), grads):
        block = (grad.shape[0] // steps, grad.shape[1])
        picked = pl.BlockSpec(block, lambda step, half: (half[0] * steps + step, 0))
        plain = pl.BlockSpec(block, lambda step, half: (step, 0))
        full += [picked] * 3 + [plain]
        out_specs += [picked] * 3
        out_shape += [jax.ShapeDtypeStruct(arr.shape, f32)] * 3
        if made is None:
            out_specs.append(plain)
            out_shape.append(jax.ShapeDtypeStruct(grad.shape, bf16))
    in_specs = [pl.BlockSpec(memory_space=pltpu.SMEM), pl.BlockSpec(clip.shape, lambda step, half: (0, 0))] + full
    args = [half_idx, rate, clip, *first, grads[0], *second, grads[1]]
    aliases = {}
    if made is not None:
        aliases = {len(args) + idx: idx for idx in range(6)}
        in_specs += [pl.BlockSpec(memory_space=pl.ANY)] * 6
        args += list(made)
    return pl.pallas_call(
        near_kernel if made is None else far_kernel,
        out_shape=tuple(out_shape),
        grid_spec=pltpu.PrefetchScalarGridSpec(num_scalar_prefetch=1, grid=(steps,), in_specs=in_specs, out_specs=tuple(out_specs)),
        input_output_aliases=aliases,
        compiler_params=pltpu.CompilerParams(vmem_limit_bytes=48 * 2 ** 20),
        cost_estimate=pl.CostEstimate(flops=30 * 2 ** 20, bytes_accessed=30 * 2 ** 20, transcendentals=0),
        name='near_update' if made is None else 'far_update',
    )(*args)


def backward_kernel(limit_ref, act_ref, dout_ref, w1_ref, w2_ref, acc1_ref, acc2_ref, g1_ref, g2_ref, clip_ref,
                    actv, grad, w1v, w2v, hid, slope, dpre, sent, accv, inbox,
                    norms, lsem, asem, csend, crecv, rsend, rrecv, nsend, nrecv):
    stage = lax.axis_index('stage')
    rep = lax.axis_index('data')
    far = 1 - rep
    n_rows, dim = actv.shape
    width = w1v.shape[1]
    n_chunks = n_rows // ROWS
    last = 3
    half1 = dim // 2
    half2 = width // 2
    n_parts = inbox.shape[0]
    n_cols = width // PART

    def chunk(idx):
        return pl.ds(pl.multiple_of(idx * ROWS, ROWS), ROWS)

    def peer(**where):
        return dict(device_id=where, device_id_type=pl.DeviceIdType.MESH)

    loads = [pltpu.make_async_copy(act_ref, actv, lsem.at[0]), pltpu.make_async_copy(w1_ref, w1v, lsem.at[1]), pltpu.make_async_copy(w2_ref, w2v, lsem.at[2])]
    for copy in loads:
        copy.start()
    top = pltpu.make_async_copy(dout_ref, grad, lsem.at[3])

    @pl.when(stage == last)
    def _():
        top.start()

    def load_acc(idx, side, step):
        slot = step % accv.shape[0]
        if idx < n_cols:
            src = acc1_ref.at[pl.ds(pl.multiple_of(side * half1, half1), half1), pl.ds(idx * PART, PART)]
        else:
            src = acc2_ref.at[pl.ds(pl.multiple_of(side * half2 + (idx - n_cols) * half1, half1), half1), :]
        return pltpu.make_async_copy(src, accv.at[slot], asem.at[slot])

    steps = [(idx, far) for idx in range(n_parts)] + [(idx, rep) for idx in range(n_parts)]
    ahead = accv.shape[0]
    for step in range(ahead):
        load_acc(*steps[step], step).start()

    barrier = pltpu.get_barrier_semaphore()
    place = rep * 4 + stage
    others = [(place + hop) % 8 for hop in range(1, 8)]
    for other in others:
        pl.semaphore_signal(barrier, inc=1, **peer(data=other // 4, stage=other % 4))
    pl.semaphore_wait(barrier, 7)

    def hop(idx):
        return pltpu.make_async_remote_copy(src_ref=sent.at[chunk(idx)], dst_ref=grad.at[chunk(idx)], send_sem=csend.at[idx], recv_sem=crecv.at[idx],
                                            **peer(stage=(stage + 3) % 4))

    def prepare(idx):
        act = actv[chunk(idx), :]
        for first in range(0, width, CHUNK):
            cols = slice(first, first + CHUNK)
            z = jnp.dot(act, w1v[:, cols], preferred_element_type=jnp.float32)
            sq = z * z
            th = jnp.tanh(z * (0.7978845608028654 + 0.035677408136300125 * sq))
            gate = 0.5 + 0.5 * th
            hid[chunk(idx), cols] = (z * gate).astype(jnp.bfloat16)
            slope[chunk(idx), cols] = gate + (0.5 * z) * (1.0 - th * th) * (0.7978845608028654 + 0.10703222440890037 * sq)

    def descend(idx):
        grad_rows = grad[chunk(idx), :]
        total = None
        for first in range(0, width, CHUNK):
            cols = slice(first, first + CHUNK)
            d_hid = lax.dot_general(grad_rows, w2v[cols, :], TRANS_DIMS, preferred_element_type=jnp.float32)
            d_pre = (slope[chunk(idx), cols] * d_hid).astype(jnp.bfloat16)
            dpre[chunk(idx), cols] = d_pre
            part = lax.dot_general(d_pre, w1v[:, cols], TRANS_DIMS, preferred_element_type=jnp.float32)
            total = part if first == 0 else total + part
        sent[chunk(idx), :] = (grad_rows.astype(jnp.float32) + total).astype(jnp.bfloat16)

    for copy in loads:
        copy.wait()
    prepare(0)

    @pl.when(stage == last)
    def _():
        top.wait()

    @pl.loop(0, n_chunks)
    def _(idx):
        @pl.when(stage < last)
        def _():
            hop(idx).wait_recv()

        descend(idx)

        @pl.when(stage > 0)
        def _():
            hop(idx).start()

        @pl.when(idx + 1 < n_chunks)
        def _():
            prepare(idx + 1)

    def weight_grad(idx, side):
        if idx < n_cols:
            left = actv[:, pl.ds(pl.multiple_of(side * half1, half1), half1)]
            right = dpre[:, idx * PART:(idx + 1) * PART]
        else:
            left = hid[:, pl.ds(pl.multiple_of(side * half2 + (idx - n_cols) * half1, half1), half1)]
            right = grad[...]
        return lax.dot_general(left, right, FIRST_DIMS, preferred_element_type=jnp.float32)

    def own_part(idx):
        if idx < n_cols:
            return g1_ref, (slice(None), slice(idx * PART, (idx + 1) * PART))
        return g2_ref, (slice((idx - n_cols) * half1, (idx - n_cols + 1) * half1), slice(None))

    def outbox(idx):
        return slope.at[pl.ds((idx // n_cols) * half1, half1), pl.ds((idx % n_cols) * PART, PART)]

    def post(idx):
        return pltpu.make_async_remote_copy(src_ref=outbox(idx), dst_ref=inbox.at[idx], send_sem=rsend.at[idx], recv_sem=rrecv.at[idx], **peer(data=far))

    for step, (idx, side) in enumerate(steps):
        load_acc(idx, side, step).wait()
        value = accv[step % ahead] + weight_grad(idx, side)
        if step < n_parts:
            outbox(idx)[...] = value
            post(idx).start()
        else:
            ref, where = own_part(idx)
            ref[where] = value
        if step + ahead < len(steps):
            load_acc(*steps[step + ahead], step + ahead).start()

    squares = jnp.zeros((8, PART), jnp.float32)
    for idx in range(n_parts):
        post(idx).wait_recv()
        ref, where = own_part(idx)
        mean = 0.5 * (ref[where] + inbox[idx])
        ref[where] = mean
        squares = squares + jnp.sum((mean * mean).reshape(half1 // 8, 8, PART), axis=0)
    norms[place] = squares

    def tell(idx):
        return pltpu.make_async_remote_copy(src_ref=norms.at[place], dst_ref=norms.at[place], send_sem=nsend.at[idx], recv_sem=nrecv.at[place],
                                            **peer(data=others[idx] // 4, stage=others[idx] % 4))

    def hear(idx):
        ref = norms.at[others[idx]]
        return pltpu.make_async_remote_copy(src_ref=ref, dst_ref=ref, send_sem=nsend.at[idx], recv_sem=nrecv.at[others[idx]],
                                            **peer(data=others[idx] // 4, stage=others[idx] % 4))

    for idx in range(7):
        tell(idx).start()
    for idx in range(7):
        hear(idx).wait_recv()
    total = norms[0]
    for idx in range(1, 8):
        total = total + norms[idx]
    total = jnp.sum(jnp.sum(total, axis=0, keepdims=True), axis=1, keepdims=True)
    clip = jnp.minimum(1.0, limit_ref[0] / (jnp.sqrt(total) + NORM_EPS))
    clip_ref[...] = jnp.broadcast_to(clip, clip_ref.shape)
    for idx in range(7):
        tell(idx).wait_send()
    for idx in range(n_parts):
        post(idx).wait_send()

    @pl.when(stage > 0)
    def _():
        @pl.loop(0, n_chunks)
        def _(idx):
            hop(idx).wait_send()


def backward_all(limit, act, d_out, w_first, w_second, acc_first, acc_second):
    n_rows, dim = act.shape
    width = w_first.shape[1]
    half1 = dim // 2
    n_chunks = n_rows // ROWS
    n_parts = 2 * (width // PART)
    dma = pltpu.SemaphoreType.DMA
    bf16, f32 = jnp.bfloat16, jnp.float32
    vmem = pl.BlockSpec(memory_space=pltpu.VMEM)
    return pl.pallas_call(
        backward_kernel,
        out_shape=(jax.ShapeDtypeStruct((half1, width), f32), jax.ShapeDtypeStruct((width // 2, dim), f32), jax.ShapeDtypeStruct((8, 128), f32)),
        in_specs=[pl.BlockSpec(memory_space=pltpu.SMEM)] + [pl.BlockSpec(memory_space=pl.ANY)] * 6,
        out_specs=(vmem, vmem, vmem),
        scratch_shapes=[
            pltpu.VMEM((n_rows, dim), bf16), pltpu.VMEM((n_rows, dim), bf16),
            pltpu.VMEM((dim, width), bf16), pltpu.VMEM((width, dim), bf16),
            pltpu.VMEM((n_rows, width), bf16), pltpu.VMEM((n_rows, width), f32), pltpu.VMEM((n_rows, width), bf16),
            pltpu.VMEM((n_rows, dim), bf16), pltpu.VMEM((4, half1, PART), f32), pltpu.VMEM((n_parts, half1, PART), f32), pltpu.VMEM((8, 8, PART), f32),
            dma((4,)), dma((4,)), dma((n_chunks,)), dma((n_chunks,)), dma((n_parts,)), dma((n_parts,)), dma((7,)), dma((8,)),
        ],
        compiler_params=pltpu.CompilerParams(collective_id=1, has_side_effects=True, vmem_limit_bytes=63 * 2 ** 20),
        cost_estimate=pl.CostEstimate(flops=10 * n_rows * dim * width, bytes_accessed=40 * 2 ** 20, transcendentals=0),
        name='backward_all',
    )(limit, act, d_out, w_first, w_second, acc_first, acc_second)


def solution(mesh):
    n_stage = mesh.shape['stage']
    w_spec = P('stage', None, None)
    acc_spec = P('data', 'stage', None, None)
    row_spec = P(None, 'data', None)

    def stage_program(w_in, w_out, mom_in, mom_out, var_in, var_out, acc_in, acc_out, stage_acts, d_out, next_x, learn_rate, max_norm):
        rep_idx = lax.axis_index('data')
        near_first, near_second, clip = backward_all(
            max_norm, stage_acts[0], d_out, w_in[0].astype(jnp.bfloat16), w_out[0].astype(jnp.bfloat16), acc_in[0, 0], acc_out[0, 0])
        first = (w_in[0], mom_in[0], var_in[0])
        second = (w_out[0], mom_out[0], var_out[0])
        near = half_update(rep_idx.reshape(1), learn_rate, clip, first, second, (near_first, near_second), None)
        n_micro, n_rows, dim = next_x.shape
        next_y, far_first, far_second = forward_all(next_x.reshape(n_micro * n_rows, dim), near[3], near[7], near_first, near_second, n_stage, SHARED)
        news = half_update((1 - rep_idx).reshape(1), learn_rate, clip, first, second, (far_first, far_second), near[:3] + near[4:7])
        return (news[0][None], news[3][None], news[1][None], news[4][None], news[2][None], news[5][None], next_y.reshape(next_x.shape))

    return jax.shard_map(stage_program, mesh=mesh, in_specs=(w_spec, w_spec, w_spec, w_spec, w_spec, w_spec, acc_spec, acc_spec, P('stage', 'data', None), P('data', None), row_spec, P(None), P(None)), out_specs=(w_spec, w_spec, w_spec, w_spec, w_spec, w_spec, row_spec), check_vma=False)
```

time: 589 us -> 484 us (0.82)
  Pallas kernels: 320 us -> 445 us
  waiting for transfers between devices: 109 us -> 0 us
  blocking collectives: 71.6 us -> 0 us
  other arithmetic: 39.9 us -> 5.42 us
  between operations: 16.1 us -> 2.31 us
    pallas_call x1 -> x3, Pallas kernels: 202 us -> 309 us  [the longest x1 283 us: forward_all(): pl.pallas_call(functools.partial(forward_kernel, n_own, n_both), out_shap...]
    ppermute x2 -> x0, waiting for transfers between devices: 74.6 us -> none  [the longest x1 74.6 us: stage_program(): far_second = lax.ppermute(half_second, 'data', swap)]
    psum x1 -> x0, blocking collectives: 71.6 us -> none  [stage_program(): total_norm = jnp.sqrt(lax.psum(jnp.sum(squares), ('data', 'stage')))]
    all_gather x2 -> x0, waiting for transfers between devices: 33.9 us -> none  [early(): lax.all_gather(new_w.astype(jnp.bfloat16), ('stage', 'data'), axis=0, til...]
    pallas_call x1, Pallas kernels: 119 us -> 137 us  [backward_all(): pl.pallas_call(backward_kernel, out_shape=(jax.ShapeDtypeStruct((half1, w...]
    sub x2 -> x0, other arithmetic: 17.4 us -> none  [adamw_update(): param_old - lr_value * (mom_hat / (jnp.sqrt(sec_hat) + ADAM_EPS) + WEIGHT...]
    concatenate x2 -> x0, other arithmetic: 15.6 us -> none  [whole(): jnp.concatenate([jnp.where(is_low, near, far), jnp.where(is_low, far, nea...]
    unnamed x13 -> x17, local copies, waits for them, and re-layouts: 27.1 us -> 30.2 us
  transfers between devices with their start and end apart: 4 -> 0, of which waited for: 2 -> 0; matrix products, arithmetic and copies ran while one was open for 5% -> 0% of each run, Pallas kernels for 0% -> 0%
where the time goes in v3:
time: 484 us; the launch traced here: 483 us
  Pallas kernels  445 us (92%)
  local copies, waits for them, and re-layouts  30.2 us (6%)
  other arithmetic  5.42 us (1%)
    pallas_call x1, Pallas kernels, forward_all(): pl.pallas_call(functools.partial(forward_kernel, n_own, n_both), out_shap...  283 us
    pallas_call x1, Pallas kernels, backward_all(): pl.pallas_call(backward_kernel, out_shape=(jax.ShapeDtypeStruct((half1, w...  137 us
    unnamed x17, local copies, waits for them, and re-layouts  30.2 us
    pallas_call x2, Pallas kernels, half_update(): pl.pallas_call(near_kernel if made is None else far_kernel, out_shape=tup...  25.5 us

profile of v3, /device:TPU:7, one launch (start us, length us, event | category | flops | bytes accessed | tf_op | source)
XLA Modules:
  0.0 483.0 jit_solution(71151400773338710)
XLA Ops:
  0.6 0.0 copy-start.7
  2.2 3.8 bitcast_convert_fusion.1.w1_ref
  6.1 0.0 copy-done.7
  6.1 1.6 bitcast_convert_fusion.w2_ref
  7.7 136.5 %backward_all.1 = (f32[256,2048]{1,0:T(8,128)}, f32[1024,512]{1,0:T(8,128)}, f32[8,128]{1,0:T(8,128)}) custom-call(f32[1]{0:T(128)S(6)} %copy.34.limit_ref, bf16[2048,512]{1,0:T(8,128)(2,1)} %bitcast.43, bf16[2048,512]{1,0:T(8,128)(2,1)} %dout_ref.1, bf16[512,2048]{1,0:T(8,128)(2,1)} %bitcast_convert_fusion.1.w1_ref, ...), custom_call_target="tpu_custom_call" | custom-call | flops 21474836480 | bytes 41943040 | tf_op jit(solution)/shard_map/backward_all/pallas_call | solution.py:510
  144.2 0.0 copy-start.2
  144.2 1.6 copy-done.2
  145.8 0.0 copy-start.3
  145.8 0.7 copy-done.3
  146.5 13.1 %near_update.1 = (f32[512,2048]{1,0:T(8,128)}, f32[512,2048]{1,0:T(8,128)}, f32[512,2048]{1,0:T(8,128)}, bf16[256,2048]{1,0:T(8,128)(2,1)S(1)}, f32[2048,512]{1,...) custom-call(s32[1]{0:T(128)} %bitcast.9.half_ref, f32[1]{0:T(128)S(6)} %copy.33.rate_ref, ...), custom_call_target="tpu_custom_call" | custom-call | flops 31457280 | bytes 31457280 | tf_op jit(solution)/shard_map/near_update/pallas_call | solution.py:317
  159.6 0.0 copy-start.5
  159.6 1.0 copy-done.5
  160.6 0.0 copy-start.6
  160.6 1.0 copy-done.6
  161.6 0.0 copy-start.4
  161.6 283.0 %forward_all.1 = (bf16[32768,512]{1,0:T(8,128)(2,1)}, f32[256,2048]{1,0:T(8,128)}, f32[1024,512]{1,0:T(8,128)}) custom-call(bf16[32768,512]{1,0:T(8,128)(2,1)} %bitcast.40, bf16[256,2048]{1,0:T(8,128)(2,1)} %copy-done.5, bf16[1024,512]{1,0:T(8,128)(2,1)} %copy-done.6, f32[256,2048]{1,0:T(8,128)} %get-tuple-element.28.refs_3_.g1_ref, ...), custom_call_target="tpu_custom_call" | custom-call | flops 154618822656 | bytes 67108864 | tf_op jit(solution)/shard_map/forward_all/pallas_call | solution.py:249
  444.5 0.0 copy-done.4
  444.6 0.0 copy-start
  444.6 1.6 copy-done
  446.1 0.0 copy-start.1
  446.1 1.6 copy-done.1
  447.7 12.4 %far_update.1 = (f32[512,2048]{1,0:T(8,128)}, f32[512,2048]{1,0:T(8,128)}, f32[512,2048]{1,0:T(8,128)}, f32[2048,512]{1,0:T(8,128)}, f32[2048,512]{1,0:T(8,128)}, /*index=5*/f32[2048,512]{1,0:T(8,128)}) custom-call(s32[1]{0:T(128)} %bitcast.half_ref, ...), custom_call_target="tpu_custom_call", output_to_operand_aliasing={{0}: (11, {}), {1}: (12, {}), {2}: (13, {}), {3}: (14, {}),... | custom-call | flops 31457280 | bytes 31457280 | tf_op jit(solution)/shard_map/far_update/pallas_call | solution.py:317
  460.1 22.9 %copy.35 = bf16[16,2048,512]{2,1,0:T(8,128)(2,1)} copy(bf16[16,2048,512]{2,1,0:T(8,128)(2,1)} %bitcast.25) | data formatting | bytes 67108864
Async XLA Ops:
  0.6 5.4 %copy-start.7 = (f32[1,2048,512]{2,1,0:T(8,128)S(1)}, f32[1,2048,512]{2,1,0:T(8,128)}, u32[]{:S(2)}) copy-start(f32[1,2048,512]{2,1,0:T(8,128)} %param.14) | copy-start | bytes 12582916
  144.2 1.6 copy-start.2
  145.8 0.7 copy-start.3
  159.6 1.0 copy-start.5
  160.6 1.0 copy-start.6
  161.6 283.0 %copy-start.4 = (f32[8,128]{1,0:T(8,128)S(1)}, f32[8,128]{1,0:T(8,128)}, u32[]{:S(2)}) copy-start(f32[8,128]{1,0:T(8,128)} %get-tuple-element.27.clip_ref) | copy-start | bytes 12292
  444.6 1.6 copy-start
  446.1 1.6 copy-start.1

commit v4 on v3

--- a/solution.py
+++ b/solution.py
@@ -16,20 +16,19 @@
 TRANS_DIMS = (((1,), (1,)), ((), ()))
 FIRST_DIMS = (((0,), (0,)), ((), ()))
 TILE = 512
-CHUNK = 512
+CHUNK = 1024
 SLOTS = 8
 LAG = 4
 PRE = 4
-SHARED = 4
+SHARED = 2
 UPDATE_STEPS = 8
 ROWS = 256
 PART = 512
-
-
-def fast_gelu(z):
-    inner = z * (0.7978845608028654 + 0.035677408136300125 * (z * z))
-    half = 0.5 * z
-    return half + half * jnp.tanh(inner)
+COLS = 512
+
+
+def gelu_of_half(half):
+    return half + half * jnp.tanh(half * (1.5957691216057308 + 0.28541926509040104 * (half * half)))
 
 
 def forward_kernel(n_own, n_both, x_ref, w1_ref, w2_ref, g1_ref, g2_ref, y_ref, far1_ref, far2_ref,
@@ -115,14 +114,23 @@
         for kind in (0, 1):
             arrive(owner, partner, kind)
 
-    def block_step(x_rows, block):
-        total = None
-        for first in range(0, width, CHUNK):
-            hidden = jnp.dot(x_rows, w1v[block, :, first:first + CHUNK], preferred_element_type=jnp.float32)
-            act_h = fast_gelu(hidden).astype(jnp.bfloat16)
-            piece = jnp.dot(act_h, w2v[block, first:first + CHUNK, :], preferred_element_type=jnp.float32)
-            total = piece if first == 0 else total + piece
-        return (x_rows.astype(jnp.float32) + total).astype(jnp.bfloat16)
+    def block_step(src, block, dst):
+        half = TILE // 2
+        pieces = [(side, first) for first in range(0, width, CHUNK) for side in (0, 1)]
+        x_rows = [src[side * half:(side + 1) * half, :] for side in (0, 1)]
+        total = [None, None]
+        act_h = {}
+        for turn in range(len(pieces) + 2):
+            if turn < len(pieces):
+                side, first = pieces[turn]
+                halved = jnp.dot(x_rows[side], w1v[block, :, first:first + CHUNK], preferred_element_type=jnp.float32)
+                act_h[turn] = gelu_of_half(halved).astype(jnp.bfloat16)
+            if turn >= 2:
+                side, first = pieces[turn - 2]
+                piece = jnp.dot(act_h.pop(turn - 2), w2v[block, first:first + CHUNK, :], preferred_element_type=jnp.float32)
+                total[side] = piece if first == 0 else total[side] + piece
+        for side in (0, 1):
+            dst[side * half:(side + 1) * half, :] = (x_rows[side].astype(jnp.float32) + total[side]).astype(jnp.bfloat16)
 
     @pl.when(early)
     def _():
@@ -132,7 +140,7 @@
 
             @pl.loop(0, 2)
             def _(block):
-                pv[tile] = block_step(pv[tile], block)
+                block_step(pv.at[tile], block, pv.at[tile])
 
     for kind in (0, 1):
         arrive(far, across, kind)
@@ -194,16 +202,9 @@
         def _(block):
             @pl.when((block >= 2) | (tile >= skip))
             def _():
-                result = block_step(xv[tile % 2], block)
-
-                @pl.when(block < n_blocks - 1)
-                def _():
-                    xv[tile % 2] = result
-
-                @pl.when(block == n_blocks - 1)
-                def _():
-                    yv[tile % SLOTS] = result
-
+                block_step(xv.at[tile % 2], block, xv.at[tile % 2])
+
+        yv[tile % SLOTS] = xv[tile % 2]
         store_own(tile).start()
         give_core(tile).start()
 
@@ -282,7 +283,7 @@
         news = adamw_rows(clip_ref[0:1, 0:1], rate_ref[0], param, moment, second, grad_val)
         for ref, new in zip(outs, news):
             ref[...] = new
-        outs[3][...] = news[0].astype(jnp.bfloat16)
+        outs[3][...] = ((0.5 if side == 0 else 1.0) * news[0]).astype(jnp.bfloat16)
 
 
 def far_kernel(half_ref, rate_ref, clip_ref, *refs):
@@ -381,8 +382,8 @@
 
     def prepare(idx):
         act = actv[chunk(idx), :]
-        for first in range(0, width, CHUNK):
-            cols = slice(first, first + CHUNK)
+        for first in range(0, width, COLS):
+            cols = slice(first, first + COLS)
             z = jnp.dot(act, w1v[:, cols], preferred_element_type=jnp.float32)
             sq = z * z
             th = jnp.tanh(z * (0.7978845608028654 + 0.035677408136300125 * sq))
@@ -393,8 +394,8 @@
     def descend(idx):
         grad_rows = grad[chunk(idx), :]
         total = None
-        for first in range(0, width, CHUNK):
-            cols = slice(first, first + CHUNK)
+        for first in range(0, width, COLS):
+            cols = slice(first, first + COLS)
             d_hid = lax.dot_general(grad_rows, w2v[cols, :], TRANS_DIMS, preferred_element_type=jnp.float32)
             d_pre = (slope[chunk(idx), cols] * d_hid).astype(jnp.bfloat16)
             dpre[chunk(idx), cols] = d_pre

time: 484 us -> 461 us (0.952); the launches traced: 483 us -> 454 us
  Pallas kernels: 445 us -> 416 us
    pallas_call x1, Pallas kernels: 283 us -> 254 us  [forward_all(): pl.pallas_call(functools.partial(forward_kernel, n_own, n_both), out_shap...]
where the time goes in v4:
time: 461 us; the launch traced here: 454 us
  Pallas kernels  416 us (90%)
  local copies, waits for them, and re-layouts  30.2 us (7%)
  other arithmetic  5.42 us (1%)
    pallas_call x1, Pallas kernels, forward_all(): pl.pallas_call(functools.partial(forward_kernel, n_own, n_both), out_shap...  254 us
    pallas_call x1, Pallas kernels, backward_all(): pl.pallas_call(backward_kernel, out_shape=(jax.ShapeDtypeStruct((half1, w...  137 us
    unnamed x17, local copies, waits for them, and re-layouts  30.2 us
    pallas_call x2, Pallas kernels, half_update(): pl.pallas_call(near_kernel if made is None else far_kernel, out_shape=tup...  25.6 us

profile of v4, /device:TPU:7, one launch (start us, length us, event | category | flops | bytes accessed | tf_op | source)
XLA Modules:
  0.0 454.2 jit_solution(14688055589451352396)
XLA Ops:
  0.6 0.0 copy-start.7
  2.2 3.8 bitcast_convert_fusion.1.w1_ref
  6.1 0.0 copy-done.7
  6.1 1.6 bitcast_convert_fusion.w2_ref
  7.7 136.5 %backward_all.1 = (f32[256,2048]{1,0:T(8,128)}, f32[1024,512]{1,0:T(8,128)}, f32[8,128]{1,0:T(8,128)}) custom-call(f32[1]{0:T(128)S(6)} %copy.34.limit_ref, bf16[2048,512]{1,0:T(8,128)(2,1)} %bitcast.43, bf16[2048,512]{1,0:T(8,128)(2,1)} %dout_ref.1, bf16[512,2048]{1,0:T(8,128)(2,1)} %bitcast_convert_fusion.1.w1_ref, ...), custom_call_target="tpu_custom_call" | custom-call | flops 21474836480 | bytes 41943040 | tf_op jit(solution)/shard_map/backward_all/pallas_call | solution.py:511
  144.2 0.0 copy-start.2
  144.2 1.6 copy-done.2
  145.8 0.0 copy-start.3
  145.8 0.7 copy-done.3
  146.5 13.1 %near_update.1 = (f32[512,2048]{1,0:T(8,128)}, f32[512,2048]{1,0:T(8,128)}, f32[512,2048]{1,0:T(8,128)}, bf16[256,2048]{1,0:T(8,128)(2,1)S(1)}, f32[2048,512]{1,...) custom-call(s32[1]{0:T(128)} %bitcast.9.half_ref, f32[1]{0:T(128)S(6)} %copy.33.rate_ref, ...), custom_call_target="tpu_custom_call" | custom-call | flops 31457280 | bytes 31457280 | tf_op jit(solution)/shard_map/near_update/pallas_call | solution.py:318
  159.6 0.0 copy-start.5
  159.7 1.0 copy-done.5
  160.6 0.0 copy-start.6
  160.6 1.0 copy-done.6
  161.6 0.0 copy-start.4
  161.6 254.1 %forward_all.1 = (bf16[32768,512]{1,0:T(8,128)(2,1)}, f32[256,2048]{1,0:T(8,128)}, f32[1024,512]{1,0:T(8,128)}) custom-call(bf16[32768,512]{1,0:T(8,128)(2,1)} %bitcast.40, bf16[256,2048]{1,0:T(8,128)(2,1)} %copy-done.5, bf16[1024,512]{1,0:T(8,128)(2,1)} %copy-done.6, f32[256,2048]{1,0:T(8,128)} %get-tuple-element.28.refs_3_.g1_ref, ...), custom_call_target="tpu_custom_call" | custom-call | flops 146028888064 | bytes 67108864 | tf_op jit(solution)/shard_map/forward_all/pallas_call | solution.py:250
  415.7 0.0 copy-done.4
  415.7 0.0 copy-start
  415.7 1.6 copy-done
  417.3 0.0 copy-start.1
  417.3 1.6 copy-done.1
  418.9 12.4 %far_update.1 = (f32[512,2048]{1,0:T(8,128)}, f32[512,2048]{1,0:T(8,128)}, f32[512,2048]{1,0:T(8,128)}, f32[2048,512]{1,0:T(8,128)}, f32[2048,512]{1,0:T(8,128)}, /*index=5*/f32[2048,512]{1,0:T(8,128)}) custom-call(s32[1]{0:T(128)} %bitcast.half_ref, ...), custom_call_target="tpu_custom_call", output_to_operand_aliasing={{0}: (11, {}), {1}: (12, {}), {2}: (13, {}), {3}: (14, {}),... | custom-call | flops 31457280 | bytes 31457280 | tf_op jit(solution)/shard_map/far_update/pallas_call | solution.py:318
  431.3 22.9 %copy.35 = bf16[16,2048,512]{2,1,0:T(8,128)(2,1)} copy(bf16[16,2048,512]{2,1,0:T(8,128)(2,1)} %bitcast.25) | data formatting | bytes 67108864
Async XLA Ops:
  0.6 5.4 %copy-start.7 = (f32[1,2048,512]{2,1,0:T(8,128)S(1)}, f32[1,2048,512]{2,1,0:T(8,128)}, u32[]{:S(2)}) copy-start(f32[1,2048,512]{2,1,0:T(8,128)} %param.14) | copy-start | bytes 12582916
  144.2 1.6 copy-start.2
  145.8 0.7 copy-start.3
  159.6 1.0 copy-start.5
  160.6 1.0 copy-start.6
  161.6 254.1 %copy-start.4 = (f32[8,128]{1,0:T(8,128)S(1)}, f32[8,128]{1,0:T(8,128)}, u32[]{:S(2)}) copy-start(f32[8,128]{1,0:T(8,128)} %get-tuple-element.27.clip_ref) | copy-start | bytes 12292
  415.7 1.6 copy-start
  417.3 1.6 copy-start.1

commit v5 on v4

--- a/solution.py
+++ b/solution.py
@@ -20,8 +20,10 @@
 SLOTS = 8
 LAG = 4
 PRE = 4
-SHARED = 2
+SHARED = 4
 UPDATE_STEPS = 8
+FINAL_STEPS = 16
+ADAM_ROWS = 32
 ROWS = 256
 PART = 512
 COLS = 512
@@ -31,7 +33,7 @@
     return half + half * jnp.tanh(half * (1.5957691216057308 + 0.28541926509040104 * (half * half)))
 
 
-def forward_kernel(n_own, n_both, x_ref, w1_ref, w2_ref, g1_ref, g2_ref, y_ref, far1_ref, far2_ref,
+def forward_kernel(n_own, n_both, x_ref, w1_ref, w2_ref, xw1_ref, xw2_ref, rw1_ref, rw2_ref, g1_ref, g2_ref, y_ref, far1_ref, far2_ref,
                    xv, pv, yv, w1v, w2v, xsem, psem, lsem, osem, csend, asend, rsend, crecv, arecv, rrecv, wsend, wrecv, fsend, frecv):
     stage = lax.axis_index('stage')
     rep = lax.axis_index('data')
@@ -71,9 +73,11 @@
     def arrive(owner, block, kind):
         move(owner, block, kind, to_core, 0).wait_recv()
 
-    own = [pltpu.make_async_copy(ref, part(rep, stage, kind), lsem.at[kind]) for kind, ref in enumerate((w1_ref, w2_ref))]
-    for copy in own:
-        copy.start()
+    fetched = {}
+    for lane, (where, kind, ref) in enumerate((('chip', 0, xw1_ref), ('rep', 1, rw2_ref), ('rep', 0, rw1_ref), ('chip', 1, xw2_ref), ('own', 0, w1_ref), ('own', 1, w2_ref))):
+        owner, block = {'own': (rep, stage), 'chip': (rep, across), 'rep': (far, stage)}[where]
+        fetched[where, kind] = pltpu.make_async_copy(ref, part(owner, block, kind), lsem.at[lane])
+        fetched[where, kind].start()
 
     @pl.when(early)
     def _():
@@ -96,20 +100,19 @@
         sends.append(copy)
         copy.start()
 
+    fetched['chip', 0].wait()
+    send(rep, across, 0, to_rep)
+    fetched['rep', 1].wait()
+    send(far, stage, 1, to_chip)
     for kind in (0, 1):
-        own[kind].wait()
-        for target in (to_chip, to_rep, to_core):
-            send(rep, stage, kind, target)
-    arrive(far, stage, 0)
-    send(far, stage, 0, to_core)
-    arrive(rep, across, 0)
-    send(rep, across, 0, to_rep)
-    send(rep, across, 0, to_core)
-    arrive(far, stage, 1)
-    send(far, stage, 1, to_chip)
-    send(far, stage, 1, to_core)
-    arrive(rep, across, 1)
-    send(rep, across, 1, to_core)
+        fetched['own', kind].wait()
+        send(rep, stage, kind, to_core)
+    fetched['rep', 0].wait()
+    for kind in (0, 1):
+        send(far, stage, kind, to_core)
+    fetched['chip', 1].wait()
+    for kind in (0, 1):
+        send(rep, across, kind, to_core)
     for owner in (rep, far):
         for kind in (0, 1):
             arrive(owner, partner, kind)
@@ -240,9 +243,9 @@
         copy.wait()
 
 
-def forward_all(x_rows, w_first, w_second, near_first, near_second, n_stage, n_both):
+def forward_all(x_rows, own, chip, twin, near_first, near_second, n_stage, n_both):
     n_rows, dim = x_rows.shape
-    width = w_first.shape[1]
+    width = own[0].shape[1]
     n_own = (n_rows // TILE - 2 * n_both) // 4
     n_tiles = n_own + n_both
     dma = pltpu.SemaphoreType.DMA
@@ -250,7 +253,7 @@
     return pl.pallas_call(
         functools.partial(forward_kernel, n_own, n_both),
         out_shape=(jax.ShapeDtypeStruct((n_rows, dim), jnp.bfloat16), jax.ShapeDtypeStruct(near_first.shape, jnp.float32), jax.ShapeDtypeStruct(near_second.shape, jnp.float32)),
-        in_specs=[pl.BlockSpec(memory_space=pl.ANY)] * 5,
+        in_specs=[pl.BlockSpec(memory_space=pl.ANY)] * 9,
         out_specs=(pl.BlockSpec(memory_space=pl.ANY),) * 3,
         scratch_shapes=[
             pltpu.VMEM((2, TILE, dim), jnp.bfloat16),
@@ -258,13 +261,13 @@
             pltpu.VMEM((SLOTS, TILE, dim), jnp.bfloat16),
             pltpu.VMEM((n_stage, dim, width), jnp.bfloat16),
             pltpu.VMEM((n_stage, width, dim), jnp.bfloat16),
-            dma((2,)), dma((PRE,)), dma((2,)), dma((SLOTS,)), dma((SLOTS,)), dma((SLOTS,)), dma((n_own,)),
-            dma((n_tiles,)), dma((n_own,)), dma((n_own,)), dma((14,)), dma((4 * n_stage,)), dma((2,)), dma((2,)),
+            dma((2,)), dma((PRE,)), dma((6,)), dma((SLOTS,)), dma((SLOTS,)), dma((SLOTS,)), dma((n_own,)),
+            dma((n_tiles,)), dma((n_own,)), dma((n_own,)), dma((10,)), dma((4 * n_stage,)), dma((2,)), dma((2,)),
         ],
         compiler_params=pltpu.CompilerParams(collective_id=0, has_side_effects=True, vmem_limit_bytes=56 * 2 ** 20),
         cost_estimate=pl.CostEstimate(flops=flops, bytes_accessed=2 * n_rows * dim * 2, transcendentals=0),
         name='forward_all',
-    )(x_rows, w_first, w_second, near_first, near_second)
+    )(x_rows, *own, *chip, *twin, near_first, near_second)
 
 
 def adamw_rows(coef, rate, param, moment, second, grad_val):
@@ -276,59 +279,53 @@
     return param - rate * (mom_hat / (jnp.sqrt(sec_hat) + ADAM_EPS) + WEIGHT_DECAY * param), mom_new, sec_new
 
 
-def near_kernel(half_ref, rate_ref, clip_ref, *refs):
-    for side in (0, 1):
-        param, moment, second, grad_val = (ref[...] for ref in refs[4 * side:4 * side + 4])
-        outs = refs[8 + 4 * side:12 + 4 * side]
-        news = adamw_rows(clip_ref[0:1, 0:1], rate_ref[0], param, moment, second, grad_val)
-        for ref, new in zip(outs, news):
-            ref[...] = new
-        outs[3][...] = ((0.5 if side == 0 else 1.0) * news[0]).astype(jnp.bfloat16)
-
-
-def far_kernel(half_ref, rate_ref, clip_ref, *refs):
+def update_kernel(n_ins, half_ref, rate_ref, clip_ref, *refs):
+    outs = refs[n_ins:]
     for side in (0, 1):
         param, moment, second, grad_val = (ref[...] for ref in refs[4 * side:4 * side + 4])
         news = adamw_rows(clip_ref[0:1, 0:1], rate_ref[0], param, moment, second, grad_val)
-        for ref, new in zip(refs[14 + 3 * side:17 + 3 * side], news):
+        for ref, new in zip(outs[3 * side:3 * side + 3], news):
             ref[...] = new
-
-
-def half_update(half_idx, rate, clip, first, second, grads, made):
-    steps = UPDATE_STEPS
-    f32, bf16 = jnp.float32, jnp.bfloat16
-    full, grad_specs, out_specs, out_shape = [], [], [], []
+    if len(outs) == 7:
+        outs[6][...] = refs[8][...]
+
+
+def half_update(half_idx, rate, clip, first, second, grads, made=(), rows=None):
+    steps = FINAL_STEPS if made else UPDATE_STEPS
+    full, out_specs, out_shape = [], [], []
     for arr, grad in zip((first[0], second[0]), grads):
         block = (grad.shape[0] // steps, grad.shape[1])
         picked = pl.BlockSpec(block, lambda step, half: (half[0] * steps + step, 0))
-        plain = pl.BlockSpec(block, lambda step, half: (step, 0))
-        full += [picked] * 3 + [plain]
+        full += [picked] * 3 + [pl.BlockSpec(block, lambda step, half: (step, 0))]
         out_specs += [picked] * 3
-        out_shape += [jax.ShapeDtypeStruct(arr.shape, f32)] * 3
-        if made is None:
-            out_specs.append(plain)
-            out_shape.append(jax.ShapeDtypeStruct(grad.shape, bf16))
+        out_shape += [jax.ShapeDtypeStruct(arr.shape, jnp.float32)] * 3
     in_specs = [pl.BlockSpec(memory_space=pltpu.SMEM), pl.BlockSpec(clip.shape, lambda step, half: (0, 0))] + full
     args = [half_idx, rate, clip, *first, grads[0], *second, grads[1]]
     aliases = {}
-    if made is not None:
+    if made:
+        spec = pl.BlockSpec((rows.shape[0] // steps, rows.shape[1]), lambda step, half: (step, 0))
+        in_specs.append(spec)
+        args.append(rows)
+        out_specs.append(spec)
+        out_shape.append(jax.ShapeDtypeStruct(rows.shape, rows.dtype))
         aliases = {len(args) + idx: idx for idx in range(6)}
         in_specs += [pl.BlockSpec(memory_space=pl.ANY)] * 6
         args += list(made)
     return pl.pallas_call(
-        near_kernel if made is None else far_kernel,
+        functools.partial(update_kernel, len(in_specs) - 2),
         out_shape=tuple(out_shape),
         grid_spec=pltpu.PrefetchScalarGridSpec(num_scalar_prefetch=1, grid=(steps,), in_specs=in_specs, out_specs=tuple(out_specs)),
         input_output_aliases=aliases,
-        compiler_params=pltpu.CompilerParams(vmem_limit_bytes=48 * 2 ** 20),
+        compiler_params=pltpu.CompilerParams(vmem_limit_bytes=62 * 2 ** 20),
         cost_estimate=pl.CostEstimate(flops=30 * 2 ** 20, bytes_accessed=30 * 2 ** 20, transcendentals=0),
-        name='near_update' if made is None else 'far_update',
+        name='far_update' if made else 'near_update',
     )(*args)
 
 
-def backward_kernel(limit_ref, act_ref, dout_ref, w1_ref, w2_ref, acc1_ref, acc2_ref, g1_ref, g2_ref, clip_ref,
+def backward_kernel(limit_ref, rate_ref, act_ref, dout_ref, w1_ref, w2_ref, m1_ref, m2_ref, v1_ref, v2_ref, acc1_ref, acc2_ref,
+                    g1_ref, g2_ref, clip_ref, b1_ref, b2_ref,
                     actv, grad, w1v, w2v, hid, slope, dpre, sent, accv, inbox,
-                    norms, lsem, asem, csend, crecv, rsend, rrecv, nsend, nrecv):
+                    norms, lsem, hsem, asem, csend, crecv, rsend, rrecv, nsend, nrecv):
     stage = lax.axis_index('stage')
     rep = lax.axis_index('data')
     far = 1 - rep
@@ -347,10 +344,11 @@
     def peer(**where):
         return dict(device_id=where, device_id_type=pl.DeviceIdType.MESH)
 
-    loads = [pltpu.make_async_copy(act_ref, actv, lsem.at[0]), pltpu.make_async_copy(w1_ref, w1v, lsem.at[1]), pltpu.make_async_copy(w2_ref, w2v, lsem.at[2])]
+    loads = [pltpu.make_async_copy(w1_ref, slope.at[2 * dim:3 * dim, :], lsem.at[0]), pltpu.make_async_copy(act_ref, actv, lsem.at[1])]
+    loads += [pltpu.make_async_copy(w2_ref.at[idx * dim:(idx + 1) * dim, :], slope.at[3 * dim:4 * dim, idx * dim:(idx + 1) * dim], lsem.at[2 + idx]) for idx in range(4)]
     for copy in loads:
         copy.start()
-    top = pltpu.make_async_copy(dout_ref, grad, lsem.at[3])
+    top = pltpu.make_async_copy(dout_ref, grad, lsem.at[6])
 
     @pl.when(stage == last)
     def _():
@@ -403,9 +401,23 @@
             total = part if first == 0 else total + part
         sent[chunk(idx), :] = (grad_rows.astype(jnp.float32) + total).astype(jnp.bfloat16)
 
-    for copy in loads:
+    loads[0].wait()
+
+    @pl.loop(0, dim // 64)
+    def _(idx):
+        span = pl.ds(pl.multiple_of(idx * 64, 64), 64)
+        w1v[span, :] = slope[pl.ds(pl.multiple_of(2 * dim + idx * 64, 64), 64), :].astype(jnp.bfloat16)
+
+    loads[1].wait()
+    prepare(0)
+    for copy in loads[2:]:
         copy.wait()
-    prepare(0)
+
+    @pl.loop(0, dim // 64)
+    def _(idx):
+        for group in range(4):
+            span = pl.ds(pl.multiple_of(group * dim + idx * 64, 64), 64)
+            w2v[span, :] = slope[pl.ds(pl.multiple_of(3 * dim + idx * 64, 64), 64), group * dim:(group + 1) * dim].astype(jnp.bfloat16)
 
     @pl.when(stage == last)
     def _():
@@ -426,6 +438,16 @@
         @pl.when(idx + 1 < n_chunks)
         def _():
             prepare(idx + 1)
+
+    near = []
+    for idx, ref in enumerate((w1_ref, m1_ref, v1_ref)):
+        near.append(pltpu.make_async_copy(ref.at[pl.ds(pl.multiple_of(rep * half1, half1), half1), :], slope.at[dim + idx * half1:dim + (idx + 1) * half1, :], hsem.at[len(near)]))
+    for idx, ref in enumerate((w2_ref, m2_ref, v2_ref)):
+        for group in range(4):
+            near.append(pltpu.make_async_copy(ref.at[pl.ds(pl.multiple_of(rep * half2 + group * half1, half1), half1), :],
+                                              slope.at[dim + (3 + idx) * half1:dim + (4 + idx) * half1, group * dim:(group + 1) * dim], hsem.at[len(near)]))
+    for copy in near:
+        copy.start()
 
     def weight_grad(idx, side):
         if idx < n_cols:
@@ -487,6 +509,25 @@
     total = jnp.sum(jnp.sum(total, axis=0, keepdims=True), axis=1, keepdims=True)
     clip = jnp.minimum(1.0, limit_ref[0] / (jnp.sqrt(total) + NORM_EPS))
     clip_ref[...] = jnp.broadcast_to(clip, clip_ref.shape)
+    for copy in near:
+        copy.wait()
+
+    @pl.loop(0, half1 // ADAM_ROWS)
+    def _(idx):
+        def from_slope(which, cols):
+            return slope[pl.ds(pl.multiple_of(dim + which * half1 + idx * ADAM_ROWS, ADAM_ROWS), ADAM_ROWS), cols]
+
+        coef = clip_ref[0:1, 0:1]
+        span = pl.ds(pl.multiple_of(idx * ADAM_ROWS, ADAM_ROWS), ADAM_ROWS)
+        every = slice(0, width)
+        new_w, _, _ = adamw_rows(coef, rate_ref[0], from_slope(0, every), from_slope(1, every), from_slope(2, every), g1_ref[span, :])
+        b1_ref[span, :] = (0.5 * new_w).astype(jnp.bfloat16)
+        for group in range(4):
+            cols = slice(group * dim, (group + 1) * dim)
+            span = pl.ds(pl.multiple_of(group * half1 + idx * ADAM_ROWS, ADAM_ROWS), ADAM_ROWS)
+            new_w, _, _ = adamw_rows(coef, rate_ref[0], from_slope(3, cols), from_slope(4, cols), from_slope(5, cols), g2_ref[span, :])
+            b2_ref[span, :] = new_w.astype(jnp.bfloat16)
+
     for idx in range(7):
         tell(idx).wait_send()
     for idx in range(n_parts):
@@ -499,9 +540,9 @@
             hop(idx).wait_send()
 
 
-def backward_all(limit, act, d_out, w_first, w_second, acc_first, acc_second):
+def backward_all(limit, rate, act, d_out, first, second, acc_first, acc_second):
     n_rows, dim = act.shape
-    width = w_first.shape[1]
+    width = first[0].shape[1]
     half1 = dim // 2
     n_chunks = n_rows // ROWS
     n_parts = 2 * (width // PART)
@@ -510,20 +551,21 @@
     vmem = pl.BlockSpec(memory_space=pltpu.VMEM)
     return pl.pallas_call(
         backward_kernel,
-        out_shape=(jax.ShapeDtypeStruct((half1, width), f32), jax.ShapeDtypeStruct((width // 2, dim), f32), jax.ShapeDtypeStruct((8, 128), f32)),
-        in_specs=[pl.BlockSpec(memory_space=pltpu.SMEM)] + [pl.BlockSpec(memory_space=pl.ANY)] * 6,
-        out_specs=(vmem, vmem, vmem),
+        out_shape=(jax.ShapeDtypeStruct((half1, width), f32), jax.ShapeDtypeStruct((width // 2, dim), f32), jax.ShapeDtypeStruct((8, 128), f32),
+                   jax.ShapeDtypeStruct((half1, width), bf16), jax.ShapeDtypeStruct((width // 2, dim), bf16)),
+        in_specs=[pl.BlockSpec(memory_space=pltpu.SMEM)] * 2 + [pl.BlockSpec(memory_space=pl.ANY)] * 10,
+        out_specs=(vmem,) * 5,
         scratch_shapes=[
             pltpu.VMEM((n_rows, dim), bf16), pltpu.VMEM((n_rows, dim), bf16),
             pltpu.VMEM((dim, width), bf16), pltpu.VMEM((width, dim), bf16),
             pltpu.VMEM((n_rows, width), bf16), pltpu.VMEM((n_rows, width), f32), pltpu.VMEM((n_rows, width), bf16),
             pltpu.VMEM((n_rows, dim), bf16), pltpu.VMEM((4, half1, PART), f32), pltpu.VMEM((n_parts, half1, PART), f32), pltpu.VMEM((8, 8, PART), f32),
-            dma((4,)), dma((4,)), dma((n_chunks,)), dma((n_chunks,)), dma((n_parts,)), dma((n_parts,)), dma((7,)), dma((8,)),
+            dma((7,)), dma((15,)), dma((4,)), dma((n_chunks,)), dma((n_chunks,)), dma((n_parts,)), dma((n_parts,)), dma((7,)), dma((8,)),
         ],
         compiler_params=pltpu.CompilerParams(collective_id=1, has_side_effects=True, vmem_limit_bytes=63 * 2 ** 20),
         cost_estimate=pl.CostEstimate(flops=10 * n_rows * dim * width, bytes_accessed=40 * 2 ** 20, transcendentals=0),
         name='backward_all',
-    )(limit, act, d_out, w_first, w_second, acc_first, acc_second)
+    )(limit, rate, act, d_out, first[0], second[0], first[1], second[1], first[2], second[2], acc_first, acc_second)
 
 
 def solution(mesh):
@@ -534,14 +576,17 @@
 
     def stage_program(w_in, w_out, mom_in, mom_out, var_in, var_out, acc_in, acc_out, stage_acts, d_out, next_x, learn_rate, max_norm):
         rep_idx = lax.axis_index('data')
-        near_first, near_second, clip = backward_all(
-            max_norm, stage_acts[0], d_out, w_in[0].astype(jnp.bfloat16), w_out[0].astype(jnp.bfloat16), acc_in[0, 0], acc_out[0, 0])
         first = (w_in[0], mom_in[0], var_in[0])
         second = (w_out[0], mom_out[0], var_out[0])
-        near = half_update(rep_idx.reshape(1), learn_rate, clip, first, second, (near_first, near_second), None)
+        near_first, near_second, clip, half_first, half_second = backward_all(
+            max_norm, learn_rate, stage_acts[0], d_out, first, second, acc_in[0, 0], acc_out[0, 0])
+        own = (half_first, half_second)
+        chip = tuple(lax.ppermute(arr, 'stage', [(src, (src + 2) % 4) for src in range(4)]) for arr in own)
+        twin = tuple(lax.ppermute(arr, 'data', [(0, 1), (1, 0)]) for arr in own)
+        near = half_update(rep_idx.reshape(1), learn_rate, clip, first, second, (near_first, near_second))
         n_micro, n_rows, dim = next_x.shape
-        next_y, far_first, far_second = forward_all(next_x.reshape(n_micro * n_rows, dim), near[3], near[7], near_first, near_second, n_stage, SHARED)
-        news = half_update((1 - rep_idx).reshape(1), learn_rate, clip, first, second, (far_first, far_second), near[:3] + near[4:7])
+        rows, far_first, far_second = forward_all(next_x.reshape(n_micro * n_rows, dim), own, chip, twin, near_first, near_second, n_stage, SHARED)
+        *news, next_y = half_update((1 - rep_idx).reshape(1), learn_rate, clip, first, second, (far_first, far_second), near, rows)
         return (news[0][None], news[3][None], news[1][None], news[4][None], news[2][None], news[5][None], next_y.reshape(next_x.shape))
 
     return jax.shard_map(stage_program, mesh=mesh, in_specs=(w_spec, w_spec, w_spec, w_spec, w_spec, w_spec, acc_spec, acc_spec, P('stage', 'data', None), P('data', None), row_spec, P(None), P(None)), out_specs=(w_spec, w_spec, w_spec, w_spec, w_spec, w_spec, row_spec), check_vma=False)

time: 461 us -> 444 us (0.963); the launches traced: 454 us -> 444 us
  waiting for transfers between devices: 0 us -> 30.7 us
  local copies, waits for them, and re-layouts: 30.2 us -> 0.01 us
  Pallas kernels: 416 us -> 408 us
  other arithmetic: 5.42 us -> 0 us
    pallas_call x1, Pallas kernels: 254 us -> 216 us  [forward_all(): pl.pallas_call(functools.partial(forward_kernel, n_own, n_both), out_shap...]
    ppermute x0 -> x4, waiting for transfers between devices: none -> 30.7 us  [the longest x2 30.7 us: stage_program(): twin = tuple((lax.ppermute(arr, 'data', [(0, 1), (1, 0)]) for arr in own))]
    unnamed x17 -> x2, local copies, waits for them, and re-layouts: 30.2 us -> 0.01 us
    pallas_call x2, Pallas kernels: 25.6 us -> 48.8 us  [half_update(): pl.pallas_call(functools.partial(update_kernel, len(in_specs) - 2), out_s...]
    pallas_call x1, Pallas kernels: 137 us -> 143 us  [backward_all(): pl.pallas_call(backward_kernel, out_shape=(jax.ShapeDtypeStruct((half1, w...]
    convert_element_type x2 -> x0, other arithmetic: 5.42 us -> none  [the longest x1 3.83 us: stage_program(): w_in[0].astype(jnp.bfloat16)]
  transfers between devices with their start and end apart: 0 -> 4, of which waited for: 0 -> 2; matrix products, arithmetic and copies ran while one was open for 0% -> 0% of each run, Pallas kernels for 0% -> 3%
where the time goes in v5:
time: 444 us
  Pallas kernels  408 us (92%)
  waiting for transfers between devices  30.7 us (7%)
    pallas_call x1, Pallas kernels, forward_all(): pl.pallas_call(functools.partial(forward_kernel, n_own, n_both), out_shap...  216 us
    pallas_call x1, Pallas kernels, backward_all(): pl.pallas_call(backward_kernel, out_shape=(jax.ShapeDtypeStruct((half1, w...  143 us
    pallas_call x2, Pallas kernels, half_update(): pl.pallas_call(functools.partial(update_kernel, len(in_specs) - 2), out_s...  48.8 us
    ppermute x2, waiting for transfers between devices, stage_program(): twin = tuple((lax.ppermute(arr, 'data', [(0, 1), (1, 0)]) for arr in own))  30.7 us
  transfers between devices with their start and end apart: 4, of which 2 were waited for; matrix products, arithmetic and copies ran while one was open for 0% of the time, Pallas kernels for 3%

profile of v5, /device:TPU:7, one launch (start us, length us, event | category | flops | bytes accessed | tf_op | source)
XLA Modules:
  0.0 443.7 jit_solution(17125939483562497506)
XLA Ops:
  1.9 143.4 %backward_all.1 = (f32[256,2048]{1,0:T(8,128)}, f32[1024,512]{1,0:T(8,128)}, f32[8,128]{1,0:T(8,128)}, bf16[256,2048]{1,0:T(8,128)(2,1)}, bf16[1024,512]{1,0:T(8,128)(2,1)}) custom-call(f32[1]{0:T(128)S(6)} %copy.33.limit_ref, f32[1]{0:T(128)S(6)} %copy.32.rate_ref, bf16[2048,512]{1,0:T(8,128)(2,1)} %bitcast.47, bf16[2048,512]{1,0:T(8,128)(2,1)} %dout_ref.1, ...), custom_call_target="tpu_custom_call" | custom-call | flops 21474836480 | bytes 41943040 | tf_op jit(solution)/shard_map/backward_all/pallas_call | solution.py:552
  145.3 0.3 collective-permute-start.2
  145.6 0.0 collective-permute-start
  145.6 1.2 collective-permute-start.3
  146.8 1.5 collective-permute-start.1
  148.3 13.3 %near_update.1 = (f32[512,2048]{1,0:T(8,128)}, f32[512,2048]{1,0:T(8,128)}, f32[512,2048]{1,0:T(8,128)}, f32[2048,512]{1,0:T(8,128)}, f32[2048,512]{1,0:T(8,128)}, /*index=5*/f32[2048,512]{1,0:T(8,128)}) custom-call(s32[1]{0:T(128)} %bitcast.11.half_ref, f32[1]{0:T(128)S(6)} %copy.32.rate_ref, f32[8,128]{1,0:T(8,128)} %get-tuple-element.28.clip_ref, ...), custom_call_target="tpu_custom_call" | custom-call | flops 31457280 | bytes 31457280 | tf_op jit(solution)/shard_map/near_update/pallas_call | solution.py:314
  161.6 8.2 %collective-permute-done.2.rw1_ref = bf16[256,2048]{1,0:T(8,128)(2,1)S(1)} collective-permute-done((bf16[256,2048]{1,0:T(8,128)(2,1)}, bf16[256,2048]{1,0:T(8,128)(2,1)S(1)}, u32[]{:S(2)}, u32[]{:S(2)}) %collective-permute-start.2) | collective-permute-done | bytes 1048608 | tf_op jit(solution)/shard_map/ppermute | solution.py:585
  169.8 0.0 copy-start
  169.8 0.0 collective-permute-done.xw1_ref
  169.8 22.5 %collective-permute-done.3.rw2_ref = bf16[1024,512]{1,0:T(8,128)(2,1)} collective-permute-done((bf16[1024,512]{1,0:T(8,128)(2,1)}, bf16[1024,512]{1,0:T(8,128)(2,1)}, u32[]{:S(2)}, u32[]{:S(2)}) %collective-permute-start.3) | collective-permute-done | bytes 1048608 | tf_op jit(solution)/shard_map/ppermute | solution.py:585
  192.3 0.0 collective-permute-done.1.xw2_ref
  192.3 0.0 copy-done
  192.3 215.7 %forward_all.1 = (bf16[32768,512]{1,0:T(8,128)(2,1)}, f32[256,2048]{1,0:T(8,128)}, f32[1024,512]{1,0:T(8,128)}) custom-call(bf16[32768,512]{1,0:T(8,128)(2,1)} %bitcast.43, bf16[256,2048]{1,0:T(8,128)(2,1)} %get-tuple-element.29.w1_ref, bf16[1024,512]{1,0:T(8,128)(2,1)} %get-tuple-element.30.w2_ref, bf16[256,2048]{1,0:T(8,128)(2,1)} %collective-permute-done.xw1_ref, ...), custom_call_target="tpu_custom_call" | custom-call | flops 154618822656 | bytes 67108864 | tf_op jit(solution)/shard_map/forward_all/pallas_call | solution.py:253
  408.0 35.6 %far_update.1 = (f32[512,2048]{1,0:T(8,128)}, f32[512,2048]{1,0:T(8,128)}, f32[512,2048]{1,0:T(8,128)}, f32[2048,512]{1,0:T(8,128)}, f32[2048,512]{1,0:T(8,128)}...) custom-call(s32[1]{0:T(128)} %bitcast.half_ref, ...), custom_call_target="tpu_custom_call", output_to_operand_aliasing={{0}: (12, {}), {1}: (13, {}), {2}: (14, {}), {3}: (15, {}),... | custom-call | flops 31457280 | bytes 31457280 | tf_op jit(solution)/shard_map/far_update/pallas_call | solution.py:314
Async XLA Ops:
  145.3 24.5 %collective-permute-start.2 = (bf16[256,2048]{1,0:T(8,128)(2,1)}, bf16[256,2048]{1,0:T(8,128)(2,1)S(1)}, u32[]{:S(2)}, u32[]{:S(2)}) collective-permute-start(bf16[256,2048]{1,0:T(8,128)(2,1)} %get-tuple-element.29.w1_ref), channel_id=1, source_target_pairs={{0,4},{4,0},{1,5},{5,1},{2,6},{6,2},{3,7},{7,3}} | collective-permute-start | bytes 3145736 | tf_op jit(solution)/shard_map/ppermute | solution.py:585
  145.6 24.2 %collective-permute-start = (bf16[256,2048]{1,0:T(8,128)(2,1)}, bf16[256,2048]{1,0:T(8,128)(2,1)}, u32[]{:S(2)}, u32[]{:S(2)}) collective-permute-start(bf16[256,2048]{1,0:T(8,128)(2,1)} %get-tuple-element.29.w1_ref), channel_id=1, source_target_pairs={{0,2},{1,3},{2,0},{3,1},{4,6},{5,7},{6,4},{7,5}} | collective-permute-start | bytes 3145736 | tf_op jit(solution)/shard_map/ppermute | solution.py:584
  145.6 46.6 %collective-permute-start.3 = (bf16[1024,512]{1,0:T(8,128)(2,1)}, bf16[1024,512]{1,0:T(8,128)(2,1)}, u32[]{:S(2)}, u32[]{:S(2)}) collective-permute-start(bf16[1024,512]{1,0:T(8,128)(2,1)} %get-tuple-element.30.w2_ref), channel_id=1, source_target_pairs={{0,4},{4,0},{1,5},{5,1},{2,6},{6,2},{3,7},{7,3}} | collective-permute-start | bytes 3145736 | tf_op jit(solution)/shard_map/ppermute | solution.py:585
  146.8 45.4 %collective-permute-start.1 = (bf16[1024,512]{1,0:T(8,128)(2,1)}, bf16[1024,512]{1,0:T(8,128)(2,1)}, u32[]{:S(2)}, u32[]{:S(2)}) collective-permute-start(bf16[1024,512]{1,0:T(8,128)(2,1)} %get-tuple-element.30.w2_ref), channel_id=1, source_target_pairs={{0,2},{1,3},{2,0},{3,1},{4,6},{5,7},{6,4},{7,5}} | collective-permute-start | bytes 3145736 | tf_op jit(solution)/shard_map/ppermute | solution.py:584
  169.8 22.5 %copy-start = (bf16[256,2048]{1,0:T(8,128)(2,1)}, bf16[256,2048]{1,0:T(8,128)(2,1)S(1)}, u32[]{:S(2)}) copy-start(bf16[256,2048]{1,0:T(8,128)(2,1)S(1)} %collective-permute-done.2.rw1_ref) | copy-start | bytes 3145732

commit v6 on v5

--- a/solution.py
+++ b/solution.py
@@ -17,7 +17,7 @@
 FIRST_DIMS = (((0,), (0,)), ((), ()))
 TILE = 512
 CHUNK = 1024
-SLOTS = 8
+FORWARD_VMEM = 30
 LAG = 4
 PRE = 4
 SHARED = 4
@@ -34,7 +34,7 @@
 
 
 def forward_kernel(n_own, n_both, x_ref, w1_ref, w2_ref, xw1_ref, xw2_ref, rw1_ref, rw2_ref, g1_ref, g2_ref, y_ref, far1_ref, far2_ref,
-                   xv, pv, yv, w1v, w2v, xsem, psem, lsem, osem, csend, asend, rsend, crecv, arecv, rrecv, wsend, wrecv, fsend, frecv):
+                   xv, pv, w1v, w2v, xsem, psem, lsem, csend, asend, rsend, crecv, arecv, rrecv, wsend, wrecv, fsend, frecv):
     stage = lax.axis_index('stage')
     rep = lax.axis_index('data')
     far = 1 - rep
@@ -155,14 +155,15 @@
         for kind in (0, 1):
             arrive(owner, corner, kind)
 
-    def store_own(tile):
-        return pltpu.make_async_copy(yv.at[tile % SLOTS], y_ref.at[rows(stage, tile)], osem.at[tile % SLOTS])
+    def give(tile, send, recv, target):
+        ref = y_ref.at[rows(stage, tile)]
+        return remote(ref, ref, send.at[tile], recv.at[tile], target)
 
     def give_core(tile):
-        return remote(yv.at[tile % SLOTS], y_ref.at[rows(stage, tile)], csend.at[tile % SLOTS], crecv.at[tile], to_core)
+        return give(tile, csend, crecv, to_core)
 
     def give_chip(tile):
-        return remote(yv.at[tile % SLOTS], y_ref.at[rows(stage, tile)], asend.at[tile % SLOTS], arecv.at[tile], to_chip)
+        return give(tile, asend, arecv, to_chip)
 
     def pass_on(tile):
         ref = y_ref.at[rows(across, tile)]
@@ -173,14 +174,6 @@
         remote(ref, ref, asend.at[0], arecv.at[tile], to_chip).wait_recv()
         pass_on(tile).start()
 
-    def free_slot(tile):
-        store_own(tile).wait()
-        give_core(tile).wait_send()
-
-        @pl.when(tile < n_own)
-        def _():
-            give_chip(tile).wait_send()
-
     @pl.loop(0, n_tiles)
     def _(tile):
         skip = jnp.where(early, PRE, 0)
@@ -196,10 +189,6 @@
         @pl.when((tile + 1 >= skip) & (tile + 1 < n_tiles))
         def _():
             load_x(tile + 1).start()
-
-        @pl.when(tile >= SLOTS)
-        def _():
-            free_slot(tile - SLOTS)
 
         @pl.loop(0, n_blocks)
         def _(block):
@@ -207,8 +196,7 @@
             def _():
                 block_step(xv.at[tile % 2], block, xv.at[tile % 2])
 
-        yv[tile % SLOTS] = xv[tile % 2]
-        store_own(tile).start()
+        y_ref[rows(stage, tile), :] = xv[tile % 2]
         give_core(tile).start()
 
         @pl.when(tile < n_own)
@@ -221,21 +209,19 @@
 
     for tile in range(max(n_tiles - LAG, 0), n_own):
         relay(tile)
-
-    @pl.loop(n_tiles - SLOTS, n_tiles)
-    def _(tile):
-        free_slot(tile)
 
     @pl.loop(0, n_tiles)
     def _(tile):
         ref = y_ref.at[rows(partner, tile)]
         remote(ref, ref, csend.at[0], crecv.at[tile], to_core).wait_recv()
+        give_core(tile).wait_send()
 
     @pl.loop(0, n_own)
     def _(tile):
         ref = y_ref.at[rows(corner, tile)]
         remote(ref, ref, rsend.at[0], rrecv.at[tile], to_core).wait_recv()
         pass_on(tile).wait_send()
+        give_chip(tile).wait_send()
 
     for copy in sends:
         copy.wait_send()
@@ -252,19 +238,18 @@
     flops = 4 * n_tiles * TILE * dim * width * n_stage
     return pl.pallas_call(
         functools.partial(forward_kernel, n_own, n_both),
-        out_shape=(jax.ShapeDtypeStruct((n_rows, dim), jnp.bfloat16), jax.ShapeDtypeStruct(near_first.shape, jnp.float32), jax.ShapeDtypeStruct(near_second.shape, jnp.float32)),
+        out_shape=(pltpu.VMEM((n_rows, dim), jnp.bfloat16), jax.ShapeDtypeStruct(near_first.shape, jnp.float32), jax.ShapeDtypeStruct(near_second.shape, jnp.float32)),
         in_specs=[pl.BlockSpec(memory_space=pl.ANY)] * 9,
-        out_specs=(pl.BlockSpec(memory_space=pl.ANY),) * 3,
+        out_specs=(pl.BlockSpec(memory_space=pltpu.VMEM),) + (pl.BlockSpec(memory_space=pl.ANY),) * 2,
         scratch_shapes=[
             pltpu.VMEM((2, TILE, dim), jnp.bfloat16),
             pltpu.VMEM((PRE, TILE, dim), jnp.bfloat16),
-            pltpu.VMEM((SLOTS, TILE, dim), jnp.bfloat16),
             pltpu.VMEM((n_stage, dim, width), jnp.bfloat16),
             pltpu.VMEM((n_stage, width, dim), jnp.bfloat16),
-            dma((2,)), dma((PRE,)), dma((6,)), dma((SLOTS,)), dma((SLOTS,)), dma((SLOTS,)), dma((n_own,)),
+            dma((2,)), dma((PRE,)), dma((6,)), dma((n_tiles,)), dma((n_own,)), dma((n_own,)),
             dma((n_tiles,)), dma((n_own,)), dma((n_own,)), dma((10,)), dma((4 * n_stage,)), dma((2,)), dma((2,)),
         ],
-        compiler_params=pltpu.CompilerParams(collective_id=0, has_side_effects=True, vmem_limit_bytes=56 * 2 ** 20),
+        compiler_params=pltpu.CompilerParams(collective_id=0, has_side_effects=True, vmem_limit_bytes=FORWARD_VMEM * 2 ** 20),
         cost_estimate=pl.CostEstimate(flops=flops, bytes_accessed=2 * n_rows * dim * 2, transcendentals=0),
         name='forward_all',
     )(x_rows, *own, *chip, *twin, near_first, near_second)
@@ -281,13 +266,26 @@
 
 def update_kernel(n_ins, half_ref, rate_ref, clip_ref, *refs):
     outs = refs[n_ins:]
+    if len(outs) == 8:
+        step, steps = pl.program_id(0), pl.num_programs(0)
+
+        def drain(idx):
+            size = outs[6].shape[0] // FINAL_STEPS
+            span = pl.ds(pl.multiple_of(idx * size, size), size)
+            return pltpu.make_async_copy(refs[8].at[span], outs[6].at[span], outs[7].at[idx])
+
+        drain(step).start()
+
     for side in (0, 1):
         param, moment, second, grad_val = (ref[...] for ref in refs[4 * side:4 * side + 4])
         news = adamw_rows(clip_ref[0:1, 0:1], rate_ref[0], param, moment, second, grad_val)
         for ref, new in zip(outs[3 * side:3 * side + 3], news):
             ref[...] = new
-    if len(outs) == 7:
-        outs[6][...] = refs[8][...]
+    if len(outs) == 8:
+        @pl.when(step == steps - 1)
+        def _():
+            for idx in range(FINAL_STEPS):
+                drain(idx).wait()
 
 
 def half_update(half_idx, rate, clip, first, second, grads, made=(), rows=None):
@@ -303,10 +301,9 @@
     args = [half_idx, rate, clip, *first, grads[0], *second, grads[1]]
     aliases = {}
     if made:
-        spec = pl.BlockSpec((rows.shape[0] // steps, rows.shape[1]), lambda step, half: (step, 0))
-        in_specs.append(spec)
-        args.append(rows)
-        out_specs.append(spec)
+        in_specs.append(pl.BlockSpec(memory_space=pl.ANY))
+        args.append(pltpu.with_memory_space_constraint(rows, pltpu.VMEM))
+        out_specs.append(pl.BlockSpec(memory_space=pl.ANY))
         out_shape.append(jax.ShapeDtypeStruct(rows.shape, rows.dtype))
         aliases = {len(args) + idx: idx for idx in range(6)}
         in_specs += [pl.BlockSpec(memory_space=pl.ANY)] * 6
@@ -314,9 +311,10 @@
     return pl.pallas_call(
         functools.partial(update_kernel, len(in_specs) - 2),
         out_shape=tuple(out_shape),
-        grid_spec=pltpu.PrefetchScalarGridSpec(num_scalar_prefetch=1, grid=(steps,), in_specs=in_specs, out_specs=tuple(out_specs)),
+        grid_spec=pltpu.PrefetchScalarGridSpec(num_scalar_prefetch=1, grid=(steps,), in_specs=in_specs, out_specs=tuple(out_specs),
+                                              scratch_shapes=[pltpu.SemaphoreType.DMA((FINAL_STEPS,))] if made else []),
         input_output_aliases=aliases,
-        compiler_params=pltpu.CompilerParams(vmem_limit_bytes=62 * 2 ** 20),
+        compiler_params=pltpu.CompilerParams(vmem_limit_bytes=(28 if made else 62) * 2 ** 20),
         cost_estimate=pl.CostEstimate(flops=30 * 2 ** 20, bytes_accessed=30 * 2 ** 20, transcendentals=0),
         name='far_update' if made else 'near_update',
     )(*args)

time: 444 us -> 431 us (0.971)
  Pallas kernels: 408 us -> 395 us
    pallas_call x2, Pallas kernels: 48.8 us -> 35.7 us  [half_update(): pl.pallas_call(functools.partial(update_kernel, len(in_specs) - 2), out_s...]
where the time goes in v6:
time: 431 us
  Pallas kernels  395 us (92%)
  waiting for transfers between devices  30.6 us (7%)
    pallas_call x1, Pallas kernels, forward_all(): pl.pallas_call(functools.partial(forward_kernel, n_own, n_both), out_shap...  216 us
    pallas_call x1, Pallas kernels, backward_all(): pl.pallas_call(backward_kernel, out_shape=(jax.ShapeDtypeStruct((half1, w...  143 us
    pallas_call x2, Pallas kernels, half_update(): pl.pallas_call(functools.partial(update_kernel, len(in_specs) - 2), out_s...  35.7 us
    ppermute x2, waiting for transfers between devices, stage_program(): twin = tuple((lax.ppermute(arr, 'data', [(0, 1), (1, 0)]) for arr in own))  30.6 us
  transfers between devices with their start and end apart: 4, of which 2 were waited for; matrix products, arithmetic and copies ran while one was open for 0% of the time, Pallas kernels for 3%

profile of v6, /device:TPU:7, one launch (start us, length us, event | category | flops | bytes accessed | tf_op | source)
XLA Modules:
  0.0 430.5 jit_solution(3884146453333245138)
XLA Ops:
  1.9 143.4 %backward_all.1 = (f32[256,2048]{1,0:T(8,128)}, f32[1024,512]{1,0:T(8,128)}, f32[8,128]{1,0:T(8,128)}, bf16[256,2048]{1,0:T(8,128)(2,1)}, bf16[1024,512]{1,0:T(8,128)(2,1)}) custom-call(f32[1]{0:T(128)S(6)} %copy.33.limit_ref, f32[1]{0:T(128)S(6)} %copy.32.rate_ref, bf16[2048,512]{1,0:T(8,128)(2,1)} %bitcast.47, bf16[2048,512]{1,0:T(8,128)(2,1)} %dout_ref.1, ...), custom_call_target="tpu_custom_call" | custom-call | flops 21474836480 | bytes 41943040 | tf_op jit(solution)/shard_map/backward_all/pallas_call | solution.py:550
  145.3 0.3 collective-permute-start.2
  145.6 0.0 collective-permute-start
  145.6 1.2 collective-permute-start.3
  146.8 1.5 collective-permute-start.1
  148.2 13.3 %near_update.1 = (f32[512,2048]{1,0:T(8,128)}, f32[512,2048]{1,0:T(8,128)}, f32[512,2048]{1,0:T(8,128)}, f32[2048,512]{1,0:T(8,128)}, f32[2048,512]{1,0:T(8,128)}, /*index=5*/f32[2048,512]{1,0:T(8,128)}) custom-call(s32[1]{0:T(128)} %bitcast.11.half_ref, f32[1]{0:T(128)S(6)} %copy.32.rate_ref, f32[8,128]{1,0:T(8,128)} %get-tuple-element.28.clip_ref, ...), custom_call_target="tpu_custom_call" | custom-call | flops 31457280 | bytes 31457280 | tf_op jit(solution)/shard_map/near_update/pallas_call | solution.py:311
  161.6 8.2 %collective-permute-done.2.rw1_ref = bf16[256,2048]{1,0:T(8,128)(2,1)S(1)} collective-permute-done((bf16[256,2048]{1,0:T(8,128)(2,1)}, bf16[256,2048]{1,0:T(8,128)(2,1)S(1)}, u32[]{:S(2)}, u32[]{:S(2)}) %collective-permute-start.2) | collective-permute-done | bytes 1048608 | tf_op jit(solution)/shard_map/ppermute | solution.py:583
  169.7 0.0 copy-start
  169.7 0.0 collective-permute-done.xw1_ref
  169.7 22.5 %collective-permute-done.3.rw2_ref = bf16[1024,512]{1,0:T(8,128)(2,1)} collective-permute-done((bf16[1024,512]{1,0:T(8,128)(2,1)}, bf16[1024,512]{1,0:T(8,128)(2,1)}, u32[]{:S(2)}, u32[]{:S(2)}) %collective-permute-start.3) | collective-permute-done | bytes 1048608 | tf_op jit(solution)/shard_map/ppermute | solution.py:583
  192.2 0.0 collective-permute-done.1.xw2_ref
  192.2 0.0 copy-done
  192.2 215.7 %forward_all.1 = (bf16[32768,512]{1,0:T(8,128)(2,1)S(1)}, f32[256,2048]{1,0:T(8,128)}, f32[1024,512]{1,0:T(8,128)}) custom-call(bf16[32768,512]{1,0:T(8,128)(2,1)} %bitcast.43, bf16[256,2048]{1,0:T(8,128)(2,1)} %get-tuple-element.29.w1_ref, bf16[1024,512]{1,0:T(8,128)(2,1)} %get-tuple-element.30.w2_ref, bf16[256,2048]{1,0:T(8,128)(2,1)} %collective-permute-done.xw1_ref, ...), custom_call_target="tpu_custom_call" | custom-call | flops 154618822656 | bytes 67108864 | tf_op jit(solution)/shard_map/forward_all/pallas_call | solution.py:239
  408.0 22.4 %far_update.1 = (f32[512,2048]{1,0:T(8,128)}, f32[512,2048]{1,0:T(8,128)}, f32[512,2048]{1,0:T(8,128)}, f32[2048,512]{1,0:T(8,128)}, f32[2048,512]{1,0:T(8,128)}...) custom-call(s32[1]{0:T(128)} %bitcast.half_ref, ...), custom_call_target="tpu_custom_call", output_to_operand_aliasing={{0}: (12, {}), {1}: (13, {}), {2}: (14, {}), {3}: (15, {}),... | custom-call | flops 31457280 | bytes 31457280 | tf_op jit(solution)/shard_map/far_update/pallas_call | solution.py:311
Async XLA Ops:
  145.3 24.5 %collective-permute-start.2 = (bf16[256,2048]{1,0:T(8,128)(2,1)}, bf16[256,2048]{1,0:T(8,128)(2,1)S(1)}, u32[]{:S(2)}, u32[]{:S(2)}) collective-permute-start(bf16[256,2048]{1,0:T(8,128)(2,1)} %get-tuple-element.29.w1_ref), channel_id=1, source_target_pairs={{0,4},{4,0},{1,5},{5,1},{2,6},{6,2},{3,7},{7,3}} | collective-permute-start | bytes 3145736 | tf_op jit(solution)/shard_map/ppermute | solution.py:583
  145.6 24.2 %collective-permute-start = (bf16[256,2048]{1,0:T(8,128)(2,1)}, bf16[256,2048]{1,0:T(8,128)(2,1)}, u32[]{:S(2)}, u32[]{:S(2)}) collective-permute-start(bf16[256,2048]{1,0:T(8,128)(2,1)} %get-tuple-element.29.w1_ref), channel_id=1, source_target_pairs={{0,2},{1,3},{2,0},{3,1},{4,6},{5,7},{6,4},{7,5}} | collective-permute-start | bytes 3145736 | tf_op jit(solution)/shard_map/ppermute | solution.py:582
  145.6 46.6 %collective-permute-start.3 = (bf16[1024,512]{1,0:T(8,128)(2,1)}, bf16[1024,512]{1,0:T(8,128)(2,1)}, u32[]{:S(2)}, u32[]{:S(2)}) collective-permute-start(bf16[1024,512]{1,0:T(8,128)(2,1)} %get-tuple-element.30.w2_ref), channel_id=1, source_target_pairs={{0,4},{4,0},{1,5},{5,1},{2,6},{6,2},{3,7},{7,3}} | collective-permute-start | bytes 3145736 | tf_op jit(solution)/shard_map/ppermute | solution.py:583
  146.8 45.4 %collective-permute-start.1 = (bf16[1024,512]{1,0:T(8,128)(2,1)}, bf16[1024,512]{1,0:T(8,128)(2,1)}, u32[]{:S(2)}, u32[]{:S(2)}) collective-permute-start(bf16[1024,512]{1,0:T(8,128)(2,1)} %get-tuple-element.30.w2_ref), channel_id=1, source_target_pairs={{0,2},{1,3},{2,0},{3,1},{4,6},{5,7},{6,4},{7,5}} | collective-permute-start | bytes 3145736 | tf_op jit(solution)/shard_map/ppermute | solution.py:582
  169.7 22.5 %copy-start = (bf16[256,2048]{1,0:T(8,128)(2,1)}, bf16[256,2048]{1,0:T(8,128)(2,1)S(1)}, u32[]{:S(2)}) copy-start(bf16[256,2048]{1,0:T(8,128)(2,1)S(1)} %collective-permute-done.2.rw1_ref) | copy-start | bytes 3145732

commit v7 on v6

--- a/solution.py
+++ b/solution.py
@@ -16,11 +16,13 @@
 TRANS_DIMS = (((1,), (1,)), ((), ()))
 FIRST_DIMS = (((0,), (0,)), ((), ()))
 TILE = 512
-CHUNK = 1024
+CHUNK = 512
+BEHIND = 3
 FORWARD_VMEM = 30
 LAG = 4
 PRE = 4
-SHARED = 4
+SHARED = 3
+OWN_TILES = (15, 15, 14, 14)
 UPDATE_STEPS = 8
 FINAL_STEPS = 16
 ADAM_ROWS = 32
@@ -33,7 +35,7 @@
     return half + half * jnp.tanh(half * (1.5957691216057308 + 0.28541926509040104 * (half * half)))
 
 
-def forward_kernel(n_own, n_both, x_ref, w1_ref, w2_ref, xw1_ref, xw2_ref, rw1_ref, rw2_ref, g1_ref, g2_ref, y_ref, far1_ref, far2_ref,
+def forward_kernel(n_low, n_high, n_both, x_ref, w1_ref, w2_ref, xw1_ref, xw2_ref, rw1_ref, rw2_ref, g1_ref, g2_ref, y_ref, far1_ref, far2_ref,
                    xv, pv, w1v, w2v, xsem, psem, lsem, csend, asend, rsend, crecv, arecv, rrecv, wsend, wrecv, fsend, frecv):
     stage = lax.axis_index('stage')
     rep = lax.axis_index('data')
@@ -43,13 +45,16 @@
     across = (stage + 2) % 4
     corner = (partner + 2) % 4
     early = stage < 2
-    n_tiles = n_own + n_both
+    mine, theirs = jnp.where(early, n_low, n_high), jnp.where(early, n_high, n_low)
+    n_tiles = mine + n_both
     n_blocks, dim, width = w1v.shape
     half1, half2 = dim // 2, width // 2
     to_core, to_chip, to_rep = {'stage': partner}, {'stage': across}, {'data': far}
 
     def rows(owner, tile):
-        place = jnp.where(tile < n_own, owner * n_own + tile, 4 * n_own + (owner % 2) * n_both + tile - n_own)
+        count = jnp.where(owner < 2, n_low, n_high)
+        base = jnp.where(owner < 2, owner * n_low, 2 * n_low + (owner - 2) * n_high)
+        place = jnp.where(tile < count, base + tile, 2 * (n_low + n_high) + (owner % 2) * n_both + tile - count)
         return pl.ds(pl.multiple_of(place * TILE, TILE), TILE)
 
     def remote(src, dst, send, recv, target):
@@ -123,14 +128,14 @@
         x_rows = [src[side * half:(side + 1) * half, :] for side in (0, 1)]
         total = [None, None]
         act_h = {}
-        for turn in range(len(pieces) + 2):
+        for turn in range(len(pieces) + BEHIND):
             if turn < len(pieces):
                 side, first = pieces[turn]
                 halved = jnp.dot(x_rows[side], w1v[block, :, first:first + CHUNK], preferred_element_type=jnp.float32)
                 act_h[turn] = gelu_of_half(halved).astype(jnp.bfloat16)
-            if turn >= 2:
-                side, first = pieces[turn - 2]
-                piece = jnp.dot(act_h.pop(turn - 2), w2v[block, first:first + CHUNK, :], preferred_element_type=jnp.float32)
+            if turn >= BEHIND:
+                side, first = pieces[turn - BEHIND]
+                piece = jnp.dot(act_h.pop(turn - BEHIND), w2v[block, first:first + CHUNK, :], preferred_element_type=jnp.float32)
                 total[side] = piece if first == 0 else total[side] + piece
         for side in (0, 1):
             dst[side * half:(side + 1) * half, :] = (x_rows[side].astype(jnp.float32) + total[side]).astype(jnp.bfloat16)
@@ -199,15 +204,16 @@
         y_ref[rows(stage, tile), :] = xv[tile % 2]
         give_core(tile).start()
 
-        @pl.when(tile < n_own)
+        @pl.when(tile < mine)
         def _():
             give_chip(tile).start()
 
-        @pl.when((tile >= LAG) & (tile < LAG + n_own))
+        @pl.when((tile >= LAG) & (tile < LAG + theirs))
         def _():
             relay(tile - LAG)
 
-    for tile in range(max(n_tiles - LAG, 0), n_own):
+    @pl.loop(n_tiles - LAG, theirs)
+    def _(tile):
         relay(tile)
 
     @pl.loop(0, n_tiles)
@@ -216,11 +222,14 @@
         remote(ref, ref, csend.at[0], crecv.at[tile], to_core).wait_recv()
         give_core(tile).wait_send()
 
-    @pl.loop(0, n_own)
+    @pl.loop(0, theirs)
     def _(tile):
         ref = y_ref.at[rows(corner, tile)]
         remote(ref, ref, rsend.at[0], rrecv.at[tile], to_core).wait_recv()
         pass_on(tile).wait_send()
+
+    @pl.loop(0, mine)
+    def _(tile):
         give_chip(tile).wait_send()
 
     for copy in sends:
@@ -232,12 +241,13 @@
 def forward_all(x_rows, own, chip, twin, near_first, near_second, n_stage, n_both):
     n_rows, dim = x_rows.shape
     width = own[0].shape[1]
-    n_own = (n_rows // TILE - 2 * n_both) // 4
+    n_own = max(OWN_TILES)
     n_tiles = n_own + n_both
+    assert TILE * (sum(OWN_TILES) + 2 * n_both) == n_rows
     dma = pltpu.SemaphoreType.DMA
     flops = 4 * n_tiles * TILE * dim * width * n_stage
     return pl.pallas_call(
-        functools.partial(forward_kernel, n_own, n_both),
+        functools.partial(forward_kernel, OWN_TILES[0], OWN_TILES[2], n_both),
         out_shape=(pltpu.VMEM((n_rows, dim), jnp.bfloat16), jax.ShapeDtypeStruct(near_first.shape, jnp.float32), jax.ShapeDtypeStruct(near_second.shape, jnp.float32)),
         in_specs=[pl.BlockSpec(memory_space=pl.ANY)] * 9,
         out_specs=(pl.BlockSpec(memory_space=pltpu.VMEM),) + (pl.BlockSpec(memory_space=pl.ANY),) * 2,

time: 431 us -> 428 us (level)
  Pallas kernels: 395 us -> 390 us
    pallas_call x1, Pallas kernels: 216 us -> 211 us  [forward_all(): pl.pallas_call(functools.partial(forward_kernel, OWN_TILES[0], OWN_TILES[...]
where the time goes in v7:
time: 428 us; the launch traced here: 426 us
  Pallas kernels  390 us (91%)
  waiting for transfers between devices  30.6 us (7%)
    pallas_call x1, Pallas kernels, forward_all(): pl.pallas_call(functools.partial(forward_kernel, OWN_TILES[0], OWN_TILES[...  211 us
    pallas_call x1, Pallas kernels, backward_all(): pl.pallas_call(backward_kernel, out_shape=(jax.ShapeDtypeStruct((half1, w...  143 us
    pallas_call x2, Pallas kernels, half_update(): pl.pallas_call(functools.partial(update_kernel, len(in_specs) - 2), out_s...  35.7 us
    ppermute x2, waiting for transfers between devices, stage_program(): twin = tuple((lax.ppermute(arr, 'data', [(0, 1), (1, 0)]) for arr in own))  30.6 us
  transfers between devices with their start and end apart: 4, of which 2 were waited for; matrix products, arithmetic and copies ran while one was open for 0% of the time, Pallas kernels for 3%

profile of v7, /device:TPU:7, one launch (start us, length us, event | category | flops | bytes accessed | tf_op | source)
XLA Modules:
  0.0 426.0 jit_solution(11897849322676071478)
XLA Ops:
  1.9 143.4 %backward_all.1 = (f32[256,2048]{1,0:T(8,128)}, f32[1024,512]{1,0:T(8,128)}, f32[8,128]{1,0:T(8,128)}, bf16[256,2048]{1,0:T(8,128)(2,1)}, bf16[1024,512]{1,0:T(8,128)(2,1)}) custom-call(f32[1]{0:T(128)S(6)} %copy.33.limit_ref, f32[1]{0:T(128)S(6)} %copy.32.rate_ref, bf16[2048,512]{1,0:T(8,128)(2,1)} %bitcast.47, bf16[2048,512]{1,0:T(8,128)(2,1)} %dout_ref.1, ...), custom_call_target="tpu_custom_call" | custom-call | flops 21474836480 | bytes 41943040 | tf_op jit(solution)/shard_map/backward_all/pallas_call | solution.py:560
  145.3 0.3 collective-permute-start.2
  145.6 0.0 collective-permute-start
  145.6 1.2 collective-permute-start.3
  146.8 1.5 collective-permute-start.1
  148.2 13.3 %near_update.1 = (f32[512,2048]{1,0:T(8,128)}, f32[512,2048]{1,0:T(8,128)}, f32[512,2048]{1,0:T(8,128)}, f32[2048,512]{1,0:T(8,128)}, f32[2048,512]{1,0:T(8,128)}, /*index=5*/f32[2048,512]{1,0:T(8,128)}) custom-call(s32[1]{0:T(128)} %bitcast.11.half_ref, f32[1]{0:T(128)S(6)} %copy.32.rate_ref, f32[8,128]{1,0:T(8,128)} %get-tuple-element.28.clip_ref, ...), custom_call_target="tpu_custom_call" | custom-call | flops 31457280 | bytes 31457280 | tf_op jit(solution)/shard_map/near_update/pallas_call | solution.py:321
  161.6 8.2 %collective-permute-done.2.rw1_ref = bf16[256,2048]{1,0:T(8,128)(2,1)S(1)} collective-permute-done((bf16[256,2048]{1,0:T(8,128)(2,1)}, bf16[256,2048]{1,0:T(8,128)(2,1)S(1)}, u32[]{:S(2)}, u32[]{:S(2)}) %collective-permute-start.2) | collective-permute-done | bytes 1048608 | tf_op jit(solution)/shard_map/ppermute | solution.py:593
  169.7 0.0 copy-start
  169.7 0.0 collective-permute-done.xw1_ref
  169.7 22.5 %collective-permute-done.3.rw2_ref = bf16[1024,512]{1,0:T(8,128)(2,1)} collective-permute-done((bf16[1024,512]{1,0:T(8,128)(2,1)}, bf16[1024,512]{1,0:T(8,128)(2,1)}, u32[]{:S(2)}, u32[]{:S(2)}) %collective-permute-start.3) | collective-permute-done | bytes 1048608 | tf_op jit(solution)/shard_map/ppermute | solution.py:593
  192.2 0.0 collective-permute-done.1.xw2_ref
  192.2 0.0 copy-done
  192.2 211.2 %forward_all.1 = (bf16[32768,512]{1,0:T(8,128)(2,1)S(1)}, f32[256,2048]{1,0:T(8,128)}, f32[1024,512]{1,0:T(8,128)}) custom-call(bf16[32768,512]{1,0:T(8,128)(2,1)} %bitcast.43, bf16[256,2048]{1,0:T(8,128)(2,1)} %get-tuple-element.29.w1_ref, bf16[1024,512]{1,0:T(8,128)(2,1)} %get-tuple-element.30.w2_ref, bf16[256,2048]{1,0:T(8,128)(2,1)} %collective-permute-done.xw1_ref, ...), custom_call_target="tpu_custom_call" | custom-call | flops 154618822656 | bytes 67108864 | tf_op jit(solution)/shard_map/forward_all/pallas_call | solution.py:249
  403.4 22.4 %far_update.1 = (f32[512,2048]{1,0:T(8,128)}, f32[512,2048]{1,0:T(8,128)}, f32[512,2048]{1,0:T(8,128)}, f32[2048,512]{1,0:T(8,128)}, f32[2048,512]{1,0:T(8,128)}...) custom-call(s32[1]{0:T(128)} %bitcast.half_ref, ...), custom_call_target="tpu_custom_call", output_to_operand_aliasing={{0}: (12, {}), {1}: (13, {}), {2}: (14, {}), {3}: (15, {}),... | custom-call | flops 31457280 | bytes 31457280 | tf_op jit(solution)/shard_map/far_update/pallas_call | solution.py:321
Async XLA Ops:
  145.3 24.5 %collective-permute-start.2 = (bf16[256,2048]{1,0:T(8,128)(2,1)}, bf16[256,2048]{1,0:T(8,128)(2,1)S(1)}, u32[]{:S(2)}, u32[]{:S(2)}) collective-permute-start(bf16[256,2048]{1,0:T(8,128)(2,1)} %get-tuple-element.29.w1_ref), channel_id=1, source_target_pairs={{0,4},{4,0},{1,5},{5,1},{2,6},{6,2},{3,7},{7,3}} | collective-permute-start | bytes 3145736 | tf_op jit(solution)/shard_map/ppermute | solution.py:593
  145.6 24.2 %collective-permute-start = (bf16[256,2048]{1,0:T(8,128)(2,1)}, bf16[256,2048]{1,0:T(8,128)(2,1)}, u32[]{:S(2)}, u32[]{:S(2)}) collective-permute-start(bf16[256,2048]{1,0:T(8,128)(2,1)} %get-tuple-element.29.w1_ref), channel_id=1, source_target_pairs={{0,2},{1,3},{2,0},{3,1},{4,6},{5,7},{6,4},{7,5}} | collective-permute-start | bytes 3145736 | tf_op jit(solution)/shard_map/ppermute | solution.py:592
  145.6 46.6 %collective-permute-start.3 = (bf16[1024,512]{1,0:T(8,128)(2,1)}, bf16[1024,512]{1,0:T(8,128)(2,1)}, u32[]{:S(2)}, u32[]{:S(2)}) collective-permute-start(bf16[1024,512]{1,0:T(8,128)(2,1)} %get-tuple-element.30.w2_ref), channel_id=1, source_target_pairs={{0,4},{4,0},{1,5},{5,1},{2,6},{6,2},{3,7},{7,3}} | collective-permute-start | bytes 3145736 | tf_op jit(solution)/shard_map/ppermute | solution.py:593
  146.8 45.4 %collective-permute-start.1 = (bf16[1024,512]{1,0:T(8,128)(2,1)}, bf16[1024,512]{1,0:T(8,128)(2,1)}, u32[]{:S(2)}, u32[]{:S(2)}) collective-permute-start(bf16[1024,512]{1,0:T(8,128)(2,1)} %get-tuple-element.30.w2_ref), channel_id=1, source_target_pairs={{0,2},{1,3},{2,0},{3,1},{4,6},{5,7},{6,4},{7,5}} | collective-permute-start | bytes 3145736 | tf_op jit(solution)/shard_map/ppermute | solution.py:592
  169.7 22.5 %copy-start = (bf16[256,2048]{1,0:T(8,128)(2,1)}, bf16[256,2048]{1,0:T(8,128)(2,1)S(1)}, u32[]{:S(2)}) copy-start(bf16[256,2048]{1,0:T(8,128)(2,1)S(1)} %collective-permute-done.2.rw1_ref) | copy-start | bytes 3145732

commit v8 on v7

--- a/solution.py
+++ b/solution.py
@@ -19,12 +19,12 @@
 CHUNK = 512
 BEHIND = 3
 FORWARD_VMEM = 30
-LAG = 4
+LAG = 5
 PRE = 4
-SHARED = 3
-OWN_TILES = (15, 15, 14, 14)
+SHARED = 4
+OWN_TILES = (14, 14, 14, 14)
 UPDATE_STEPS = 8
-FINAL_STEPS = 16
+FINAL_STEPS = 8
 ADAM_ROWS = 32
 ROWS = 256
 PART = 512
@@ -122,23 +122,25 @@
         for kind in (0, 1):
             arrive(owner, partner, kind)
 
-    def block_step(src, block, dst):
+    def two_blocks(ref, pair):
         half = TILE // 2
         pieces = [(side, first) for first in range(0, width, CHUNK) for side in (0, 1)]
-        x_rows = [src[side * half:(side + 1) * half, :] for side in (0, 1)]
-        total = [None, None]
-        act_h = {}
-        for turn in range(len(pieces) + BEHIND):
-            if turn < len(pieces):
-                side, first = pieces[turn]
-                halved = jnp.dot(x_rows[side], w1v[block, :, first:first + CHUNK], preferred_element_type=jnp.float32)
-                act_h[turn] = gelu_of_half(halved).astype(jnp.bfloat16)
-            if turn >= BEHIND:
-                side, first = pieces[turn - BEHIND]
-                piece = jnp.dot(act_h.pop(turn - BEHIND), w2v[block, first:first + CHUNK, :], preferred_element_type=jnp.float32)
-                total[side] = piece if first == 0 else total[side] + piece
+        x_rows = [ref[side * half:(side + 1) * half, :] for side in (0, 1)]
+        for block in (2 * pair, 2 * pair + 1):
+            total = [None, None]
+            act_h = {}
+            for turn in range(len(pieces) + BEHIND):
+                if turn < len(pieces):
+                    side, first = pieces[turn]
+                    halved = jnp.dot(x_rows[side], w1v[block, :, first:first + CHUNK], preferred_element_type=jnp.float32)
+                    act_h[turn] = gelu_of_half(halved).astype(jnp.bfloat16)
+                if turn >= BEHIND:
+                    side, first = pieces[turn - BEHIND]
+                    piece = jnp.dot(act_h.pop(turn - BEHIND), w2v[block, first:first + CHUNK, :], preferred_element_type=jnp.float32)
+                    total[side] = piece if first == 0 else total[side] + piece
+            x_rows = [(x_rows[side].astype(jnp.float32) + total[side]).astype(jnp.bfloat16) for side in (0, 1)]
         for side in (0, 1):
-            dst[side * half:(side + 1) * half, :] = (x_rows[side].astype(jnp.float32) + total[side]).astype(jnp.bfloat16)
+            ref[side * half:(side + 1) * half, :] = x_rows[side]
 
     @pl.when(early)
     def _():
@@ -146,9 +148,7 @@
         def _(tile):
             load_p(tile).wait()
 
-            @pl.loop(0, 2)
-            def _(block):
-                block_step(pv.at[tile], block, pv.at[tile])
+            two_blocks(pv.at[tile], 0)
 
     for kind in (0, 1):
         arrive(far, across, kind)
@@ -195,11 +195,11 @@
         def _():
             load_x(tile + 1).start()
 
-        @pl.loop(0, n_blocks)
-        def _(block):
-            @pl.when((block >= 2) | (tile >= skip))
+        @pl.loop(0, n_blocks // 2)
+        def _(pair):
+            @pl.when((pair > 0) | (tile >= skip))
             def _():
-                block_step(xv.at[tile % 2], block, xv.at[tile % 2])
+                two_blocks(xv.at[tile % 2], pair)
 
         y_ref[rows(stage, tile), :] = xv[tile % 2]
         give_core(tile).start()
@@ -324,7 +324,7 @@
         grid_spec=pltpu.PrefetchScalarGridSpec(num_scalar_prefetch=1, grid=(steps,), in_specs=in_specs, out_specs=tuple(out_specs),
                                               scratch_shapes=[pltpu.SemaphoreType.DMA((FINAL_STEPS,))] if made else []),
         input_output_aliases=aliases,
-        compiler_params=pltpu.CompilerParams(vmem_limit_bytes=(28 if made else 62) * 2 ** 20),
+        compiler_params=pltpu.CompilerParams(vmem_limit_bytes=(24 if made else 62) * 2 ** 20),
         cost_estimate=pl.CostEstimate(flops=30 * 2 ** 20, bytes_accessed=30 * 2 ** 20, transcendentals=0),
         name='far_update' if made else 'near_update',
     )(*args)

time: 428 us -> 421 us (0.984)
  Pallas kernels: 390 us -> 384 us
    pallas_call x1, Pallas kernels: 211 us -> 207 us  [forward_all(): pl.pallas_call(functools.partial(forward_kernel, OWN_TILES[0], OWN_TILES[...]
where the time goes in v8:
time: 421 us; the launch traced here: 420 us
  Pallas kernels  384 us (91%)
  waiting for transfers between devices  30.6 us (7%)
    pallas_call x1, Pallas kernels, forward_all(): pl.pallas_call(functools.partial(forward_kernel, OWN_TILES[0], OWN_TILES[...  207 us
    pallas_call x1, Pallas kernels, backward_all(): pl.pallas_call(backward_kernel, out_shape=(jax.ShapeDtypeStruct((half1, w...  143 us
    pallas_call x2, Pallas kernels, half_update(): pl.pallas_call(functools.partial(update_kernel, len(in_specs) - 2), out_s...  34.4 us
    ppermute x2, waiting for transfers between devices, stage_program(): twin = tuple((lax.ppermute(arr, 'data', [(0, 1), (1, 0)]) for arr in own))  30.6 us
  transfers between devices with their start and end apart: 4, of which 2 were waited for; matrix products, arithmetic and copies ran while one was open for 0% of the time, Pallas kernels for 3%

profile of v8, /device:TPU:7, one launch (start us, length us, event | category | flops | bytes accessed | tf_op | source)
XLA Modules:
  0.0 420.0 jit_solution(17435561178521400349)
XLA Ops:
  1.9 143.4 %backward_all.1 = (f32[256,2048]{1,0:T(8,128)}, f32[1024,512]{1,0:T(8,128)}, f32[8,128]{1,0:T(8,128)}, bf16[256,2048]{1,0:T(8,128)(2,1)}, bf16[1024,512]{1,0:T(8,128)(2,1)}) custom-call(f32[1]{0:T(128)S(6)} %copy.33.limit_ref, f32[1]{0:T(128)S(6)} %copy.32.rate_ref, bf16[2048,512]{1,0:T(8,128)(2,1)} %bitcast.47, bf16[2048,512]{1,0:T(8,128)(2,1)} %dout_ref.1, ...), custom_call_target="tpu_custom_call" | custom-call | flops 21474836480 | bytes 41943040 | tf_op jit(solution)/shard_map/backward_all/pallas_call | solution.py:560
  145.3 0.3 collective-permute-start.2
  145.6 0.0 collective-permute-start
  145.6 1.2 collective-permute-start.3
  146.8 1.5 collective-permute-start.1
  148.2 13.3 %near_update.1 = (f32[512,2048]{1,0:T(8,128)}, f32[512,2048]{1,0:T(8,128)}, f32[512,2048]{1,0:T(8,128)}, f32[2048,512]{1,0:T(8,128)}, f32[2048,512]{1,0:T(8,128)}, /*index=5*/f32[2048,512]{1,0:T(8,128)}) custom-call(s32[1]{0:T(128)} %bitcast.11.half_ref, f32[1]{0:T(128)S(6)} %copy.32.rate_ref, f32[8,128]{1,0:T(8,128)} %get-tuple-element.28.clip_ref, ...), custom_call_target="tpu_custom_call" | custom-call | flops 31457280 | bytes 31457280 | tf_op jit(solution)/shard_map/near_update/pallas_call | solution.py:321
  161.6 8.2 %collective-permute-done.2.rw1_ref = bf16[256,2048]{1,0:T(8,128)(2,1)S(1)} collective-permute-done((bf16[256,2048]{1,0:T(8,128)(2,1)}, bf16[256,2048]{1,0:T(8,128)(2,1)S(1)}, u32[]{:S(2)}, u32[]{:S(2)}) %collective-permute-start.2) | collective-permute-done | bytes 1048608 | tf_op jit(solution)/shard_map/ppermute | solution.py:593
  169.7 0.0 copy-start
  169.7 0.0 collective-permute-done.xw1_ref
  169.7 22.5 %collective-permute-done.3.rw2_ref = bf16[1024,512]{1,0:T(8,128)(2,1)} collective-permute-done((bf16[1024,512]{1,0:T(8,128)(2,1)}, bf16[1024,512]{1,0:T(8,128)(2,1)}, u32[]{:S(2)}, u32[]{:S(2)}) %collective-permute-start.3) | collective-permute-done | bytes 1048608 | tf_op jit(solution)/shard_map/ppermute | solution.py:593
  192.2 0.0 collective-permute-done.1.xw2_ref
  192.2 0.0 copy-done
  192.2 206.5 %forward_all.1 = (bf16[32768,512]{1,0:T(8,128)(2,1)S(1)}, f32[256,2048]{1,0:T(8,128)}, f32[1024,512]{1,0:T(8,128)}) custom-call(bf16[32768,512]{1,0:T(8,128)(2,1)} %bitcast.43, bf16[256,2048]{1,0:T(8,128)(2,1)} %get-tuple-element.29.w1_ref, bf16[1024,512]{1,0:T(8,128)(2,1)} %get-tuple-element.30.w2_ref, bf16[256,2048]{1,0:T(8,128)(2,1)} %collective-permute-done.xw1_ref, ...), custom_call_target="tpu_custom_call" | custom-call | flops 154618822656 | bytes 67108864 | tf_op jit(solution)/shard_map/forward_all/pallas_call | solution.py:249
  398.8 21.1 %far_update.1 = (f32[512,2048]{1,0:T(8,128)}, f32[512,2048]{1,0:T(8,128)}, f32[512,2048]{1,0:T(8,128)}, f32[2048,512]{1,0:T(8,128)}, f32[2048,512]{1,0:T(8,128)}...) custom-call(s32[1]{0:T(128)} %bitcast.half_ref, ...), custom_call_target="tpu_custom_call", output_to_operand_aliasing={{0}: (12, {}), {1}: (13, {}), {2}: (14, {}), {3}: (15, {}),... | custom-call | flops 31457280 | bytes 31457280 | tf_op jit(solution)/shard_map/far_update/pallas_call | solution.py:321
Async XLA Ops:
  145.3 24.5 %collective-permute-start.2 = (bf16[256,2048]{1,0:T(8,128)(2,1)}, bf16[256,2048]{1,0:T(8,128)(2,1)S(1)}, u32[]{:S(2)}, u32[]{:S(2)}) collective-permute-start(bf16[256,2048]{1,0:T(8,128)(2,1)} %get-tuple-element.29.w1_ref), channel_id=1, source_target_pairs={{0,4},{4,0},{1,5},{5,1},{2,6},{6,2},{3,7},{7,3}} | collective-permute-start | bytes 3145736 | tf_op jit(solution)/shard_map/ppermute | solution.py:593
  145.6 24.2 %collective-permute-start = (bf16[256,2048]{1,0:T(8,128)(2,1)}, bf16[256,2048]{1,0:T(8,128)(2,1)}, u32[]{:S(2)}, u32[]{:S(2)}) collective-permute-start(bf16[256,2048]{1,0:T(8,128)(2,1)} %get-tuple-element.29.w1_ref), channel_id=1, source_target_pairs={{0,2},{1,3},{2,0},{3,1},{4,6},{5,7},{6,4},{7,5}} | collective-permute-start | bytes 3145736 | tf_op jit(solution)/shard_map/ppermute | solution.py:592
  145.6 46.6 %collective-permute-start.3 = (bf16[1024,512]{1,0:T(8,128)(2,1)}, bf16[1024,512]{1,0:T(8,128)(2,1)}, u32[]{:S(2)}, u32[]{:S(2)}) collective-permute-start(bf16[1024,512]{1,0:T(8,128)(2,1)} %get-tuple-element.30.w2_ref), channel_id=1, source_target_pairs={{0,4},{4,0},{1,5},{5,1},{2,6},{6,2},{3,7},{7,3}} | collective-permute-start | bytes 3145736 | tf_op jit(solution)/shard_map/ppermute | solution.py:593
  146.8 45.4 %collective-permute-start.1 = (bf16[1024,512]{1,0:T(8,128)(2,1)}, bf16[1024,512]{1,0:T(8,128)(2,1)}, u32[]{:S(2)}, u32[]{:S(2)}) collective-permute-start(bf16[1024,512]{1,0:T(8,128)(2,1)} %get-tuple-element.30.w2_ref), channel_id=1, source_target_pairs={{0,2},{1,3},{2,0},{3,1},{4,6},{5,7},{6,4},{7,5}} | collective-permute-start | bytes 3145736 | tf_op jit(solution)/shard_map/ppermute | solution.py:592
  169.7 22.5 %copy-start = (bf16[256,2048]{1,0:T(8,128)(2,1)}, bf16[256,2048]{1,0:T(8,128)(2,1)S(1)}, u32[]{:S(2)}) copy-start(bf16[256,2048]{1,0:T(8,128)(2,1)S(1)} %collective-permute-done.2.rw1_ref) | copy-start | bytes 3145732

commit v9 on v8

--- a/solution.py
+++ b/solution.py
@@ -331,9 +331,9 @@
 
 
 def backward_kernel(limit_ref, rate_ref, act_ref, dout_ref, w1_ref, w2_ref, m1_ref, m2_ref, v1_ref, v2_ref, acc1_ref, acc2_ref,
-                    g1_ref, g2_ref, clip_ref, b1_ref, b2_ref,
+                    g1_out, g2_out, clip_ref, b1_out, b2_out, g1_ref, g2_ref, b1_ref, b2_ref,
                     actv, grad, w1v, w2v, hid, slope, dpre, sent, accv, inbox,
-                    norms, lsem, hsem, asem, csend, crecv, rsend, rrecv, nsend, nrecv):
+                    norms, lsem, hsem, gsem, bsem, asem, csend, crecv, rsend, rrecv, nsend, nrecv):
     stage = lax.axis_index('stage')
     rep = lax.axis_index('data')
     far = 1 - rep
@@ -489,12 +489,38 @@
         if step + ahead < len(steps):
             load_acc(*steps[step + ahead], step + ahead).start()
 
+    for copy in near:
+        copy.wait()
+    mom_fix, sec_fix = 1.0 / (1.0 - BETA_ONE ** STEP_COUNT), 1.0 / (1.0 - BETA_TWO ** STEP_COUNT)
+    kept = (1.0 - WEIGHT_DECAY * rate_ref[0], BETA_ONE * mom_fix, BETA_TWO * sec_fix)
+
+    @pl.loop(0, half1 // ADAM_ROWS)
+    def _(idx):
+        for which in range(6):
+            span = pl.ds(pl.multiple_of(dim + which * half1 + idx * ADAM_ROWS, ADAM_ROWS), ADAM_ROWS)
+            slope[span, :] = kept[which % 3] * slope[span, :]
+
+    def new_weight(which, coef, slope_rows, cols, grad_val):
+        base, mom, sec = (slope[pl.ds(pl.multiple_of(dim + (which + idx) * half1 + slope_rows, ADAM_ROWS), ADAM_ROWS), cols] for idx in range(3))
+        scaled = coef * grad_val
+        top = mom + ((1.0 - BETA_ONE) * mom_fix) * scaled
+        low = jnp.sqrt(sec + ((1.0 - BETA_TWO) * sec_fix) * (scaled * scaled)) + ADAM_EPS
+        return base - rate_ref[0] * (top / low)
+
+    def put_grad(idx):
+        if idx < n_cols:
+            where = (slice(None), slice(idx * PART, (idx + 1) * PART))
+            return pltpu.make_async_copy(g1_ref.at[where], g1_out.at[where], gsem.at[idx])
+        where = slice((idx - n_cols) * half1, (idx - n_cols + 1) * half1)
+        return pltpu.make_async_copy(g2_ref.at[where], g2_out.at[where], gsem.at[idx])
+
     squares = jnp.zeros((8, PART), jnp.float32)
     for idx in range(n_parts):
         post(idx).wait_recv()
         ref, where = own_part(idx)
         mean = 0.5 * (ref[where] + inbox[idx])
         ref[where] = mean
+        put_grad(idx).start()
         squares = squares + jnp.sum((mean * mean).reshape(half1 // 8, 8, PART), axis=0)
     norms[place] = squares
 
@@ -517,25 +543,28 @@
     total = jnp.sum(jnp.sum(total, axis=0, keepdims=True), axis=1, keepdims=True)
     clip = jnp.minimum(1.0, limit_ref[0] / (jnp.sqrt(total) + NORM_EPS))
     clip_ref[...] = jnp.broadcast_to(clip, clip_ref.shape)
-    for copy in near:
-        copy.wait()
+    puts = [pltpu.make_async_copy(b1_ref, b1_out, bsem.at[0]), pltpu.make_async_copy(b2_ref, b2_out, bsem.at[1])]
 
     @pl.loop(0, half1 // ADAM_ROWS)
     def _(idx):
-        def from_slope(which, cols):
-            return slope[pl.ds(pl.multiple_of(dim + which * half1 + idx * ADAM_ROWS, ADAM_ROWS), ADAM_ROWS), cols]
-
-        coef = clip_ref[0:1, 0:1]
         span = pl.ds(pl.multiple_of(idx * ADAM_ROWS, ADAM_ROWS), ADAM_ROWS)
-        every = slice(0, width)
-        new_w, _, _ = adamw_rows(coef, rate_ref[0], from_slope(0, every), from_slope(1, every), from_slope(2, every), g1_ref[span, :])
+        new_w = new_weight(0, clip_ref[0:1, 0:1], idx * ADAM_ROWS, slice(0, width), g1_ref[span, :])
         b1_ref[span, :] = (0.5 * new_w).astype(jnp.bfloat16)
+
+    puts[0].start()
+
+    @pl.loop(0, half1 // ADAM_ROWS)
+    def _(idx):
         for group in range(4):
-            cols = slice(group * dim, (group + 1) * dim)
             span = pl.ds(pl.multiple_of(group * half1 + idx * ADAM_ROWS, ADAM_ROWS), ADAM_ROWS)
-            new_w, _, _ = adamw_rows(coef, rate_ref[0], from_slope(3, cols), from_slope(4, cols), from_slope(5, cols), g2_ref[span, :])
+            new_w = new_weight(3, clip_ref[0:1, 0:1], idx * ADAM_ROWS, slice(group * dim, (group + 1) * dim), g2_ref[span, :])
             b2_ref[span, :] = new_w.astype(jnp.bfloat16)
 
+    puts[1].start()
+    for idx in range(n_parts):
+        put_grad(idx).wait()
+    for copy in puts:
+        copy.wait()
     for idx in range(7):
         tell(idx).wait_send()
     for idx in range(n_parts):
@@ -562,13 +591,14 @@
         out_shape=(jax.ShapeDtypeStruct((half1, width), f32), jax.ShapeDtypeStruct((width // 2, dim), f32), jax.ShapeDtypeStruct((8, 128), f32),
                    jax.ShapeDtypeStruct((half1, width), bf16), jax.ShapeDtypeStruct((width // 2, dim), bf16)),
         in_specs=[pl.BlockSpec(memory_space=pltpu.SMEM)] * 2 + [pl.BlockSpec(memory_space=pl.ANY)] * 10,
-        out_specs=(vmem,) * 5,
+        out_specs=(pl.BlockSpec(memory_space=pl.ANY),) * 2 + (vmem,) + (pl.BlockSpec(memory_space=pl.ANY),) * 2,
         scratch_shapes=[
+            pltpu.VMEM((half1, width), f32), pltpu.VMEM((width // 2, dim), f32), pltpu.VMEM((half1, width), bf16), pltpu.VMEM((width // 2, dim), bf16),
             pltpu.VMEM((n_rows, dim), bf16), pltpu.VMEM((n_rows, dim), bf16),
             pltpu.VMEM((dim, width), bf16), pltpu.VMEM((width, dim), bf16),
             pltpu.VMEM((n_rows, width), bf16), pltpu.VMEM((n_rows, width), f32), pltpu.VMEM((n_rows, width), bf16),
             pltpu.VMEM((n_rows, dim), bf16), pltpu.VMEM((4, half1, PART), f32), pltpu.VMEM((n_parts, half1, PART), f32), pltpu.VMEM((8, 8, PART), f32),
-            dma((7,)), dma((15,)), dma((4,)), dma((n_chunks,)), dma((n_chunks,)), dma((n_parts,)), dma((n_parts,)), dma((7,)), dma((8,)),
+            dma((7,)), dma((15,)), dma((n_parts,)), dma((2,)), dma((4,)), dma((n_chunks,)), dma((n_chunks,)), dma((n_parts,)), dma((n_parts,)), dma((7,)), dma((8,)),
         ],
         compiler_params=pltpu.CompilerParams(collective_id=1, has_side_effects=True, vmem_limit_bytes=63 * 2 ** 20),
         cost_estimate=pl.CostEstimate(flops=10 * n_rows * dim * width, bytes_accessed=40 * 2 ** 20, transcendentals=0),

time: 421 us -> 418 us (level)
  no operation moved by 1% of the time
where the time goes in v9:
time: 418 us; the launch traced here: 417 us
  Pallas kernels  381 us (91%)
  waiting for transfers between devices  30.6 us (7%)
    pallas_call x1, Pallas kernels, forward_all(): pl.pallas_call(functools.partial(forward_kernel, OWN_TILES[0], OWN_TILES[...  207 us
    pallas_call x1, Pallas kernels, backward_all(): pl.pallas_call(backward_kernel, out_shape=(jax.ShapeDtypeStruct((half1, w...  141 us
    pallas_call x2, Pallas kernels, half_update(): pl.pallas_call(functools.partial(update_kernel, len(in_specs) - 2), out_s...  34.4 us
    ppermute x2, waiting for transfers between devices, stage_program(): twin = tuple((lax.ppermute(arr, 'data', [(0, 1), (1, 0)]) for arr in own))  30.6 us
  transfers between devices with their start and end apart: 4, of which 2 were waited for; matrix products, arithmetic and copies ran while one was open for 0% of the time, Pallas kernels for 3%

profile of v9, /device:TPU:7, one launch (start us, length us, event | category | flops | bytes accessed | tf_op | source)
XLA Modules:
  0.0 417.2 jit_solution(12817418104277671635)
XLA Ops:
  1.9 140.5 %backward_all.1 = (f32[256,2048]{1,0:T(8,128)}, f32[1024,512]{1,0:T(8,128)}, f32[8,128]{1,0:T(8,128)}, bf16[256,2048]{1,0:T(8,128)(2,1)}, bf16[1024,512]{1,0:T(8,128)(2,1)}) custom-call(f32[1]{0:T(128)S(6)} %copy.33.limit_ref, f32[1]{0:T(128)S(6)} %copy.32.rate_ref, bf16[2048,512]{1,0:T(8,128)(2,1)} %bitcast.47, bf16[2048,512]{1,0:T(8,128)(2,1)} %dout_ref.1, ...), custom_call_target="tpu_custom_call" | custom-call | flops 21474836480 | bytes 41943040 | tf_op jit(solution)/shard_map/backward_all/pallas_call | solution.py:589
  142.4 0.3 collective-permute-start.2
  142.7 0.0 collective-permute-start
  142.7 1.2 collective-permute-start.3
  143.9 1.5 collective-permute-start.1
  145.4 13.3 %near_update.1 = (f32[512,2048]{1,0:T(8,128)}, f32[512,2048]{1,0:T(8,128)}, f32[512,2048]{1,0:T(8,128)}, f32[2048,512]{1,0:T(8,128)}, f32[2048,512]{1,0:T(8,128)}, /*index=5*/f32[2048,512]{1,0:T(8,128)}) custom-call(s32[1]{0:T(128)} %bitcast.11.half_ref, f32[1]{0:T(128)S(6)} %copy.32.rate_ref, f32[8,128]{1,0:T(8,128)} %get-tuple-element.28.clip_ref, ...), custom_call_target="tpu_custom_call" | custom-call | flops 31457280 | bytes 31457280 | tf_op jit(solution)/shard_map/near_update/pallas_call | solution.py:321
  158.7 8.2 %collective-permute-done.2.rw1_ref = bf16[256,2048]{1,0:T(8,128)(2,1)S(1)} collective-permute-done((bf16[256,2048]{1,0:T(8,128)(2,1)}, bf16[256,2048]{1,0:T(8,128)(2,1)S(1)}, u32[]{:S(2)}, u32[]{:S(2)}) %collective-permute-start.2) | collective-permute-done | bytes 1048608 | tf_op jit(solution)/shard_map/ppermute | solution.py:623
  166.9 0.0 copy-start
  166.9 0.0 collective-permute-done.xw1_ref
  166.9 22.5 %collective-permute-done.3.rw2_ref = bf16[1024,512]{1,0:T(8,128)(2,1)} collective-permute-done((bf16[1024,512]{1,0:T(8,128)(2,1)}, bf16[1024,512]{1,0:T(8,128)(2,1)}, u32[]{:S(2)}, u32[]{:S(2)}) %collective-permute-start.3) | collective-permute-done | bytes 1048608 | tf_op jit(solution)/shard_map/ppermute | solution.py:623
  189.4 0.0 collective-permute-done.1.xw2_ref
  189.4 0.0 copy-done
  189.4 206.5 %forward_all.1 = (bf16[32768,512]{1,0:T(8,128)(2,1)S(1)}, f32[256,2048]{1,0:T(8,128)}, f32[1024,512]{1,0:T(8,128)}) custom-call(bf16[32768,512]{1,0:T(8,128)(2,1)} %bitcast.43, bf16[256,2048]{1,0:T(8,128)(2,1)} %get-tuple-element.29.w1_ref, bf16[1024,512]{1,0:T(8,128)(2,1)} %get-tuple-element.30.w2_ref, bf16[256,2048]{1,0:T(8,128)(2,1)} %collective-permute-done.xw1_ref, ...), custom_call_target="tpu_custom_call" | custom-call | flops 154618822656 | bytes 67108864 | tf_op jit(solution)/shard_map/forward_all/pallas_call | solution.py:249
  395.9 21.1 %far_update.1 = (f32[512,2048]{1,0:T(8,128)}, f32[512,2048]{1,0:T(8,128)}, f32[512,2048]{1,0:T(8,128)}, f32[2048,512]{1,0:T(8,128)}, f32[2048,512]{1,0:T(8,128)}...) custom-call(s32[1]{0:T(128)} %bitcast.half_ref, ...), custom_call_target="tpu_custom_call", output_to_operand_aliasing={{0}: (12, {}), {1}: (13, {}), {2}: (14, {}), {3}: (15, {}),... | custom-call | flops 31457280 | bytes 31457280 | tf_op jit(solution)/shard_map/far_update/pallas_call | solution.py:321
Async XLA Ops:
  142.4 24.5 %collective-permute-start.2 = (bf16[256,2048]{1,0:T(8,128)(2,1)}, bf16[256,2048]{1,0:T(8,128)(2,1)S(1)}, u32[]{:S(2)}, u32[]{:S(2)}) collective-permute-start(bf16[256,2048]{1,0:T(8,128)(2,1)} %get-tuple-element.29.w1_ref), channel_id=1, source_target_pairs={{0,4},{4,0},{1,5},{5,1},{2,6},{6,2},{3,7},{7,3}} | collective-permute-start | bytes 3145736 | tf_op jit(solution)/shard_map/ppermute | solution.py:623
  142.7 24.2 %collective-permute-start = (bf16[256,2048]{1,0:T(8,128)(2,1)}, bf16[256,2048]{1,0:T(8,128)(2,1)}, u32[]{:S(2)}, u32[]{:S(2)}) collective-permute-start(bf16[256,2048]{1,0:T(8,128)(2,1)} %get-tuple-element.29.w1_ref), channel_id=1, source_target_pairs={{0,2},{1,3},{2,0},{3,1},{4,6},{5,7},{6,4},{7,5}} | collective-permute-start | bytes 3145736 | tf_op jit(solution)/shard_map/ppermute | solution.py:622
  142.7 46.6 %collective-permute-start.3 = (bf16[1024,512]{1,0:T(8,128)(2,1)}, bf16[1024,512]{1,0:T(8,128)(2,1)}, u32[]{:S(2)}, u32[]{:S(2)}) collective-permute-start(bf16[1024,512]{1,0:T(8,128)(2,1)} %get-tuple-element.30.w2_ref), channel_id=1, source_target_pairs={{0,4},{4,0},{1,5},{5,1},{2,6},{6,2},{3,7},{7,3}} | collective-permute-start | bytes 3145736 | tf_op jit(solution)/shard_map/ppermute | solution.py:623
  143.9 45.4 %collective-permute-start.1 = (bf16[1024,512]{1,0:T(8,128)(2,1)}, bf16[1024,512]{1,0:T(8,128)(2,1)}, u32[]{:S(2)}, u32[]{:S(2)}) collective-permute-start(bf16[1024,512]{1,0:T(8,128)(2,1)} %get-tuple-element.30.w2_ref), channel_id=1, source_target_pairs={{0,2},{1,3},{2,0},{3,1},{4,6},{5,7},{6,4},{7,5}} | collective-permute-start | bytes 3145736 | tf_op jit(solution)/shard_map/ppermute | solution.py:622
  166.9 22.5 %copy-start = (bf16[256,2048]{1,0:T(8,128)(2,1)}, bf16[256,2048]{1,0:T(8,128)(2,1)S(1)}, u32[]{:S(2)}) copy-start(bf16[256,2048]{1,0:T(8,128)(2,1)S(1)} %collective-permute-done.2.rw1_ref) | copy-start | bytes 3145732

commit v10 on v9

--- a/solution.py
+++ b/solution.py
@@ -24,7 +24,7 @@
 SHARED = 4
 OWN_TILES = (14, 14, 14, 14)
 UPDATE_STEPS = 8
-FINAL_STEPS = 8
+FINAL_STEPS = 4
 ADAM_ROWS = 32
 ROWS = 256
 PART = 512
@@ -122,10 +122,10 @@
         for kind in (0, 1):
             arrive(owner, partner, kind)
 
-    def two_blocks(ref, pair):
+    def two_blocks(src, pair, dst):
         half = TILE // 2
         pieces = [(side, first) for first in range(0, width, CHUNK) for side in (0, 1)]
-        x_rows = [ref[side * half:(side + 1) * half, :] for side in (0, 1)]
+        x_rows = [src[side * half:(side + 1) * half, :] for side in (0, 1)]
         for block in (2 * pair, 2 * pair + 1):
             total = [None, None]
             act_h = {}
@@ -140,7 +140,7 @@
                     total[side] = piece if first == 0 else total[side] + piece
             x_rows = [(x_rows[side].astype(jnp.float32) + total[side]).astype(jnp.bfloat16) for side in (0, 1)]
         for side in (0, 1):
-            ref[side * half:(side + 1) * half, :] = x_rows[side]
+            dst[side * half:(side + 1) * half, :] = x_rows[side]
 
     @pl.when(early)
     def _():
@@ -148,7 +148,7 @@
         def _(tile):
             load_p(tile).wait()
 
-            two_blocks(pv.at[tile], 0)
+            two_blocks(pv.at[tile], 0, pv.at[tile])
 
     for kind in (0, 1):
         arrive(far, across, kind)
@@ -195,13 +195,11 @@
         def _():
             load_x(tile + 1).start()
 
-        @pl.loop(0, n_blocks // 2)
-        def _(pair):
-            @pl.when((pair > 0) | (tile >= skip))
-            def _():
-                two_blocks(xv.at[tile % 2], pair)
-
-        y_ref[rows(stage, tile), :] = xv[tile % 2]
+        @pl.when(tile >= skip)
+        def _():
+            two_blocks(xv.at[tile % 2], 0, xv.at[tile % 2])
+
+        two_blocks(xv.at[tile % 2], 1, y_ref.at[rows(stage, tile)])
         give_core(tile).start()
 
         @pl.when(tile < mine)

time: 418 us -> 416 us (level)
  no operation moved by 1% of the time
where the time goes in v10:
time: 416 us
  Pallas kernels  380 us (91%)
  waiting for transfers between devices  30.6 us (7%)
    pallas_call x1, Pallas kernels, forward_all(): pl.pallas_call(functools.partial(forward_kernel, OWN_TILES[0], OWN_TILES[...  206 us
    pallas_call x1, Pallas kernels, backward_all(): pl.pallas_call(backward_kernel, out_shape=(jax.ShapeDtypeStruct((half1, w...  141 us
    pallas_call x2, Pallas kernels, half_update(): pl.pallas_call(functools.partial(update_kernel, len(in_specs) - 2), out_s...  33.9 us
    ppermute x2, waiting for transfers between devices, stage_program(): twin = tuple((lax.ppermute(arr, 'data', [(0, 1), (1, 0)]) for arr in own))  30.6 us
  transfers between devices with their start and end apart: 4, of which 2 were waited for; matrix products, arithmetic and copies ran while one was open for 0% of the time, Pallas kernels for 3%

profile of v10, /device:TPU:7, one launch (start us, length us, event | category | flops | bytes accessed | tf_op | source)
XLA Modules:
  0.0 416.0 jit_solution(6621335354018771326)
XLA Ops:
  1.9 140.5 %backward_all.1 = (f32[256,2048]{1,0:T(8,128)}, f32[1024,512]{1,0:T(8,128)}, f32[8,128]{1,0:T(8,128)}, bf16[256,2048]{1,0:T(8,128)(2,1)}, bf16[1024,512]{1,0:T(8,128)(2,1)}) custom-call(f32[1]{0:T(128)S(6)} %copy.33.limit_ref, f32[1]{0:T(128)S(6)} %copy.32.rate_ref, bf16[2048,512]{1,0:T(8,128)(2,1)} %bitcast.47, bf16[2048,512]{1,0:T(8,128)(2,1)} %dout_ref.1, ...), custom_call_target="tpu_custom_call" | custom-call | flops 21474836480 | bytes 41943040 | tf_op jit(solution)/shard_map/backward_all/pallas_call | solution.py:587
  142.4 0.3 collective-permute-start.2
  142.7 0.0 collective-permute-start
  142.7 1.2 collective-permute-start.3
  143.9 1.5 collective-permute-start.1
  145.4 13.3 %near_update.1 = (f32[512,2048]{1,0:T(8,128)}, f32[512,2048]{1,0:T(8,128)}, f32[512,2048]{1,0:T(8,128)}, f32[2048,512]{1,0:T(8,128)}, f32[2048,512]{1,0:T(8,128)}, /*index=5*/f32[2048,512]{1,0:T(8,128)}) custom-call(s32[1]{0:T(128)} %bitcast.11.half_ref, f32[1]{0:T(128)S(6)} %copy.32.rate_ref, f32[8,128]{1,0:T(8,128)} %get-tuple-element.28.clip_ref, ...), custom_call_target="tpu_custom_call" | custom-call | flops 31457280 | bytes 31457280 | tf_op jit(solution)/shard_map/near_update/pallas_call | solution.py:319
  158.7 8.2 %collective-permute-done.2.rw1_ref = bf16[256,2048]{1,0:T(8,128)(2,1)S(1)} collective-permute-done((bf16[256,2048]{1,0:T(8,128)(2,1)}, bf16[256,2048]{1,0:T(8,128)(2,1)S(1)}, u32[]{:S(2)}, u32[]{:S(2)}) %collective-permute-start.2) | collective-permute-done | bytes 1048608 | tf_op jit(solution)/shard_map/ppermute | solution.py:621
  166.9 0.0 copy-start
  166.9 0.0 collective-permute-done.xw1_ref
  166.9 22.5 %collective-permute-done.3.rw2_ref = bf16[1024,512]{1,0:T(8,128)(2,1)} collective-permute-done((bf16[1024,512]{1,0:T(8,128)(2,1)}, bf16[1024,512]{1,0:T(8,128)(2,1)}, u32[]{:S(2)}, u32[]{:S(2)}) %collective-permute-start.3) | collective-permute-done | bytes 1048608 | tf_op jit(solution)/shard_map/ppermute | solution.py:621
  189.4 0.0 collective-permute-done.1.xw2_ref
  189.4 0.0 copy-done
  189.4 205.9 %forward_all.1 = (bf16[32768,512]{1,0:T(8,128)(2,1)S(1)}, f32[256,2048]{1,0:T(8,128)}, f32[1024,512]{1,0:T(8,128)}) custom-call(bf16[32768,512]{1,0:T(8,128)(2,1)} %bitcast.43, bf16[256,2048]{1,0:T(8,128)(2,1)} %get-tuple-element.29.w1_ref, bf16[1024,512]{1,0:T(8,128)(2,1)} %get-tuple-element.30.w2_ref, bf16[256,2048]{1,0:T(8,128)(2,1)} %collective-permute-done.xw1_ref, ...), custom_call_target="tpu_custom_call" | custom-call | flops 154618822656 | bytes 67108864 | tf_op jit(solution)/shard_map/forward_all/pallas_call | solution.py:247
  395.3 20.5 %far_update.1 = (f32[512,2048]{1,0:T(8,128)}, f32[512,2048]{1,0:T(8,128)}, f32[512,2048]{1,0:T(8,128)}, f32[2048,512]{1,0:T(8,128)}, f32[2048,512]{1,0:T(8,128)}...) custom-call(s32[1]{0:T(128)} %bitcast.half_ref, ...), custom_call_target="tpu_custom_call", output_to_operand_aliasing={{0}: (12, {}), {1}: (13, {}), {2}: (14, {}), {3}: (15, {}),... | custom-call | flops 31457280 | bytes 31457280 | tf_op jit(solution)/shard_map/far_update/pallas_call | solution.py:319
Async XLA Ops:
  142.4 24.5 %collective-permute-start.2 = (bf16[256,2048]{1,0:T(8,128)(2,1)}, bf16[256,2048]{1,0:T(8,128)(2,1)S(1)}, u32[]{:S(2)}, u32[]{:S(2)}) collective-permute-start(bf16[256,2048]{1,0:T(8,128)(2,1)} %get-tuple-element.29.w1_ref), channel_id=1, source_target_pairs={{0,4},{4,0},{1,5},{5,1},{2,6},{6,2},{3,7},{7,3}} | collective-permute-start | bytes 3145736 | tf_op jit(solution)/shard_map/ppermute | solution.py:621
  142.7 24.2 %collective-permute-start = (bf16[256,2048]{1,0:T(8,128)(2,1)}, bf16[256,2048]{1,0:T(8,128)(2,1)}, u32[]{:S(2)}, u32[]{:S(2)}) collective-permute-start(bf16[256,2048]{1,0:T(8,128)(2,1)} %get-tuple-element.29.w1_ref), channel_id=1, source_target_pairs={{0,2},{1,3},{2,0},{3,1},{4,6},{5,7},{6,4},{7,5}} | collective-permute-start | bytes 3145736 | tf_op jit(solution)/shard_map/ppermute | solution.py:620
  142.7 46.6 %collective-permute-start.3 = (bf16[1024,512]{1,0:T(8,128)(2,1)}, bf16[1024,512]{1,0:T(8,128)(2,1)}, u32[]{:S(2)}, u32[]{:S(2)}) collective-permute-start(bf16[1024,512]{1,0:T(8,128)(2,1)} %get-tuple-element.30.w2_ref), channel_id=1, source_target_pairs={{0,4},{4,0},{1,5},{5,1},{2,6},{6,2},{3,7},{7,3}} | collective-permute-start | bytes 3145736 | tf_op jit(solution)/shard_map/ppermute | solution.py:621
  143.9 45.4 %collective-permute-start.1 = (bf16[1024,512]{1,0:T(8,128)(2,1)}, bf16[1024,512]{1,0:T(8,128)(2,1)}, u32[]{:S(2)}, u32[]{:S(2)}) collective-permute-start(bf16[1024,512]{1,0:T(8,128)(2,1)} %get-tuple-element.30.w2_ref), channel_id=1, source_target_pairs={{0,2},{1,3},{2,0},{3,1},{4,6},{5,7},{6,4},{7,5}} | collective-permute-start | bytes 3145736 | tf_op jit(solution)/shard_map/ppermute | solution.py:620
  166.9 22.5 %copy-start = (bf16[256,2048]{1,0:T(8,128)(2,1)}, bf16[256,2048]{1,0:T(8,128)(2,1)S(1)}, u32[]{:S(2)}) copy-start(bf16[256,2048]{1,0:T(8,128)(2,1)S(1)} %collective-permute-done.2.rw1_ref) | copy-start | bytes 3145732
